TPU v7x, 32 devices: a whole 2x2x4 slice. The times are simulated.
32 devices in a mesh: clip: 16 (over z, x, core), strip: 2 (over y).
Axes of the slice: x: 2, y: 2, z: 4, core: 2. Of those that a mesh axis runs over, the one named last changes fastest.
Arguments:
- video: bfloat16 [32, 2, 32, 32, 256], P('clip', None, 'strip')
- gain_first: float32 [256], replicated, may hold values from 0.1 to 1.9
- conv_weight: bfloat16 [3, 3, 3, 256, 256], replicated, may hold values from -0.078125 to 0.078125
- gain_second: float32 [256], replicated, may hold values from 0.1 to 1.9
- proj_weight: bfloat16 [256, 256], replicated, may hold values from -0.375 to 0.375
- codes: int32 [32, 2, 32, 32], P('clip', None, 'strip'), may hold values from 0 to 1023
- ema_sum: float32 [1024, 256], replicated, may hold values from -12 to 12
- ema_count: float32 [1024], replicated, may hold values from 0.5 to 8
Outputs:
- latent: float32 [32, 2, 32, 32, 256], P('clip', None, 'strip')
- codebook: float32 [1024, 256], replicated
- code_count: float32 [1024], replicated
- clip_error: float32 [32], P('clip')
All inputs are finite; a program needn't handle non-finite values.
Results may differ from a plain program's by a relative error of at most 0.0029.
Values may be sent and summed in bfloat16 or wider, within the bound.
No kernel may reach another device: no remote copies, remote signals or barrier semaphores. Data moves between devices by JAX's collectives and lax.ppermute only.
A program may use at most 64 MiB of HBM per device.

v0:
```python
import jax
import jax.numpy as jnp
from jax import lax
from jax.sharding import PartitionSpec as P

EMB = 256
CODES = 1024
GROUPS = 32


norm_eps = 1e-06
smooth_eps = 1e-05
ema_decay = 0.9


def extended(cells, sides, width):
    for axis, dim in sides:
        count = lax.axis_size(axis)
        ends = count - 1
        head = lax.slice_in_dim(cells, 0, width, axis=dim)
        tail = lax.slice_in_dim(cells, cells.shape[dim] - width, cells.shape[dim], axis=dim)
        cells = jnp.concatenate(
            [
                lax.ppermute(tail, axis, [(i, (i + 1) % count) for i in range(ends)]),
                cells,
                lax.ppermute(head, axis, [((i + 1) % count, i) for i in range(ends)]),
            ],
            axis=dim,
        )
    return cells


def group_norm(values, gain_vec):
    shaped = values.reshape(values.shape[:4] + (GROUPS, values.shape[4] // GROUPS))
    members = (
        shaped.shape[1]
        * shaped.shape[2]
        * lax.axis_size("strip")
        * shaped.shape[3]
        * shaped.shape[5]
    )
    first_sum = lax.psum(jnp.sum(shaped, axis=(1, 2, 3, 5)), "strip")
    centre = (first_sum / members)[:, None, None, None, :, None]
    deviation = shaped - centre
    spread = lax.psum(jnp.sum(deviation * deviation, axis=(1, 2, 3, 5)), "strip") / members
    spread = spread[:, None, None, None, :, None]
    normed = (shaped - centre) * lax.rsqrt(spread + norm_eps)
    return normed.reshape(values.shape) * gain_vec


def smoothed_book(sums, counts, grand):
    smooth = (counts + smooth_eps) / (grand + CODES * smooth_eps) * grand
    return sums / smooth[:, None]


def body(video, gain_first, conv_weight, gain_second, proj_weight, codes, ema_sum, ema_count):
    batch_clips, frame_count, row_count, col_count, channels = video.shape
    values = video.astype(jnp.float32)
    act_first = jax.nn.silu(group_norm(values, gain_first)).astype(jnp.bfloat16)
    padded = extended(act_first, (("strip", 2),), 1)
    convolved = lax.conv_general_dilated(
        padded,
        conv_weight,
        (1, 1, 1),
        [(2, 0), (0, 0), (1, 1)],
        dimension_numbers=("NDHWC", "DHWIO", "NDHWC"),
        preferred_element_type=jnp.float32,
    )
    hidden = values + convolved
    act_second = jax.nn.silu(group_norm(hidden, gain_second)).astype(jnp.bfloat16)
    flat_latent = jnp.dot(
        act_second.reshape(-1, channels), proj_weight, preferred_element_type=jnp.float32
    )
    flat_codes = codes.reshape(-1)
    old_book = smoothed_book(ema_sum, ema_count, jnp.sum(ema_count))
    quantized = jnp.take(old_book, flat_codes, axis=0)
    squared = jnp.sum((flat_latent - quantized) ** 2, axis=1).reshape(batch_clips, -1)
    clip_tokens = squared.shape[1] * lax.axis_size("strip")
    error_sum = lax.psum(jnp.sum(squared, axis=1), "strip")
    clip_error = error_sum / (clip_tokens * EMB)
    code_sums = jax.ops.segment_sum(flat_latent, flat_codes, CODES)
    token_counts = jax.ops.segment_sum(jnp.ones(flat_codes.shape, jnp.float32), flat_codes, CODES)
    all_tokens = flat_codes.shape[0] * lax.axis_size("clip") * lax.axis_size("strip")
    grand_total = ema_decay * jnp.sum(ema_count) + (1.0 - ema_decay) * all_tokens
    half_sums, half_counts = (
        lax.psum_scatter(
            code_sums.astype(jnp.bfloat16), "strip", scatter_dimension=0, tiled=True
        ).astype(jnp.float32),
        lax.psum_scatter(
            token_counts.astype(jnp.bfloat16), "strip", scatter_dimension=0, tiled=True
        ).astype(jnp.float32),
    )
    half_sums, half_counts = lax.psum((half_sums, half_counts), "clip")
    share_rows = half_counts.shape[0]
    offset = lax.axis_index("strip") * share_rows
    own_sum = lax.dynamic_slice_in_dim(ema_sum, offset, share_rows, 0)
    own_count = lax.dynamic_slice_in_dim(ema_count, offset, share_rows, 0)
    count_part = ema_decay * own_count + (1.0 - ema_decay) * half_counts
    book_part = smoothed_book(
        ema_decay * own_sum + (1.0 - ema_decay) * half_sums, count_part, grand_total
    )
    codebook, code_count = (
        lax.all_gather(book_part, "strip", axis=0, tiled=True),
        lax.all_gather(count_part, "strip", axis=0, tiled=True),
    )
    latent = flat_latent.reshape(batch_clips, frame_count, row_count, col_count, EMB)
    return (latent, codebook, code_count, clip_error)


def solution(mesh):
    in_specs = (
        P("clip", None, "strip", None, None),
        P(),
        P(),
        P(),
        P(),
        P("clip", None, "strip", None),
        P(),
        P(),
    )
    out_specs = (P("clip", None, "strip", None, None), P(), P(), P("clip"))
    return jax.shard_map(body, mesh=mesh, in_specs=in_specs, out_specs=out_specs, check_vma=False)
```

profile of v0, /device:TPU:0, one launch (start us, length us, event | category | flops | bytes accessed | tf_op | source)
XLA Modules:
  0.0 241.4 jit_solution(10608032350053788916)
XLA Ops:
  7.2 1.9 convert_reduce_fusion
  10.7 5.9 %psum.49 = f32[2,32]{1,0:T(2,128)S(1)} all-reduce(f32[2,32]{1,0:T(2,128)S(1)} %reduce_sum.97), channel_id=1, replica_groups=mesh['clip'=16,'strip'=2] {'strip'}, use_global_device_ids=true, to_apply=%region_2.0 | all-reduce | flops 64 | bytes 512 | tf_op jit(solution)/shard_map/psum | solution.py:42
  21.5 4.9 %psum.50 = f32[2,32]{1,0:T(2,128)S(1)} all-reduce(f32[2,32]{1,0:T(2,128)S(1)} %reduce_sum.100), channel_id=1, replica_groups=mesh['clip'=16,'strip'=2] {'strip'}, use_global_device_ids=true, to_apply=%region_5.6 | all-reduce | flops 64 | bytes 512 | tf_op jit(solution)/shard_map/psum | solution.py:45
  28.0 2.2 fusion.9
  32.1 4.6 %collective-permute-start = (bf16[2,2,1,32,256]{4,2,3,0,1:T(2,128)(2,1)}, bf16[2,2,1,32,256]{4,2,3,0,1:T(2,128)(2,1)}, u32[]{:S(2)}, u32[]{:S(2)}) collective-permute-start(bf16[2,2,1,32,256]{4,2,3,0,1:T(2,128)(2,1)} %get-tuple-element.8), channel_id=1, source_target_pairs={{0,1},{2,3},{4,5},{6,7},{8,9},{10,11},{12,13},{14,15},{16,17},{18,... | collective-permute-start | bytes 196616 | tf_op jit(solution)/shard_map/ppermute | solution.py:24
  43.0 2.4 broadcast_divide_fusion
  46.0 9.8 %gather_fusion = f32[2048,256]{1,0:T(8,128)} fusion(f32[1024,256]{1,0:T(8,128)} %broadcast_divide_fusion, s32[2048]{0:T(1024)S(1)} %broadcast_clamp_fusion), kind=kCustom, calls=%fused_computation | custom fusion | bytes 4202496 | tf_op jit(solution)/shard_map/jit(_take)/gather | solution.py:76
  55.8 2.3 maximum_bitcast_fusion
  60.8 2.1 fusion.10
  63.0 10.3 %fusion.14 = f32[2,16,16,5,256]{4,2,3,1,0:T(8,128)S(1)} fusion(bf16[3,3,3,256,256]{4,3,2,1,0:T(8,128)(2,1)S(1)} %copy-done, bf16[2,18,2,8,7,256]{5,2,4,3,1,0:T(2,128)(2,1)S(1)} %fusion.10, pred[16,5]{0,1:T(8,128)(4,1)S(1)} %copy-done.5), kind=kOutput, calls=%fused_computation.25 | convolution fusion | flops 4530503680 | bytes 8224848 | tf_op jit(solution)/shard_map/conv_general_dilated | solution.py:61
  78.8 6.2 %psum.51 = f32[2,32]{1,0:T(2,128)S(1)} all-reduce(f32[2,32]{1,0:T(2,128)S(1)} %reduce_sum.103), channel_id=1, replica_groups=mesh['clip'=16,'strip'=2] {'strip'}, use_global_device_ids=true, to_apply=%region_8.9 | all-reduce | flops 64 | bytes 512 | tf_op jit(solution)/shard_map/psum | solution.py:42
  86.5 2.6 %multiply_reduce_fusion.1 = f32[2,256]{1,0:T(2,128)S(1)} fusion(f32[2,256]{1,0:T(2,128)S(1)} %sub.44, f32[2,16,2,40,256]{4,1,3,2,0:T(8,128)} %bitcast.33, bf16[2,2,16,32,256]{4,3,2,1,0:T(8,128)(2,1)} %param.8), kind=kLoop, calls=%fused_computation.20 | loop fusion | flops 2620928 | bytes 3149824 | tf_op jit(solution)/shard_map/reduce_sum | solution.py:45
  90.7 5.5 %psum.52 = f32[2,32]{1,0:T(2,128)} all-reduce(f32[2,32]{1,0:T(2,128)S(1)} %reduce_sum.106), channel_id=1, replica_groups=mesh['clip'=16,'strip'=2] {'strip'}, use_global_device_ids=true, to_apply=%region_11.12 | all-reduce | flops 64 | bytes 512 | tf_op jit(solution)/shard_map/psum | solution.py:45
  98.4 3.0 %multiply_convert_fusion = bf16[2,2,16,32,256]{4,2,3,0,1:T(8,128)(2,1)S(1)} fusion(f32[256]{0:T(256)} %param.11, f32[2,256]{1,0:T(2,128)S(1)} %mul.109, f32[2,256]{1,0:T(2,128)S(1)} %sub.44, f32[2,16,2,40,256]{4,1,3,2,0:T(8,128)} %bitcast.34, bf16[2,2,16,32,256]{4,3,2,1,0:T(8,128)(2,1)} %param.8), kind=kLoop, calls=%fused_computation.19 | loop fusion | flops 5242880 | bytes 4199424 | tf_op jit(solution)/shard_map/convert_element_type | solution.py:70
  104.7 13.0 %scatter_custom_fusion = f32[1024,256]{1,0:T(8,128)} fusion(s32[2048]{0:T(1024)S(1)} %reshape.104, f32[2048,256]{1,0:T(8,128)} %get-tuple-element.11, f32[]{:T(128)} %constant.17.clone.1), kind=kCustom, calls=%fused_computation.29 | custom fusion | flops 524288 | bytes 1049088 | tf_op jit(solution)/shard_map/scatter-add | solution.py:81
  117.6 2.1 convert_element_type.24
  120.4 15.4 %scatter_custom_fusion.1 = f32[1024]{0:T(1024)} fusion(s32[2048]{0:T(1024)S(1)} %reshape.104, f32[2048]{0:T(1024)} %broadcast.68, f32[]{:T(128)} %constant.17.clone.1), kind=kCustom, calls=%fused_computation.39 | custom fusion | flops 2048 | bytes 4608 | tf_op jit(solution)/shard_map/scatter-add | solution.py:82
  139.0 4.9 %all-reduce = bf16[1024]{0:T(1024)(128)(2,1)S(1)} all-reduce(bf16[1024]{0:T(1024)(128)(2,1)S(1)} %convert_element_type.26), channel_id=3, replica_groups=mesh['clip'=16,'strip'=2] {'strip'}, use_global_device_ids=true, to_apply=%region_16.17.clone | all-reduce | flops 1024 | bytes 4096
  144.0 64.9 %all-reduce.3 = (f32[512,256]{1,0:T(8,128)}, f32[512]{0:T(512)S(1)}) all-reduce(bf16[512,256]{1,0:T(8,128)(2,1)} %reduce-scatter.2.cloned.1.call-done, f32[512]{0:T(512)S(1)} %dynamic-slice_convert_fusion), channel_id=1, replica_groups=mesh['clip'=16,'strip'=2] {'clip'}, use_global_device_ids=true, to_apply=%region_14.15 | all-reduce | flops 131584 | bytes 790528 | tf_op jit(solution)/shard_map/psum | solution.py:93
  210.2 2.1 add_divide_fusion
  212.5 4.9 %psum.55 = f32[2]{0:T(128)S(1)} all-reduce(f32[2]{0:T(128)S(1)} %reduce_sum.109), channel_id=1, replica_groups=mesh['clip'=16,'strip'=2] {'strip'}, use_global_device_ids=true, to_apply=%region_21.22 | all-reduce | flops 2 | bytes 16 | tf_op jit(solution)/shard_map/psum | solution.py:79
  218.0 4.7 %all-gather = f32[2,1,512]{2,1,0:T(1,128)S(1)} all-gather(f32[1,1,512]{2,1,0:T(1,128)} %bitcast.41), channel_id=1, replica_groups=mesh['clip'=16,'strip'=2] {'strip'}, dimensions={0}, use_global_device_ids=true | all-gather | bytes 6144 | tf_op jit(solution)/shard_map/all_gather | solution.py:104
  222.7 8.9 %all-gather.3.cloned.1.call-done = f32[1024,256]{1,0:T(8,128)} async-done(((f32[512,256]{1,0:T(8,128)}), f32[1024,256]{1,0:T(8,128)}) %all-gather.3.cloned.1.call-update) | async-done | bytes 1048592 | tf_op jit(solution)/shard_map/all_gather | solution.py:103
  231.7 2.3 copy.55
  (71 shorter events, 38.2 us)
Async XLA Ops:
  7.2 55.8 %copy-start = (bf16[3,3,3,256,256]{4,3,2,1,0:T(8,128)(2,1)S(1)}, bf16[3,3,3,256,256]{4,3,2,1,0:T(8,128)(2,1)}, u32[]{:S(2)}) copy-start(bf16[3,3,3,256,256]{4,3,2,1,0:T(8,128)(2,1)} %param.10) | copy-start | bytes 10616836
  7.2 20.8 %copy-start.8 = (f32[256]{0:T(256)S(1)}, f32[256]{0:T(256)}, u32[]{:S(2)}) copy-start(f32[256]{0:T(256)} %param.9) | copy-start | bytes 3076
  7.2 136.9 %reduce-scatter.2.cloned.1.call-start = ((), (), s32[]{:S(2)}) async-start(), calls=%async_computation.1 | async-start | bytes 786432 | tf_op jit(solution)/shard_map/reduce_scatter | solution.py:86
  30.2 1.0 copy-start.4
  32.1 23.7 %collective-permute-start = (bf16[2,2,1,32,256]{4,2,3,0,1:T(2,128)(2,1)}, bf16[2,2,1,32,256]{4,2,3,0,1:T(2,128)(2,1)}, u32[]{:S(2)}, u32[]{:S(2)}) collective-permute-start(bf16[2,2,1,32,256]{4,2,3,0,1:T(2,128)(2,1)} %get-tuple-element.8), channel_id=1, source_target_pairs={{0,1},{2,3},{4,5},{6,7},{8,9},{10,11},{12,13},{14,15},{16,17},{18,... | collective-permute-start | bytes 196616 | tf_op jit(solution)/shard_map/ppermute | solution.py:24
  36.7 19.1 %collective-permute-start.1 = (bf16[2,2,1,32,256]{4,2,3,0,1:T(2,128)(2,1)}, bf16[2,2,1,32,256]{4,2,3,0,1:T(2,128)(2,1)}, u32[]{:S(2)}, u32[]{:S(2)}) collective-permute-start(bf16[2,2,1,32,256]{4,2,3,0,1:T(2,128)(2,1)} %get-tuple-element.9), channel_id=1, source_target_pairs={{1,0},{3,2},{5,4},{7,6},{9,8},{11,10},{13,12},{15,14},{17,16},{19,... | collective-permute-start | bytes 196616 | tf_op jit(solution)/shard_map/ppermute | solution.py:26
  60.8 2.1 copy-start.5
  73.3 3.0 %copy-start.1 = (bf16[2,2,16,32,256]{4,3,2,1,0:T(8,128)(2,1)S(1)}, bf16[2,2,16,32,256]{4,3,2,1,0:T(8,128)(2,1)}, u32[]{:S(2)}) copy-start(bf16[2,2,16,32,256]{4,3,2,1,0:T(8,128)(2,1)} %param.8) | copy-start | bytes 3145732
  74.8 1.5 copy-start.2
  98.4 3.4 %copy-start.6 = (bf16[256,256]{1,0:T(8,128)(2,1)S(1)}, bf16[256,256]{1,0:T(8,128)(2,1)}, u32[]{:S(2)}) copy-start(bf16[256,256]{1,0:T(8,128)(2,1)} %param.12) | copy-start | bytes 393220
  98.4 3.4 %copy-start.7 = (pred[2048]{0:T(1024)(128)(4,1)S(1)}, pred[2048]{0:T(1024)(128)(4,1)}, u32[]{:S(2)}) copy-start(pred[2048]{0:T(1024)(128)(4,1)} %compare_and_fusion) | copy-start | bytes 6148
  101.3 1.6 copy-start.3
  119.7 112.0 %all-gather.3.cloned.1.call-start = ((), (), s32[]{:S(2)}) async-start(), calls=%async_computation.2 | async-start | bytes 1572864 | tf_op jit(solution)/shard_map/all_gather | solution.py:103
Sparse Core Ops, SparseCore 0:
  119.8 16.3 reduce-scatter.1
  212.5 19.0 all-gather.2
where the time goes:
time: 243 us; the launch traced here: 241 us
  blocking collectives  102 us (42%)
  other arithmetic  61.8 us (25%)
  local copies, waits for them, and re-layouts  34.4 us (14%)
  between operations  16.2 us (7%)
  matrix products  12 us (5%)
  waiting for transfers between devices  8.98 us (4%)
  starting transfers between devices  5.95 us (2%)
    psum x1, blocking collectives, body(): half_sums, half_counts = lax.psum((half_sums, half_counts), 'clip')  64.9 us
    scatter-add x1, other arithmetic, body(): jax.ops.segment_sum(jnp.ones(flat_codes.shape, jnp.float32), flat_codes,...  15.4 us
    scatter-add x1, other arithmetic, body(): code_sums = jax.ops.segment_sum(flat_latent, flat_codes, CODES)  13 us
    psum x2, blocking collectives, group_norm(): first_sum = lax.psum(jnp.sum(shaped, axis=(1, 2, 3, 5)), 'strip')  12 us
    psum x2, blocking collectives, group_norm(): lax.psum(jnp.sum(deviation * deviation, axis=(1, 2, 3, 5)), 'strip')  10.4 us
    conv_general_dilated x1, matrix products, body(): lax.conv_general_dilated(padded, conv_weight, (1, 1, 1), [(2, 0), (0, 0),...  10.3 us
    gather x1, local copies, waits for them, and re-layouts, body(): quantized = jnp.take(old_book, flat_codes, axis=0)  9.82 us
    unnamed x22, local copies, waits for them, and re-layouts  9.03 us
  transfers between devices with their start and end apart: 4, of which 1 were waited for; matrix products, arithmetic and copies ran while one was open for 15% of the time, Pallas kernels for 0%

commit v1 on v0

v1 whole, which is shorter than its diff:
```python
import functools

import jax
import jax.numpy as jnp
from jax import lax
from jax.experimental import pallas as pl
from jax.experimental.pallas import tpu as pltpu
from jax.sharding import PartitionSpec as P

GROUPS = 32

norm_eps = 1e-06
smooth_eps = 1e-05
ema_decay = 0.9

f32 = jnp.float32
bf16 = jnp.bfloat16
LANES = 128
SHARDS = 8
TAIL = 8
BOTH = ("clip", "strip")
VMEM = pltpu.VMEM
VSPEC = pl.BlockSpec(memory_space=pltpu.VMEM)


def call(kernel, outs, args, scratch=(), flops=0, limit=None, name=None):
    return pl.pallas_call(
        kernel,
        out_shape=tuple(jax.ShapeDtypeStruct(s, d) for s, d in outs),
        in_specs=[VSPEC] * len(args),
        out_specs=tuple(VSPEC for _ in outs),
        scratch_shapes=list(scratch),
        compiler_params=pltpu.CompilerParams(vmem_limit_bytes=limit),
        cost_estimate=pl.CostEstimate(flops=flops, bytes_accessed=0, transcendentals=0),
        name=name,
    )(*args)


def pieces(value):
    head = value.astype(bf16)
    rest = value - head.astype(f32)
    middle = rest.astype(bf16)
    last = (rest - middle.astype(f32)).astype(bf16)
    return head, middle, last


def group_matrix(channels):
    shift = (channels // GROUPS).bit_length() - 1
    rows = lax.broadcasted_iota(jnp.int32, (channels, channels), 0) >> shift
    cols = lax.broadcasted_iota(jnp.int32, (channels, channels), 1) >> shift
    return jnp.where(rows == cols, 1.0, 0.0).astype(f32)


def group_total(rows, matrix):
    return jnp.dot(rows, matrix, precision=lax.Precision.HIGHEST, preferred_element_type=f32)


def stacked(rows, channels):
    row = lax.broadcasted_iota(jnp.int32, (8, channels), 0)
    out = jnp.zeros((8, channels), f32)
    for i, value in enumerate(rows):
        out = jnp.where(row == i, value, out)
    return out


def local_stats(read, clips, blocks, rows, channels):
    matrix = group_matrix(channels)
    members = blocks * rows * (channels // GROUPS)
    sums = []
    for c in range(clips):
        total = lax.fori_loop(
            0, blocks, lambda i, acc: acc + read(c, i), jnp.zeros((rows, channels), f32), unroll=4
        )
        sums.append(jnp.sum(total, axis=0, keepdims=True))
    means = group_total(stacked(sums, channels), matrix) / members
    squares = []
    for c in range(clips):
        mean = means[c : c + 1]

        def step(i, acc):
            away = read(c, i) - mean
            return acc + away * away

        total = lax.fori_loop(0, blocks, step, jnp.zeros((rows, channels), f32), unroll=4)
        squares.append(jnp.sum(total, axis=0, keepdims=True))
    squares = group_total(stacked(squares, channels), matrix)
    return means, squares, members


def merged(mean_a, square_a, mean_b, square_b, members):
    mean = 0.5 * (mean_a + mean_b)
    apart = mean_a - mean_b
    spread = (square_a + square_b + apart * apart * (0.5 * members)) / (2 * members)
    return mean, lax.rsqrt(spread + norm_eps)


def silu(v):
    half = 0.5 * v
    return half + half * jnp.tanh(half)


def stats_kernel(video_ref, pay_ref, loc_ref):
    clips, frames, rows, cols, channels = video_ref.shape
    strip = lax.axis_index("strip")
    edge = (1 - strip) * (rows - 1)
    for c in range(clips):
        for t in range(frames):
            at = (c * frames + t) * cols
            pay_ref[at : at + cols] = video_ref[c, t, edge]

    def read(c, i):
        return video_ref[c, i // rows, i % rows].astype(f32)

    means, squares, _ = local_stats(read, clips, frames * rows, cols, channels)
    loc_ref[0:8] = means
    loc_ref[8:16] = squares
    base = clips * frames * cols
    row = lax.broadcasted_iota(jnp.int32, (16, channels), 0)
    out = jnp.zeros((16, channels), f32)
    for j, value in enumerate((means, squares)):
        for k, piece in enumerate(pieces(value)):
            piece = piece.astype(f32)
            for c in range(clips):
                out = jnp.where(row == (j * clips + c) * 3 + k, piece[c : c + 1], out)
    pay_ref[base : base + 16] = out.astype(bf16)


def conv_kernel(video_ref, pay_ref, loc_ref, gain_ref, w_ref, hid_ref, st_ref, buf_ref):
    clips, frames, rows, cols, channels = video_ref.shape
    strip = lax.axis_index("strip")
    members = frames * rows * cols * (channels // GROUPS)
    base = clips * frames * cols
    far = pay_ref[base : base + 16].astype(f32)
    gain = gain_ref[...]
    col = lax.broadcasted_iota(jnp.int32, (cols, channels), 0)

    def put(c, t, r, act):
        left = jnp.where(col == 0, 0.0, pltpu.roll(act, 1, 0))
        right = jnp.where(col == cols - 1, 0.0, pltpu.roll(act, cols - 1, 0))
        buf_ref[c, t, r, :, 0:channels] = left.astype(bf16)
        buf_ref[c, t, r, :, channels : 2 * channels] = act.astype(bf16)
        buf_ref[c, t, r, :, 2 * channels : 3 * channels] = right.astype(bf16)

    for c in range(clips):
        at = [(j * clips + c) * 3 for j in (0, 1)]
        far_mean, far_square = [far[i : i + 1] + far[i + 1 : i + 2] + far[i + 2 : i + 3] for i in at]
        mean, inverse = merged(
            loc_ref[c : c + 1], loc_ref[8 + c : 9 + c], far_mean, far_square, members
        )
        scale = inverse * gain
        for t in range(frames):
            def row_step(r, carry):
                x = video_ref[c, t, r].astype(f32)
                put(c, t, r + 1, silu((x - mean) * scale))
                return carry

            lax.fori_loop(0, rows, row_step, 0, unroll=4)
            where_at = (c * frames + t) * cols
            halo = silu((pay_ref[where_at : where_at + cols].astype(f32) - mean) * scale)
            put(c, t, 0, jnp.where(strip > 0, halo, 0.0))
            put(c, t, rows + 1, jnp.where(strip > 0, 0.0, halo))

        def patches(t):
            return jnp.concatenate(
                [
                    buf_ref[c, t, b : b + rows].reshape(rows * cols, 3 * channels)
                    for b in range(3)
                ],
                axis=1,
            )

        for t in range(frames):
            total = video_ref[c, t].reshape(rows * cols, channels).astype(f32)
            for a in range(3):
                if t + a - 2 >= 0:
                    total = total + jnp.dot(
                        patches(t + a - 2), w_ref[a], preferred_element_type=f32
                    )
            hid_ref[c, t * rows * cols : (t + 1) * rows * cols] = total

    def read(c, i):
        return hid_ref[c, pl.ds(pl.multiple_of(i * cols, cols), cols)]

    means, squares, _ = local_stats(read, clips, frames * rows, cols, channels)
    st_ref[0:8] = means
    st_ref[8:16] = squares


def shard_bits():
    clip = lax.axis_index("clip")
    return ((clip & 1) << 2) | (((clip >> 1) & 1) << 1) | lax.axis_index("strip")


def tail_rows(count, extra=None):
    row = lax.broadcasted_iota(jnp.int32, (TAIL, 2 * LANES), 0)
    zero = jnp.zeros((1, LANES), f32)
    out = jnp.zeros((TAIL, 2 * LANES), f32)
    for i, value in enumerate((count,) if extra is None else (count, extra)):
        head, middle, last = [p.astype(f32) for p in pieces(value)]
        out = jnp.where(row == 2 * i, jnp.concatenate([head, middle], axis=1), out)
        out = jnp.where(row == 2 * i + 1, jnp.concatenate([last, zero], axis=1), out)
    return out.astype(bf16)


def untail(block, which=0):
    block = block.astype(f32)
    i = 2 * which
    return (
        block[i : i + 1, :LANES] + block[i : i + 1, LANES:] + block[i + 1 : i + 2, :LANES]
    )


def segment_kernel(
    hid_ref, near_ref, far_ref, gain_ref, codes_ref, act_ref, send_ref, keep_ref, cnt_ref, acc_ref
):
    clips, tokens, channels = hid_ref.shape
    members = tokens * (channels // GROUPS)
    gain = gain_ref[...]
    block = 64
    for c in range(clips):
        mean, inverse = merged(
            near_ref[c : c + 1],
            near_ref[8 + c : 9 + c],
            far_ref[c : c + 1],
            far_ref[8 + c : 9 + c],
            members,
        )
        scale = inverse * gain

        def step(i, carry):
            x = hid_ref[c, pl.ds(pl.multiple_of(i * block, block), block)]
            act = silu((x - mean) * scale).astype(bf16)
            act_ref[pl.ds(pl.multiple_of(c * tokens + i * block, block), block)] = act
            return carry

        lax.fori_loop(0, tokens // block, step, 0, unroll=2)

    me = shard_bits()
    codes_count = acc_ref.shape[0]
    share = codes_count // SHARDS
    codes = codes_ref[...] ^ (me * share)
    row_code = lax.broadcasted_iota(jnp.int32, (codes_count, LANES), 0)
    low_code = lax.broadcasted_iota(jnp.int32, (share, LANES), 0)
    high_code = lax.broadcasted_iota(jnp.int32, (SHARDS, LANES), 0)
    count = jnp.zeros((SHARDS, LANES), f32)
    width = 2
    shift = share.bit_length() - 1
    for k in range(codes.shape[0] // width):
        hot = []
        for j in range(width):
            line = codes[k * width + j : k * width + j + 1]
            hot.append(jnp.where(row_code == line, 1.0, 0.0).astype(bf16))
            low = jnp.where(low_code == (line & (share - 1)), 1.0, 0.0).astype(bf16)
            high = jnp.where(high_code == (line >> shift), 1.0, 0.0).astype(bf16)
            count = count + lax.dot_general(
                high, low, (((1,), (1,)), ((), ())), preferred_element_type=f32
            )
        part = jnp.dot(
            jnp.concatenate(hot, axis=1),
            act_ref[k * width * LANES : (k + 1) * width * LANES],
            preferred_element_type=f32,
        )
        if k == 0:
            acc_ref[...] = part
        else:
            acc_ref[...] += part
    cnt_ref[...] = count
    half = SHARDS // 2
    keep_ref[...] = acc_ref[: half * share].reshape(half, share, channels)
    for p in range(half):
        send_ref[p, :share] = acc_ref[(half + p) * share : (half + p + 1) * share].astype(bf16)
        send_ref[p, share:] = tail_rows(count[half + p : half + p + 1])


def quarter_kernel(keep_ref, cnt_ref, got_ref, mine_ref, mcnt_ref, s1_ref, s2_ref, s3_ref):
    share = keep_ref.shape[1]
    for p, out in enumerate((None, s1_ref, s2_ref, s3_ref)):
        value = keep_ref[p] + got_ref[p, :share].astype(f32)
        count = cnt_ref[p : p + 1] + untail(got_ref[p, share:])
        if out is None:
            mine_ref[...] = value
            mcnt_ref[...] = jnp.broadcast_to(count, (8, LANES))
        else:
            out[:share] = value.astype(bf16)
            out[share:] = tail_rows(count)


def gathered_kernel(mine_ref, mcnt_ref, a_ref, b_ref, c_ref, out_ref):
    share = mine_ref.shape[0]
    value = mine_ref[...]
    count = mcnt_ref[0:1]
    for ref in (a_ref, b_ref, c_ref):
        value = value + ref[:share].astype(f32)
        count = count + untail(ref[share:])
    out_ref[:share] = value.astype(bf16)
    out_ref[share:] = tail_rows(count)


def pair_kernel(own_ref, got_ref, out_ref):
    share = own_ref.shape[0] - TAIL
    value = own_ref[:share].astype(f32) + got_ref[:share].astype(f32)
    out_ref[:share] = value.astype(bf16)
    out_ref[share:] = tail_rows(untail(own_ref[share:]) + untail(got_ref[share:]))


def project_kernel(own_ref, got_ref, w_ref, err_ref, out_ref):
    share = own_ref.shape[0] - TAIL
    value = own_ref[:share].astype(f32) + got_ref[:share].astype(f32)
    head = value.astype(bf16)
    rest = (value - head.astype(f32)).astype(bf16)
    sums = jnp.dot(head, w_ref[...], preferred_element_type=f32) + jnp.dot(
        rest, w_ref[...], preferred_element_type=f32
    )
    out_ref[:share] = sums.astype(bf16)
    out_ref[share:] = tail_rows(
        untail(own_ref[share:]) + untail(got_ref[share:]), err_ref[0:1]
    )


def as_column(row):
    return jnp.transpose(jnp.broadcast_to(row, (LANES, LANES)))


def latent_kernel(act_ref, w_ref, codes_ref, sum_ref, cnt_ref, lat_ref, err_ref, head_ref, rest_ref):
    tokens, channels = lat_ref.shape
    codes_count = sum_ref.shape[0]
    clips = 2
    counts = cnt_ref[...]
    grand = jnp.sum(counts)
    smooth = (counts + smooth_eps) / (grand + codes_count * smooth_eps) * grand
    for i in range(codes_count // LANES):
        divisor = as_column(smooth[i : i + 1])
        divisor = jnp.concatenate([divisor] * (channels // LANES), axis=1)
        book = sum_ref[i * LANES : (i + 1) * LANES] / divisor
        head = book.astype(bf16)
        head_ref[i * LANES : (i + 1) * LANES] = head
        rest_ref[i * LANES : (i + 1) * LANES] = (book - head.astype(f32)).astype(bf16)
    lane_code = lax.broadcasted_iota(jnp.int32, (LANES, codes_count), 1)
    lane = lax.broadcasted_iota(jnp.int32, (1, LANES), 1)
    lines = tokens // LANES
    per_clip = lines // clips
    errors = jnp.zeros((1, LANES), f32)
    for c in range(clips):
        def step(i, acc):
            line = c * per_clip + i
            at = pl.ds(pl.multiple_of(line * LANES, LANES), LANES)
            latent = jnp.dot(act_ref[at], w_ref[...], preferred_element_type=f32)
            lat_ref[at] = latent
            column = as_column(codes_ref[pl.ds(line, 1)])
            column = jnp.concatenate([column] * (codes_count // LANES), axis=1)
            hot = jnp.where(column == lane_code, 1.0, 0.0).astype(bf16)
            chosen = jnp.dot(hot, head_ref[...], preferred_element_type=f32) + jnp.dot(
                hot, rest_ref[...], preferred_element_type=f32
            )
            away = latent - chosen
            away = away * away
            return acc + jnp.sum(away.reshape(LANES // 8, 8, channels), axis=0)

        total = lax.fori_loop(0, per_clip, step, jnp.zeros((8, channels), f32), unroll=2)
        errors = jnp.where(lane == c, jnp.sum(total), errors)
    err_ref[...] = jnp.broadcast_to(errors, (8, LANES))


def final_kernel(scale, tokens, p0, p1, p2, p3, q_ref, sum_ref, cnt_ref, err_ref, book_ref, count_ref, error_ref):
    share = LANES
    me = shard_bits()
    grand = ema_decay * jnp.sum(cnt_ref[...]) + (1.0 - ema_decay) * tokens
    for p in range(SHARDS):
        src = (p0, p1, p2, p3)[p] if p < 4 else q_ref.at[p - 4]
        shard = p ^ me
        count = ema_decay * cnt_ref[pl.ds(shard, 1)] + (1.0 - ema_decay) * untail(src[share:])
        count_ref[pl.ds(shard, 1)] = count
        smooth = (count + smooth_eps) / (grand + SHARDS * share * smooth_eps) * grand
        divisor = as_column(smooth)
        channels = book_ref.shape[1]
        divisor = jnp.concatenate([divisor] * (channels // LANES), axis=1)
        at = pl.ds(pl.multiple_of(shard * share, share), share)
        fresh = ema_decay * sum_ref[at] + (1.0 - ema_decay) * src[:share].astype(f32)
        book_ref[at] = fresh / divisor
    error_ref[...] = jnp.broadcast_to((err_ref[0:1] + untail(p1[share:], 1)) * scale, (8, LANES))


def body(video, gain_first, conv_weight, gain_second, proj_weight, codes, ema_sum, ema_count):
    clips, frames, rows, cols, channels = video.shape
    codes_count = ema_sum.shape[0]
    clip_size, strips = lax.axis_size("clip"), lax.axis_size("strip")
    n = clip_size * strips
    share = codes_count // SHARDS
    assert strips == 2 and clip_size >= 4 and clip_size & (clip_size - 1) == 0
    assert share == LANES and channels == 2 * LANES and clips == 2

    def swap(x, mask):
        return lax.ppermute(x, BOTH, [(i, i ^ mask) for i in range(n)])

    tokens = frames * rows * cols
    halo = clips * frames * cols
    pay, near = call(
        stats_kernel,
        [((halo + 16, channels), bf16), ((16, channels), f32)],
        [video],
        flops=10_000_000,
        limit=8 << 20,
        name="stats",
    )
    far_pay = swap(pay, 1)
    code_lines = codes.reshape(-1, LANES)
    weights = conv_weight.reshape(3, 9 * channels, channels)
    hidden, near_two = call(
        conv_kernel,
        [((clips, tokens, channels), f32), ((16, channels), f32)],
        [video, far_pay, near, gain_first.reshape(1, channels), weights],
        scratch=[VMEM((clips, frames, rows + 2, cols, 3 * channels), bf16)],
        flops=4_000_000_000,
        limit=24 << 20,
        name="conv",
    )
    far_two = swap(near_two, 1)
    act, send, keep, cnt = call(
        segment_kernel,
        [
            ((clips * tokens, channels), bf16),
            ((SHARDS // 2, share + TAIL, channels), bf16),
            ((SHARDS // 2, share, channels), f32),
            ((SHARDS, LANES), f32),
        ],
        [hidden, near_two, far_two, gain_second.reshape(1, channels), code_lines],
        scratch=[VMEM((codes_count, channels), f32)],
        flops=1_500_000_000,
        limit=24 << 20,
        name="segment",
    )
    core, x_bit = 2, 4
    got = swap(send, core)
    counts = ema_count.reshape(SHARDS, LANES)
    latent, err = call(
        latent_kernel,
        [((clips * tokens, channels), f32), ((8, LANES), f32)],
        [act, proj_weight, code_lines, ema_sum, counts],
        scratch=[VMEM((codes_count, channels), bf16)] * 2,
        flops=2_500_000_000,
        limit=24 << 20,
        name="latent",
    )
    flat = ((share + TAIL, channels), bf16)
    mine, mine_cnt, s1, s2, s3 = call(
        quarter_kernel,
        [((share, channels), f32), ((8, LANES), f32), flat, flat, flat],
        [keep, cnt, got],
        flops=1_000_000,
        limit=8 << 20,
        name="quarter",
    )
    near_masks = (1, x_bit, 1 | x_bit)
    parts = [swap(s, m) for s, m in zip((s1, s2, s3), near_masks)]
    (own,) = call(
        gathered_kernel, [flat], [mine, mine_cnt, *parts], flops=1_000_000, limit=8 << 20, name="gathered"
    )
    bit = 8
    while bit < n // 2:
        (own,) = call(
            pair_kernel, [flat], [own, swap(own, bit)], flops=1_000_000, limit=8 << 20, name="pair"
        )
        bit *= 2
    last = swap(own, bit) if bit < n else jnp.zeros_like(own)
    (done,) = call(
        project_kernel, [flat], [own, last, proj_weight, err], flops=1_000_000, limit=8 << 20, name="project"
    )
    peers = [swap(done, m) for m in near_masks]
    across = swap(jnp.stack([done, *peers]), core)
    scale = 1.0 / (tokens * strips * channels)
    book, count, error = call(
        functools.partial(final_kernel, scale, float(clips * tokens * n)),
        [((codes_count, channels), f32), ((SHARDS, LANES), f32), ((8, LANES), f32)],
        [done, *peers, across, ema_sum, counts, err],
        flops=1_000_000,
        limit=8 << 20,
        name="final",
    )
    return (
        latent.reshape(clips, frames, rows, cols, channels),
        book,
        count.reshape(codes_count),
        error[0, :clips],
    )


def solution(mesh):
    in_specs = (
        P("clip", None, "strip", None, None),
        P(),
        P(),
        P(),
        P(),
        P("clip", None, "strip", None),
        P(),
        P(),
    )
    out_specs = (P("clip", None, "strip", None, None), P(), P(), P("clip"))
    return jax.shard_map(body, mesh=mesh, in_specs=in_specs, out_specs=out_specs, check_vma=False)
```

time: 243 us -> 62.3 us (0.26)
  blocking collectives: 102 us -> 0 us
  other arithmetic: 61.8 us -> 0.04 us
  local copies, waits for them, and re-layouts: 34.4 us -> 5.73 us
  Pallas kernels: 0 us -> 21.1 us
  between operations: 16.2 us -> 0.71 us
  matrix products: 12 us -> 0 us
  starting transfers between devices: 5.95 us -> 16.9 us
  waiting for transfers between devices: 8.98 us -> 17.7 us
    psum x6 -> x0, blocking collectives: 92.2 us -> none  [the longest x1 64.9 us: body(): half_sums, half_counts = lax.psum((half_sums, half_counts), 'clip')]
    scatter-add x2 -> x0, other arithmetic: 28.4 us -> none  [the longest x1 15.4 us: body(): jax.ops.segment_sum(jnp.ones(flat_codes.shape, jnp.float32), flat_codes,...]
    pallas_call x0 -> x9, Pallas kernels: none -> 21.1 us  [call(): pl.pallas_call(kernel, out_shape=tuple((jax.ShapeDtypeStruct(s, d) for s,...]
    ppermute x2 -> x12, waiting for transfers between devices: 0.01 us -> 17.7 us  [swap(): return lax.ppermute(x, BOTH, [(i, i ^ mask) for i in range(n)])]
    reduce_sum x10 -> x0, other arithmetic: 12 us -> none  [the longest x4 6.06 us: group_norm(): jnp.sum(deviation * deviation, axis=(1, 2, 3, 5))]
    ppermute x2 -> x12, starting transfers between devices: 5.87 us -> 16.9 us  [swap(): return lax.ppermute(x, BOTH, [(i, i ^ mask) for i in range(n)])]
    conv_general_dilated x1 -> x0, matrix products: 10.3 us -> none  [body(): lax.conv_general_dilated(padded, conv_weight, (1, 1, 1), [(2, 0), (0, 0),...]
    gather x1 -> x0, local copies, waits for them, and re-layouts: 9.82 us -> none  [body(): quantized = jnp.take(old_book, flat_codes, axis=0)]
  transfers between devices with their start and end apart: 4 -> 12, of which waited for: 1 -> 11; matrix products, arithmetic and copies ran while one was open for 15% -> 0% of each run, Pallas kernels for 0% -> 10%
where the time goes in v1:
time: 62.3 us; the launch traced here: 62.1 us
  Pallas kernels  21.1 us (34%)
  waiting for transfers between devices  17.7 us (28%)
  starting transfers between devices  16.9 us (27%)
  local copies, waits for them, and re-layouts  5.73 us (9%)
  between operations  0.71 us (1%)
    pallas_call x9, Pallas kernels, call(): pl.pallas_call(kernel, out_shape=tuple((jax.ShapeDtypeStruct(s, d) for s,...  21.1 us
    ppermute x12, waiting for transfers between devices, swap(): return lax.ppermute(x, BOTH, [(i, i ^ mask) for i in range(n)])  17.7 us
    ppermute x12, starting transfers between devices, swap(): return lax.ppermute(x, BOTH, [(i, i ^ mask) for i in range(n)])  16.9 us
    unnamed x18, local copies, waits for them, and re-layouts  5.14 us
  transfers between devices with their start and end apart: 12, of which 11 were waited for; matrix products, arithmetic and copies ran while one was open for 0% of the time, Pallas kernels for 10%

profile of v1, /device:TPU:0, one launch (start us, length us, event | category | flops | bytes accessed | tf_op | source)
XLA Modules:
  0.0 62.1 jit_solution(11709551744544439931)
XLA Ops:
  0.6 1.2 %copy-done = bf16[2,2,16,32,256]{4,3,2,1,0:T(8,128)(2,1)S(1)} copy-done((bf16[2,2,16,32,256]{4,3,2,1,0:T(8,128)(2,1)S(1)}, bf16[2,2,16,32,256]{4,3,2,1,0:T(8,128)(2,1)}, u32[]{:S(2)}) %copy-start) | copy-done | bytes 1048600
  1.9 1.7 %stats.1 = (bf16[144,256]{1,0:T(8,128)(2,1)S(1)}, f32[16,256]{1,0:T(8,128)S(1)}) custom-call(bf16[2,2,16,32,256]{4,3,2,1,0:T(8,128)(2,1)S(1)} %copy-done), custom_call_target="tpu_custom_call" | custom-call | flops 10000000 | tf_op jit(solution)/shard_map/stats/pallas_call | solution.py:27
  3.6 3.1 %collective-permute-start = (bf16[144,256]{1,0:T(8,128)(2,1)S(1)}, bf16[144,256]{1,0:T(8,128)(2,1)S(1)}, u32[]{:S(2)}, u32[]{:S(2)}) collective-permute-start(bf16[144,256]{1,0:T(8,128)(2,1)S(1)} %get-tuple-element.22), channel_id=1, source_target_pairs={{0,1},{1,0},{2,3},{3,2},{4,5},{5,4},{6,7},{7,6},{8,9},{9,8},{10,11... | collective-permute-start | bytes 221192 | tf_op jit(solution)/shard_map/ppermute | solution.py:393
  6.7 2.3 %collective-permute-done.pay_ref = bf16[144,256]{1,0:T(8,128)(2,1)S(1)} collective-permute-done((bf16[144,256]{1,0:T(8,128)(2,1)S(1)}, bf16[144,256]{1,0:T(8,128)(2,1)S(1)}, u32[]{:S(2)}, u32[]{:S(2)}) %collective-permute-start) | collective-permute-done | bytes 73760 | tf_op jit(solution)/shard_map/ppermute | solution.py:393
  9.0 1.2 %copy-done.1 = bf16[2,2,16,32,256]{4,3,2,1,0:T(8,128)(2,1)S(1)} copy-done((bf16[2,2,16,32,256]{4,3,2,1,0:T(8,128)(2,1)S(1)}, bf16[2,2,16,32,256]{4,3,2,1,0:T(8,128)(2,1)}, u32[]{:S(2)}) %copy-start.1) | copy-done | bytes 1048600
  10.2 2.0 %copy-done.5 = bf16[3,3,3,256,256]{4,3,2,1,0:T(8,128)(2,1)S(1)} copy-done((bf16[3,3,3,256,256]{4,3,2,1,0:T(8,128)(2,1)S(1)}, bf16[3,3,3,256,256]{4,3,2,1,0:T(8,128)(2,1)}, u32[]{:S(2)}) %copy-start.5) | copy-done | bytes 3538968
  12.9 9.6 %conv.1 = (f32[2,1024,256]{2,1,0:T(8,128)S(1)}, f32[16,256]{1,0:T(8,128)S(1)}) custom-call(bf16[2,2,16,32,256]{4,3,2,1,0:T(8,128)(2,1)S(1)} %copy-done.1, bf16[144,256]{1,0:T(8,128)(2,1)S(1)} %collective-permute-done.pay_ref, f32[16,256]{1,0:T(8,128)S(1)} %get-tuple-element.23.loc_ref, f32[1,256]{1,0:T(1,128)S(1)} %bitcast.21, bf16[3,2304,256]{2,1,0:T(8,128)(2,1)S(1)} %bitcast.20), custom_call_target="tpu_custom_call" | custom-call | flops 4000000000 | tf_op jit(solution)/shard_map/conv/pallas_call | solution.py:27
  22.4 2.0 %collective-permute-start.1 = (f32[16,256]{1,0:T(8,128)S(1)}, f32[16,256]{1,0:T(8,128)S(1)}, u32[]{:S(2)}, u32[]{:S(2)}) collective-permute-start(f32[16,256]{1,0:T(8,128)S(1)} %get-tuple-element.25.near_ref), channel_id=1, source_target_pairs={{0,1},{1,0},{2,3},{3,2},{4,5},{5,4},{6,7},{7,6},{8,9},{9,8},{10,11... | collective-permute-start | bytes 49160 | tf_op jit(solution)/shard_map/ppermute | solution.py:393
  24.6 1.6 %collective-permute-done.1.far_ref = f32[16,256]{1,0:T(8,128)S(1)} collective-permute-done((f32[16,256]{1,0:T(8,128)S(1)}, f32[16,256]{1,0:T(8,128)S(1)}, u32[]{:S(2)}, u32[]{:S(2)}) %collective-permute-start.1) | collective-permute-done | bytes 16416 | tf_op jit(solution)/shard_map/ppermute | solution.py:393
  26.2 2.1 %segment.1 = (bf16[2048,256]{1,0:T(8,128)(2,1)S(1)}, bf16[4,136,256]{2,1,0:T(8,128)(2,1)S(1)}, f32[4,128,256]{2,1,0:T(8,128)S(1)}, f32[8,128]{1,0:T(8,128)S(1)}) custom-call(f32[2,1024,256]{2,1,0:T(8,128)S(1)} %get-tuple-element.24.hid_ref, f32[16,256]{1,0:T(8,128)S(1)} %get-tuple-element.25.near_ref, f32[16,256]{1,0:T(8,128)S(1)} %collective-permute-done.1.far_ref, ...), custom_call_target="tpu_custom_call" | custom-call | flops 1500000000 | tf_op jit(solution)/shard_map/segment/pallas_call | solution.py:27
  28.4 1.5 %collective-permute-done.2.got_ref = bf16[4,136,256]{2,1,0:T(8,128)(2,1)S(1)} collective-permute-done((bf16[4,136,256]{2,1,0:T(8,128)(2,1)S(1)}, bf16[4,136,256]{2,1,0:T(8,128)(2,1)S(1)}, u32[]{:S(2)}, u32[]{:S(2)}) %collective-permute-start.2) | collective-permute-done | bytes 278560 | tf_op jit(solution)/shard_map/ppermute | solution.py:393
  30.1 2.1 %collective-permute-start.3 = (bf16[136,256]{1,0:T(8,128)(2,1)S(1)}, bf16[136,256]{1,0:T(8,128)(2,1)S(1)}, u32[]{:S(2)}, u32[]{:S(2)}) collective-permute-start(bf16[136,256]{1,0:T(8,128)(2,1)S(1)} %get-tuple-element.33), channel_id=1, source_target_pairs={{0,1},{1,0},{2,3},{3,2},{4,5},{5,4},{6,7},{7,6},{8,9},{9,8},{10,11... | collective-permute-start | bytes 208904 | tf_op jit(solution)/shard_map/ppermute | solution.py:393
  32.2 1.5 %collective-permute-start.4 = (bf16[136,256]{1,0:T(8,128)(2,1)S(1)}, bf16[136,256]{1,0:T(8,128)(2,1)S(1)}, u32[]{:S(2)}, u32[]{:S(2)}) collective-permute-start(bf16[136,256]{1,0:T(8,128)(2,1)S(1)} %get-tuple-element.34), channel_id=1, source_target_pairs={{0,4},{1,5},{2,6},{3,7},{4,0},{5,1},{6,2},{7,3},{8,12},{9,13},{10,... | collective-permute-start | bytes 208904 | tf_op jit(solution)/shard_map/ppermute | solution.py:393
  34.6 2.5 %collective-permute-done.4.b_ref = bf16[136,256]{1,0:T(8,128)(2,1)S(1)} collective-permute-done((bf16[136,256]{1,0:T(8,128)(2,1)S(1)}, bf16[136,256]{1,0:T(8,128)(2,1)S(1)}, u32[]{:S(2)}, u32[]{:S(2)}) %collective-permute-start.4) | collective-permute-done | bytes 69664 | tf_op jit(solution)/shard_map/ppermute | solution.py:393
  37.2 1.7 %collective-permute-done.5.c_ref = bf16[136,256]{1,0:T(8,128)(2,1)S(1)} collective-permute-done((bf16[136,256]{1,0:T(8,128)(2,1)S(1)}, bf16[136,256]{1,0:T(8,128)(2,1)S(1)}, u32[]{:S(2)}, u32[]{:S(2)}) %collective-permute-start.5) | collective-permute-done | bytes 69664 | tf_op jit(solution)/shard_map/ppermute | solution.py:393
  38.9 1.6 %collective-permute-start.6 = (bf16[136,256]{1,0:T(8,128)(2,1)S(1)}, bf16[136,256]{1,0:T(8,128)(2,1)S(1)}, u32[]{:S(2)}, u32[]{:S(2)}) collective-permute-start(bf16[136,256]{1,0:T(8,128)(2,1)S(1)} %gathered.1.own_ref), channel_id=1, source_target_pairs={{0,8},{1,9},{2,10},{3,11},{4,12},{5,13},{6,14},{7,15},{8,0},{9,1},... | collective-permute-start | bytes 208904 | tf_op jit(solution)/shard_map/ppermute | solution.py:393
  40.5 2.7 %collective-permute-done.6.got_ref = bf16[136,256]{1,0:T(8,128)(2,1)S(1)} collective-permute-done((bf16[136,256]{1,0:T(8,128)(2,1)S(1)}, bf16[136,256]{1,0:T(8,128)(2,1)S(1)}, u32[]{:S(2)}, u32[]{:S(2)}) %collective-permute-start.6) | collective-permute-done | bytes 69664 | tf_op jit(solution)/shard_map/ppermute | solution.py:393
  43.3 2.8 %collective-permute-start.7 = (bf16[136,256]{1,0:T(8,128)(2,1)S(1)}, bf16[136,256]{1,0:T(8,128)(2,1)S(1)}, u32[]{:S(2)}, u32[]{:S(2)}) collective-permute-start(bf16[136,256]{1,0:T(8,128)(2,1)S(1)} %pair.1.own_ref), channel_id=1, source_target_pairs={{0,16},{1,17},{2,18},{3,19},{4,20},{5,21},{6,22},{7,23},{8,24},{9,... | collective-permute-start | bytes 208904 | tf_op jit(solution)/shard_map/ppermute | solution.py:393
  46.1 6.0 %latent.1 = (f32[2048,256]{1,0:T(8,128)}, f32[8,128]{1,0:T(8,128)S(1)}) custom-call(bf16[2048,256]{1,0:T(8,128)(2,1)S(1)} %get-tuple-element.26.act_ref, bf16[256,256]{1,0:T(8,128)(2,1)S(1)} %copy-done.3, s32[16,128]{1,0:T(8,128)S(1)} %reshape.32.codes_ref, f32[1024,256]{1,0:T(8,128)S(1)} %copy-done.2, f32[8,128]{1,0:T(8,128)S(1)} %bitcast.18), custom_call_target="tpu_custom_call" | custom-call | flops 2500000000 | tf_op jit(solution)/shard_map/latent/pallas_call | solution.py:27
  52.3 1.0 %collective-permute-start.10 = (bf16[136,256]{1,0:T(8,128)(2,1)S(1)}, bf16[136,256]{1,0:T(8,128)(2,1)S(1)}, u32[]{:S(2)}, u32[]{:S(2)}) collective-permute-start(bf16[136,256]{1,0:T(8,128)(2,1)S(1)} %project.1.p0), channel_id=1, source_target_pairs={{0,5},{1,4},{2,7},{3,6},{4,1},{5,0},{6,3},{7,2},{8,13},{9,12},{10,... | collective-permute-start | bytes 208904 | tf_op jit(solution)/shard_map/ppermute | solution.py:393
  54.2 1.6 %collective-permute-start.8 = (bf16[136,256]{1,0:T(8,128)(2,1)S(1)}, bf16[136,256]{1,0:T(8,128)(2,1)S(1)}, u32[]{:S(2)}, u32[]{:S(2)}) collective-permute-start(bf16[136,256]{1,0:T(8,128)(2,1)S(1)} %project.1.p0), channel_id=1, source_target_pairs={{0,1},{1,0},{2,3},{3,2},{4,5},{5,4},{6,7},{7,6},{8,9},{9,8},{10,11... | collective-permute-start | bytes 208904 | tf_op jit(solution)/shard_map/ppermute | solution.py:393
  55.8 1.7 %collective-permute-done.10.p3 = bf16[136,256]{1,0:T(8,128)(2,1)S(1)} collective-permute-done((bf16[136,256]{1,0:T(8,128)(2,1)S(1)}, bf16[136,256]{1,0:T(8,128)(2,1)S(1)}, u32[]{:S(2)}, u32[]{:S(2)}) %collective-permute-start.10) | collective-permute-done | bytes 69664 | tf_op jit(solution)/shard_map/ppermute | solution.py:393
  58.7 1.5 %collective-permute-done.11.q_ref = bf16[4,136,256]{2,1,0:T(8,128)(2,1)S(1)} collective-permute-done((bf16[4,136,256]{2,1,0:T(8,128)(2,1)S(1)}, bf16[4,136,256]{2,1,0:T(8,128)(2,1)S(1)}, u32[]{:S(2)}, u32[]{:S(2)}) %collective-permute-start.11) | collective-permute-done | bytes 278560 | tf_op jit(solution)/shard_map/ppermute | solution.py:393
  60.2 1.3 %final.1 = (f32[1024,256]{1,0:T(8,128)}, f32[8,128]{1,0:T(8,128)}, f32[8,128]{1,0:T(8,128)S(1)}) custom-call(bf16[136,256]{1,0:T(8,128)(2,1)S(1)} %project.1.p0, bf16[136,256]{1,0:T(8,128)(2,1)S(1)} %collective-permute-done.8.p1, bf16[136,256]{1,0:T(8,128)(2,1)S(1)} %collective-permute-done.9.p2, bf16[136,256]{1,0:T(8,128)(2,1)S(1)} %collective-permute-done.10.p3, ...), custom_call_target="tpu_custom_call" | custom-call | flops 1000000 | tf_op jit(solution)/shard_map/final/pallas_call | solution.py:27
  (30 shorter events, 4.7 us)
Async XLA Ops:
  0.6 1.2 %copy-start = (bf16[2,2,16,32,256]{4,3,2,1,0:T(8,128)(2,1)S(1)}, bf16[2,2,16,32,256]{4,3,2,1,0:T(8,128)(2,1)}, u32[]{:S(2)}) copy-start(bf16[2,2,16,32,256]{4,3,2,1,0:T(8,128)(2,1)} %video_ref.3) | copy-start | bytes 3145732
  3.6 5.4 %collective-permute-start = (bf16[144,256]{1,0:T(8,128)(2,1)S(1)}, bf16[144,256]{1,0:T(8,128)(2,1)S(1)}, u32[]{:S(2)}, u32[]{:S(2)}) collective-permute-start(bf16[144,256]{1,0:T(8,128)(2,1)S(1)} %get-tuple-element.22), channel_id=1, source_target_pairs={{0,1},{1,0},{2,3},{3,2},{4,5},{5,4},{6,7},{7,6},{8,9},{9,8},{10,11... | collective-permute-start | bytes 221192 | tf_op jit(solution)/shard_map/ppermute | solution.py:393
  9.0 1.2 %copy-start.1 = (bf16[2,2,16,32,256]{4,3,2,1,0:T(8,128)(2,1)S(1)}, bf16[2,2,16,32,256]{4,3,2,1,0:T(8,128)(2,1)}, u32[]{:S(2)}) copy-start(bf16[2,2,16,32,256]{4,3,2,1,0:T(8,128)(2,1)} %video_ref.3) | copy-start | bytes 3145732
  10.2 2.0 %copy-start.5 = (bf16[3,3,3,256,256]{4,3,2,1,0:T(8,128)(2,1)S(1)}, bf16[3,3,3,256,256]{4,3,2,1,0:T(8,128)(2,1)}, u32[]{:S(2)}) copy-start(bf16[3,3,3,256,256]{4,3,2,1,0:T(8,128)(2,1)} %param.10) | copy-start | bytes 10616836
  12.2 0.7 %copy-start.6 = (f32[256]{0:T(256)S(1)}, f32[256]{0:T(256)}, u32[]{:S(2)}) copy-start(f32[256]{0:T(256)} %param.9) | copy-start | bytes 3076
  12.9 11.6 %copy-start.8 = (s32[2,2,16,32]{3,2,1,0:T(8,128)S(1)}, s32[2,2,16,32]{3,2,1,0:T(8,128)}, u32[]{:S(2)}) copy-start(s32[2,2,16,32]{3,2,1,0:T(8,128)} %param.13) | copy-start | bytes 24580
  12.9 13.3 %copy-start.7 = (f32[256]{0:T(256)S(1)}, f32[256]{0:T(256)}, u32[]{:S(2)}) copy-start(f32[256]{0:T(256)} %param.11) | copy-start | bytes 3076
  22.4 3.8 %collective-permute-start.1 = (f32[16,256]{1,0:T(8,128)S(1)}, f32[16,256]{1,0:T(8,128)S(1)}, u32[]{:S(2)}, u32[]{:S(2)}) collective-permute-start(f32[16,256]{1,0:T(8,128)S(1)} %get-tuple-element.25.near_ref), channel_id=1, source_target_pairs={{0,1},{1,0},{2,3},{3,2},{4,5},{5,4},{6,7},{7,6},{8,9},{9,8},{10,11... | collective-permute-start | bytes 49160 | tf_op jit(solution)/shard_map/ppermute | solution.py:393
  26.2 19.9 %copy-start.2 = (f32[1024,256]{1,0:T(8,128)S(1)}, f32[1024,256]{1,0:T(8,128)}, u32[]{:S(2)}) copy-start(f32[1024,256]{1,0:T(8,128)} %sum_ref.3) | copy-start | bytes 3145732
  26.2 19.9 %copy-start.3 = (bf16[256,256]{1,0:T(8,128)(2,1)S(1)}, bf16[256,256]{1,0:T(8,128)(2,1)}, u32[]{:S(2)}) copy-start(bf16[256,256]{1,0:T(8,128)(2,1)} %w_ref.3) | copy-start | bytes 393220
  26.2 19.9 %copy-start.4 = (f32[1024]{0:T(1024)S(1)}, f32[1024]{0:T(1024)}, u32[]{:S(2)}) copy-start(f32[1024]{0:T(1024)} %param.15) | copy-start | bytes 12292
  28.4 1.6 %collective-permute-start.2 = (bf16[4,136,256]{2,1,0:T(8,128)(2,1)S(1)}, bf16[4,136,256]{2,1,0:T(8,128)(2,1)S(1)}, u32[]{:S(2)}, u32[]{:S(2)}) collective-permute-start(bf16[4,136,256]{2,1,0:T(8,128)(2,1)S(1)} %get-tuple-element.30), channel_id=1, source_target_pairs={{0,2},{1,3},{2,0},{3,1},{4,6},{5,7},{6,4},{7,5},{8,10},{9,11},{10,... | collective-permute-start | bytes 835592 | tf_op jit(solution)/shard_map/ppermute | solution.py:393
  30.1 4.6 %collective-permute-start.3 = (bf16[136,256]{1,0:T(8,128)(2,1)S(1)}, bf16[136,256]{1,0:T(8,128)(2,1)S(1)}, u32[]{:S(2)}, u32[]{:S(2)}) collective-permute-start(bf16[136,256]{1,0:T(8,128)(2,1)S(1)} %get-tuple-element.33), channel_id=1, source_target_pairs={{0,1},{1,0},{2,3},{3,2},{4,5},{5,4},{6,7},{7,6},{8,9},{9,8},{10,11... | collective-permute-start | bytes 208904 | tf_op jit(solution)/shard_map/ppermute | solution.py:393
  32.2 5.0 %collective-permute-start.4 = (bf16[136,256]{1,0:T(8,128)(2,1)S(1)}, bf16[136,256]{1,0:T(8,128)(2,1)S(1)}, u32[]{:S(2)}, u32[]{:S(2)}) collective-permute-start(bf16[136,256]{1,0:T(8,128)(2,1)S(1)} %get-tuple-element.34), channel_id=1, source_target_pairs={{0,4},{1,5},{2,6},{3,7},{4,0},{5,1},{6,2},{7,3},{8,12},{9,13},{10,... | collective-permute-start | bytes 208904 | tf_op jit(solution)/shard_map/ppermute | solution.py:393
  33.6 5.2 %collective-permute-start.5 = (bf16[136,256]{1,0:T(8,128)(2,1)S(1)}, bf16[136,256]{1,0:T(8,128)(2,1)S(1)}, u32[]{:S(2)}, u32[]{:S(2)}) collective-permute-start(bf16[136,256]{1,0:T(8,128)(2,1)S(1)} %get-tuple-element.35), channel_id=1, source_target_pairs={{0,5},{1,4},{2,7},{3,6},{4,1},{5,0},{6,3},{7,2},{8,13},{9,12},{10,... | collective-permute-start | bytes 208904 | tf_op jit(solution)/shard_map/ppermute | solution.py:393
  38.9 4.4 %collective-permute-start.6 = (bf16[136,256]{1,0:T(8,128)(2,1)S(1)}, bf16[136,256]{1,0:T(8,128)(2,1)S(1)}, u32[]{:S(2)}, u32[]{:S(2)}) collective-permute-start(bf16[136,256]{1,0:T(8,128)(2,1)S(1)} %gathered.1.own_ref), channel_id=1, source_target_pairs={{0,8},{1,9},{2,10},{3,11},{4,12},{5,13},{6,14},{7,15},{8,0},{9,1},... | collective-permute-start | bytes 208904 | tf_op jit(solution)/shard_map/ppermute | solution.py:393
  43.3 8.8 %collective-permute-start.7 = (bf16[136,256]{1,0:T(8,128)(2,1)S(1)}, bf16[136,256]{1,0:T(8,128)(2,1)S(1)}, u32[]{:S(2)}, u32[]{:S(2)}) collective-permute-start(bf16[136,256]{1,0:T(8,128)(2,1)S(1)} %pair.1.own_ref), channel_id=1, source_target_pairs={{0,16},{1,17},{2,18},{3,19},{4,20},{5,21},{6,22},{7,23},{8,24},{9,... | collective-permute-start | bytes 208904 | tf_op jit(solution)/shard_map/ppermute | solution.py:393
  52.3 5.3 %collective-permute-start.10 = (bf16[136,256]{1,0:T(8,128)(2,1)S(1)}, bf16[136,256]{1,0:T(8,128)(2,1)S(1)}, u32[]{:S(2)}, u32[]{:S(2)}) collective-permute-start(bf16[136,256]{1,0:T(8,128)(2,1)S(1)} %project.1.p0), channel_id=1, source_target_pairs={{0,5},{1,4},{2,7},{3,6},{4,1},{5,0},{6,3},{7,2},{8,13},{9,12},{10,... | collective-permute-start | bytes 208904 | tf_op jit(solution)/shard_map/ppermute | solution.py:393
  53.3 4.3 %collective-permute-start.9 = (bf16[136,256]{1,0:T(8,128)(2,1)S(1)}, bf16[136,256]{1,0:T(8,128)(2,1)S(1)}, u32[]{:S(2)}, u32[]{:S(2)}) collective-permute-start(bf16[136,256]{1,0:T(8,128)(2,1)S(1)} %project.1.p0), channel_id=1, source_target_pairs={{0,4},{1,5},{2,6},{3,7},{4,0},{5,1},{6,2},{7,3},{8,12},{9,13},{10,... | collective-permute-start | bytes 208904 | tf_op jit(solution)/shard_map/ppermute | solution.py:393
  54.2 4.3 %collective-permute-start.8 = (bf16[136,256]{1,0:T(8,128)(2,1)S(1)}, bf16[136,256]{1,0:T(8,128)(2,1)S(1)}, u32[]{:S(2)}, u32[]{:S(2)}) collective-permute-start(bf16[136,256]{1,0:T(8,128)(2,1)S(1)} %project.1.p0), channel_id=1, source_target_pairs={{0,1},{1,0},{2,3},{3,2},{4,5},{5,4},{6,7},{7,6},{8,9},{9,8},{10,11... | collective-permute-start | bytes 208904 | tf_op jit(solution)/shard_map/ppermute | solution.py:393
  58.6 1.6 %collective-permute-start.11 = (bf16[4,136,256]{2,1,0:T(8,128)(2,1)S(1)}, bf16[4,136,256]{2,1,0:T(8,128)(2,1)S(1)}, u32[]{:S(2)}, u32[]{:S(2)}) collective-permute-start(bf16[4,136,256]{2,1,0:T(8,128)(2,1)S(1)} %pad_maximum_fusion), channel_id=1, source_target_pairs={{0,2},{1,3},{2,0},{3,1},{4,6},{5,7},{6,4},{7,5},{8,10},{9,11},{10,... | collective-permute-start | bytes 835592 | tf_op jit(solution)/shard_map/ppermute | solution.py:393

commit v2 on v1

--- a/solution.py
+++ b/solution.py
@@ -23,13 +23,15 @@
 VSPEC = pl.BlockSpec(memory_space=pltpu.VMEM)
 
 
-def call(kernel, outs, args, scratch=(), flops=0, limit=None, name=None):
+def call(kernel, outs, args, scratch=(), flops=0, limit=None, name=None, far=(), far_outs=(), alias=None):
+    far_spec = pl.BlockSpec(memory_space=pltpu.HBM)
     return pl.pallas_call(
         kernel,
         out_shape=tuple(jax.ShapeDtypeStruct(s, d) for s, d in outs),
-        in_specs=[VSPEC] * len(args),
-        out_specs=tuple(VSPEC for _ in outs),
+        in_specs=[far_spec if i in far else VSPEC for i in range(len(args))],
+        out_specs=tuple(far_spec if i in far_outs else VSPEC for i in range(len(outs))),
         scratch_shapes=list(scratch),
+        input_output_aliases=alias or {},
         compiler_params=pltpu.CompilerParams(vmem_limit_bytes=limit),
         cost_estimate=pl.CostEstimate(flops=flops, bytes_accessed=0, transcendentals=0),
         name=name,
@@ -48,11 +50,14 @@
     shift = (channels // GROUPS).bit_length() - 1
     rows = lax.broadcasted_iota(jnp.int32, (channels, channels), 0) >> shift
     cols = lax.broadcasted_iota(jnp.int32, (channels, channels), 1) >> shift
-    return jnp.where(rows == cols, 1.0, 0.0).astype(f32)
+    return jnp.where(rows == cols, 1.0, 0.0).astype(bf16)
 
 
 def group_total(rows, matrix):
-    return jnp.dot(rows, matrix, precision=lax.Precision.HIGHEST, preferred_element_type=f32)
+    split = [p.astype(f32) for p in pieces(rows)]
+    split = jnp.concatenate(split + [jnp.zeros_like(rows)], axis=0).astype(bf16)
+    total = jnp.dot(split, matrix, preferred_element_type=f32)
+    return total[0:8] + total[8:16] + total[16:24]
 
 
 def stacked(rows, channels):
@@ -69,7 +74,7 @@
     sums = []
     for c in range(clips):
         total = lax.fori_loop(
-            0, blocks, lambda i, acc: acc + read(c, i), jnp.zeros((rows, channels), f32), unroll=4
+            0, blocks, lambda i, acc: acc + read(c, i), jnp.zeros((rows, channels), f32), unroll=8
         )
         sums.append(jnp.sum(total, axis=0, keepdims=True))
     means = group_total(stacked(sums, channels), matrix) / members
@@ -81,7 +86,7 @@
             away = read(c, i) - mean
             return acc + away * away
 
-        total = lax.fori_loop(0, blocks, step, jnp.zeros((rows, channels), f32), unroll=4)
+        total = lax.fori_loop(0, blocks, step, jnp.zeros((rows, channels), f32), unroll=8)
         squares.append(jnp.sum(total, axis=0, keepdims=True))
     squares = group_total(stacked(squares, channels), matrix)
     return means, squares, members
@@ -99,9 +104,19 @@
     return half + half * jnp.tanh(half)
 
 
-def stats_kernel(video_ref, pay_ref, loc_ref):
+def stats_kernel(video_hbm, w_hbm, pay_ref, loc_ref, video_ref, w_ref, sems):
     clips, frames, rows, cols, channels = video_ref.shape
     strip = lax.axis_index("strip")
+    loads = [
+        pltpu.make_async_copy(video_hbm.at[c], video_ref.at[c], sems.at[c]) for c in range(clips)
+    ]
+    first_tap = w_hbm.shape[0] - w_ref.shape[0]
+    taps = pltpu.make_async_copy(w_hbm.at[pl.ds(first_tap, w_ref.shape[0])], w_ref, sems.at[clips])
+    for load in loads:
+        load.start()
+    taps.start()
+    for load in loads:
+        load.wait()
     edge = (1 - strip) * (rows - 1)
     for c in range(clips):
         for t in range(frames):
@@ -123,6 +138,7 @@
             for c in range(clips):
                 out = jnp.where(row == (j * clips + c) * 3 + k, piece[c : c + 1], out)
     pay_ref[base : base + 16] = out.astype(bf16)
+    taps.wait()
 
 
 def conv_kernel(video_ref, pay_ref, loc_ref, gain_ref, w_ref, hid_ref, st_ref, buf_ref):
@@ -130,6 +146,7 @@
     strip = lax.axis_index("strip")
     members = frames * rows * cols * (channels // GROUPS)
     base = clips * frames * cols
+    first_tap = 3 - w_ref.shape[0]
     far = pay_ref[base : base + 16].astype(f32)
     gain = gain_ref[...]
     col = lax.broadcasted_iota(jnp.int32, (cols, channels), 0)
@@ -154,7 +171,7 @@
                 put(c, t, r + 1, silu((x - mean) * scale))
                 return carry
 
-            lax.fori_loop(0, rows, row_step, 0, unroll=4)
+            lax.fori_loop(0, rows, row_step, 0, unroll=True)
             where_at = (c * frames + t) * cols
             halo = silu((pay_ref[where_at : where_at + cols].astype(f32) - mean) * scale)
             put(c, t, 0, jnp.where(strip > 0, halo, 0.0))
@@ -174,7 +191,7 @@
             for a in range(3):
                 if t + a - 2 >= 0:
                     total = total + jnp.dot(
-                        patches(t + a - 2), w_ref[a], preferred_element_type=f32
+                        patches(t + a - 2), w_ref[a - first_tap], preferred_element_type=f32
                     )
             hid_ref[c, t * rows * cols : (t + 1) * rows * cols] = total
 
@@ -233,7 +250,7 @@
             act_ref[pl.ds(pl.multiple_of(c * tokens + i * block, block), block)] = act
             return carry
 
-        lax.fori_loop(0, tokens // block, step, 0, unroll=2)
+        lax.fori_loop(0, tokens // block, step, 0, unroll=True)
 
     me = shard_bits()
     codes_count = acc_ref.shape[0]
@@ -285,7 +302,7 @@
             out[share:] = tail_rows(count)
 
 
-def gathered_kernel(mine_ref, mcnt_ref, a_ref, b_ref, c_ref, out_ref):
+def gathered_kernel(mine_ref, mcnt_ref, a_ref, b_ref, c_ref, after_ref, out_ref):
     share = mine_ref.shape[0]
     value = mine_ref[...]
     count = mcnt_ref[0:1]
@@ -321,7 +338,7 @@
     return jnp.transpose(jnp.broadcast_to(row, (LANES, LANES)))
 
 
-def latent_kernel(act_ref, w_ref, codes_ref, sum_ref, cnt_ref, lat_ref, err_ref, head_ref, rest_ref):
+def latent_kernel(act_ref, w_ref, codes_ref, sum_ref, cnt_ref, after_ref, lat_ref, err_ref, head_ref, rest_ref):
     tokens, channels = lat_ref.shape
     codes_count = sum_ref.shape[0]
     clips = 2
@@ -356,28 +373,54 @@
             away = away * away
             return acc + jnp.sum(away.reshape(LANES // 8, 8, channels), axis=0)
 
-        total = lax.fori_loop(0, per_clip, step, jnp.zeros((8, channels), f32), unroll=2)
+        total = lax.fori_loop(0, per_clip, step, jnp.zeros((8, channels), f32), unroll=True)
         errors = jnp.where(lane == c, jnp.sum(total), errors)
     err_ref[...] = jnp.broadcast_to(errors, (8, LANES))
 
 
-def final_kernel(scale, tokens, p0, p1, p2, p3, q_ref, sum_ref, cnt_ref, err_ref, book_ref, count_ref, error_ref):
+def book_kernel(first, tokens, *refs):
+    parts, (sum_ref, cnt_ref), rest = refs[:-8], refs[-8:-6], refs[-6:]
+    _, _, book_hbm, count_ref, page_ref, sems = rest
+    me = shard_bits()
     share = LANES
-    me = shard_bits()
+    channels = sum_ref.shape[1]
     grand = ema_decay * jnp.sum(cnt_ref[...]) + (1.0 - ema_decay) * tokens
-    for p in range(SHARDS):
-        src = (p0, p1, p2, p3)[p] if p < 4 else q_ref.at[p - 4]
-        shard = p ^ me
+    copies = []
+    for i in range(SHARDS // 2):
+        src = parts[i] if len(parts) > 1 else parts[0].at[i]
+        shard = (first + i) ^ me
         count = ema_decay * cnt_ref[pl.ds(shard, 1)] + (1.0 - ema_decay) * untail(src[share:])
-        count_ref[pl.ds(shard, 1)] = count
+        count_ref[i : i + 1] = count
         smooth = (count + smooth_eps) / (grand + SHARDS * share * smooth_eps) * grand
-        divisor = as_column(smooth)
-        channels = book_ref.shape[1]
-        divisor = jnp.concatenate([divisor] * (channels // LANES), axis=1)
+        inverse = as_column(1.0 / smooth)
+        inverse = jnp.concatenate([inverse] * (channels // LANES), axis=1)
         at = pl.ds(pl.multiple_of(shard * share, share), share)
         fresh = ema_decay * sum_ref[at] + (1.0 - ema_decay) * src[:share].astype(f32)
-        book_ref[at] = fresh / divisor
-    error_ref[...] = jnp.broadcast_to((err_ref[0:1] + untail(p1[share:], 1)) * scale, (8, LANES))
+        page_ref[i] = fresh * inverse
+        copies.append(pltpu.make_async_copy(page_ref.at[i], book_hbm.at[at], sems.at[i]))
+        copies[-1].start()
+    for copy in copies:
+        copy.wait()
+
+
+def early_kernel(tokens, p0, p1, p2, p3, sum_ref, cnt_ref, book_hbm, count_ref, page_ref, sems):
+    book_kernel(0, tokens, p0, p1, p2, p3, sum_ref, cnt_ref, None, None, book_hbm, count_ref, page_ref, sems)
+
+
+def late_kernel(tokens, q_ref, sum_ref, cnt_ref, book_in, early_ref, book_hbm, count_ref, page_ref, late_ref, sems):
+    book_kernel(
+        SHARDS // 2, tokens, q_ref, sum_ref, cnt_ref, None, None, book_hbm, late_ref, page_ref, sems
+    )
+    me = shard_bits()
+    for i in range(SHARDS // 2):
+        count_ref[pl.ds(i ^ me, 1)] = early_ref[i : i + 1]
+        count_ref[pl.ds((SHARDS // 2 + i) ^ me, 1)] = late_ref[i : i + 1]
+
+
+def error_kernel(scale, p1, err_ref, error_ref):
+    error_ref[...] = jnp.broadcast_to(
+        (err_ref[0:1] + untail(p1[LANES:], 1)) * scale, (8, LANES)
+    )
 
 
 def body(video, gain_first, conv_weight, gain_second, proj_weight, codes, ema_sum, ema_count):
@@ -394,21 +437,27 @@
 
     tokens = frames * rows * cols
     halo = clips * frames * cols
-    pay, near = call(
+    pay, near, held, taps = call(
         stats_kernel,
-        [((halo + 16, channels), bf16), ((16, channels), f32)],
-        [video],
+        [
+            ((halo + 16, channels), bf16),
+            ((16, channels), f32),
+            (video.shape, bf16),
+            ((min(3, frames), 9 * channels, channels), bf16),
+        ],
+        [pltpu.with_memory_space_constraint(video, pltpu.HBM), pltpu.with_memory_space_constraint(conv_weight.reshape(3, 9 * channels, channels), pltpu.HBM)],
+        scratch=[pltpu.SemaphoreType.DMA((clips + 1,))],
         flops=10_000_000,
-        limit=8 << 20,
+        limit=16 << 20,
         name="stats",
+        far=(0, 1),
     )
     far_pay = swap(pay, 1)
     code_lines = codes.reshape(-1, LANES)
-    weights = conv_weight.reshape(3, 9 * channels, channels)
     hidden, near_two = call(
         conv_kernel,
         [((clips, tokens, channels), f32), ((16, channels), f32)],
-        [video, far_pay, near, gain_first.reshape(1, channels), weights],
+        [held, far_pay, near, gain_first.reshape(1, channels), taps],
         scratch=[VMEM((clips, frames, rows + 2, cols, 3 * channels), bf16)],
         flops=4_000_000_000,
         limit=24 << 20,
@@ -432,15 +481,6 @@
     core, x_bit = 2, 4
     got = swap(send, core)
     counts = ema_count.reshape(SHARDS, LANES)
-    latent, err = call(
-        latent_kernel,
-        [((clips * tokens, channels), f32), ((8, LANES), f32)],
-        [act, proj_weight, code_lines, ema_sum, counts],
-        scratch=[VMEM((codes_count, channels), bf16)] * 2,
-        flops=2_500_000_000,
-        limit=24 << 20,
-        name="latent",
-    )
     flat = ((share + TAIL, channels), bf16)
     mine, mine_cnt, s1, s2, s3 = call(
         quarter_kernel,
@@ -452,8 +492,17 @@
     )
     near_masks = (1, x_bit, 1 | x_bit)
     parts = [swap(s, m) for s, m in zip((s1, s2, s3), near_masks)]
+    latent, err = call(
+        latent_kernel,
+        [((clips * tokens, channels), f32), ((8, LANES), f32)],
+        [act, proj_weight, code_lines, ema_sum, counts, mine_cnt],
+        scratch=[VMEM((codes_count, channels), bf16)] * 2,
+        flops=2_500_000_000,
+        limit=24 << 20,
+        name="latent",
+    )
     (own,) = call(
-        gathered_kernel, [flat], [mine, mine_cnt, *parts], flops=1_000_000, limit=8 << 20, name="gathered"
+        gathered_kernel, [flat], [mine, mine_cnt, *parts, err], flops=1_000_000, limit=8 << 20, name="gathered"
     )
     bit = 8
     while bit < n // 2:
@@ -468,13 +517,39 @@
     peers = [swap(done, m) for m in near_masks]
     across = swap(jnp.stack([done, *peers]), core)
     scale = 1.0 / (tokens * strips * channels)
-    book, count, error = call(
-        functools.partial(final_kernel, scale, float(clips * tokens * n)),
-        [((codes_count, channels), f32), ((SHARDS, LANES), f32), ((8, LANES), f32)],
-        [done, *peers, across, ema_sum, counts, err],
+    total_tokens = float(clips * tokens * n)
+    half = SHARDS // 2
+    (error,) = call(
+        functools.partial(error_kernel, scale),
+        [((8, LANES), f32)],
+        [peers[0], err],
         flops=1_000_000,
         limit=8 << 20,
-        name="final",
+        name="error",
+    )
+    page = VMEM((half, share, channels), f32)
+    book_shape = ((codes_count, channels), f32)
+    book, early = call(
+        functools.partial(early_kernel, total_tokens),
+        [book_shape, ((8, LANES), f32)],
+        [done, *peers, ema_sum, counts],
+        scratch=[page, pltpu.SemaphoreType.DMA((half,))],
+        flops=1_000_000,
+        limit=8 << 20,
+        name="early",
+        far_outs=(0,),
+    )
+    book, count = call(
+        functools.partial(late_kernel, total_tokens),
+        [book_shape, ((SHARDS, LANES), f32)],
+        [across, ema_sum, counts, book, early],
+        scratch=[page, VMEM((8, LANES), f32), pltpu.SemaphoreType.DMA((half,))],
+        flops=1_000_000,
+        limit=8 << 20,
+        name="late",
+        far=(3,),
+        far_outs=(0,),
+        alias={3: 0},
     )
     return (
         latent.reshape(clips, frames, rows, cols, channels),

time: 62.3 us -> 49.6 us (0.80)
  local copies, waits for them, and re-layouts: 5.73 us -> 0.61 us
  Pallas kernels: 21.1 us -> 16.3 us
  waiting for transfers between devices: 17.7 us -> 15.1 us
    unnamed x18 -> x12, local copies, waits for them, and re-layouts: 5.14 us -> 0.02 us
    pallas_call x9 -> x11, Pallas kernels: 21.1 us -> 16.3 us  [call(): pl.pallas_call(kernel, out_shape=tuple((jax.ShapeDtypeStruct(s, d) for s,...]
    ppermute x12, waiting for transfers between devices: 17.7 us -> 15.1 us  [swap(): return lax.ppermute(x, BOTH, [(i, i ^ mask) for i in range(n)])]
  transfers between devices with their start and end apart: 12 -> 12, of which waited for: 11 -> 9; matrix products, arithmetic and copies ran while one was open for 0% -> 1% of each run, Pallas kernels for 10% -> 11%
where the time goes in v2:
time: 49.6 us; the launch traced here: 49.4 us
  starting transfers between devices  16.7 us (34%)
  Pallas kernels  16.3 us (33%)
  waiting for transfers between devices  15.1 us (30%)
  between operations  0.72 us (1%)
  local copies, waits for them, and re-layouts  0.61 us (1%)
    ppermute x12, starting transfers between devices, swap(): return lax.ppermute(x, BOTH, [(i, i ^ mask) for i in range(n)])  16.7 us
    pallas_call x11, Pallas kernels, call(): pl.pallas_call(kernel, out_shape=tuple((jax.ShapeDtypeStruct(s, d) for s,...  16.3 us
    ppermute x12, waiting for transfers between devices, swap(): return lax.ppermute(x, BOTH, [(i, i ^ mask) for i in range(n)])  15.1 us
  transfers between devices with their start and end apart: 12, of which 9 were waited for; matrix products, arithmetic and copies ran while one was open for 1% of the time, Pallas kernels for 11%

profile of v2, /device:TPU:0, one launch (start us, length us, event | category | flops | bytes accessed | tf_op | source)
XLA Modules:
  0.0 49.4 jit_solution(2443093608166654785)
XLA Ops:
  0.6 2.5 %stats.1 = (bf16[144,256]{1,0:T(8,128)(2,1)S(1)}, f32[16,256]{1,0:T(8,128)S(1)}, bf16[2,2,16,32,256]{4,3,2,1,0:T(8,128)(2,1)S(1)}, bf16[2,2304,256]{2,1,0:T(8,128)(2,1)S(1)}) custom-call(bf16[2,2,16,32,256]{4,3,2,1,0:T(8,128)(2,1)} %video_hbm.1, bf16[3,2304,256]{2,1,0:T(8,128)(2,1)} %bitcast.23), custom_call_target="tpu_custom_call" | custom-call | flops 10000000 | tf_op jit(solution)/shard_map/stats/pallas_call | solution.py:28
  3.2 3.1 %collective-permute-start = (bf16[144,256]{1,0:T(8,128)(2,1)S(1)}, bf16[144,256]{1,0:T(8,128)(2,1)S(1)}, u32[]{:S(2)}, u32[]{:S(2)}) collective-permute-start(bf16[144,256]{1,0:T(8,128)(2,1)S(1)} %get-tuple-element.26), channel_id=1, source_target_pairs={{0,1},{1,0},{2,3},{3,2},{4,5},{5,4},{6,7},{7,6},{8,9},{9,8},{10,11... | collective-permute-start | bytes 221192 | tf_op jit(solution)/shard_map/ppermute | solution.py:436
  6.2 2.3 %collective-permute-done.pay_ref = bf16[144,256]{1,0:T(8,128)(2,1)S(1)} collective-permute-done((bf16[144,256]{1,0:T(8,128)(2,1)S(1)}, bf16[144,256]{1,0:T(8,128)(2,1)S(1)}, u32[]{:S(2)}, u32[]{:S(2)}) %collective-permute-start) | collective-permute-done | bytes 73760 | tf_op jit(solution)/shard_map/ppermute | solution.py:436
  8.6 4.8 %conv.1 = (f32[2,1024,256]{2,1,0:T(8,128)S(1)}, f32[16,256]{1,0:T(8,128)S(1)}) custom-call(bf16[2,2,16,32,256]{4,3,2,1,0:T(8,128)(2,1)S(1)} %get-tuple-element.25.video_ref, bf16[144,256]{1,0:T(8,128)(2,1)S(1)} %collective-permute-done.pay_ref, f32[16,256]{1,0:T(8,128)S(1)} %get-tuple-element.27.loc_ref, f32[1,256]{1,0:T(1,128)S(1)} %bitcast.21, ...), custom_call_target="tpu_custom_call" | custom-call | flops 4000000000 | tf_op jit(solution)/shard_map/conv/pallas_call | solution.py:28
  13.4 2.0 %collective-permute-start.1 = (f32[16,256]{1,0:T(8,128)S(1)}, f32[16,256]{1,0:T(8,128)S(1)}, u32[]{:S(2)}, u32[]{:S(2)}) collective-permute-start(f32[16,256]{1,0:T(8,128)S(1)} %get-tuple-element.30.near_ref), channel_id=1, source_target_pairs={{0,1},{1,0},{2,3},{3,2},{4,5},{5,4},{6,7},{7,6},{8,9},{9,8},{10,11... | collective-permute-start | bytes 49160 | tf_op jit(solution)/shard_map/ppermute | solution.py:436
  15.5 1.6 %collective-permute-done.1.far_ref = f32[16,256]{1,0:T(8,128)S(1)} collective-permute-done((f32[16,256]{1,0:T(8,128)S(1)}, f32[16,256]{1,0:T(8,128)S(1)}, u32[]{:S(2)}, u32[]{:S(2)}) %collective-permute-start.1) | collective-permute-done | bytes 16416 | tf_op jit(solution)/shard_map/ppermute | solution.py:436
  17.1 1.7 %segment.1 = (bf16[2048,256]{1,0:T(8,128)(2,1)S(1)}, bf16[4,136,256]{2,1,0:T(8,128)(2,1)S(1)}, f32[4,128,256]{2,1,0:T(8,128)S(1)}, f32[8,128]{1,0:T(8,128)S(1)}) custom-call(f32[2,1024,256]{2,1,0:T(8,128)S(1)} %get-tuple-element.29.hid_ref, f32[16,256]{1,0:T(8,128)S(1)} %get-tuple-element.30.near_ref, f32[16,256]{1,0:T(8,128)S(1)} %collective-permute-done.1.far_ref, ...), custom_call_target="tpu_custom_call" | custom-call | flops 1500000000 | tf_op jit(solution)/shard_map/segment/pallas_call | solution.py:28
  18.9 1.5 %collective-permute-done.2.got_ref = bf16[4,136,256]{2,1,0:T(8,128)(2,1)S(1)} collective-permute-done((bf16[4,136,256]{2,1,0:T(8,128)(2,1)S(1)}, bf16[4,136,256]{2,1,0:T(8,128)(2,1)S(1)}, u32[]{:S(2)}, u32[]{:S(2)}) %collective-permute-start.2) | collective-permute-done | bytes 278560 | tf_op jit(solution)/shard_map/ppermute | solution.py:436
  20.5 2.1 %collective-permute-start.3 = (bf16[136,256]{1,0:T(8,128)(2,1)S(1)}, bf16[136,256]{1,0:T(8,128)(2,1)S(1)}, u32[]{:S(2)}, u32[]{:S(2)}) collective-permute-start(bf16[136,256]{1,0:T(8,128)(2,1)S(1)} %get-tuple-element.38), channel_id=1, source_target_pairs={{0,1},{1,0},{2,3},{3,2},{4,5},{5,4},{6,7},{7,6},{8,9},{9,8},{10,11... | collective-permute-start | bytes 208904 | tf_op jit(solution)/shard_map/ppermute | solution.py:436
  22.6 1.5 %collective-permute-start.4 = (bf16[136,256]{1,0:T(8,128)(2,1)S(1)}, bf16[136,256]{1,0:T(8,128)(2,1)S(1)}, u32[]{:S(2)}, u32[]{:S(2)}) collective-permute-start(bf16[136,256]{1,0:T(8,128)(2,1)S(1)} %get-tuple-element.39), channel_id=1, source_target_pairs={{0,4},{1,5},{2,6},{3,7},{4,0},{5,1},{6,2},{7,3},{8,12},{9,13},{10,... | collective-permute-start | bytes 208904 | tf_op jit(solution)/shard_map/ppermute | solution.py:436
  24.2 4.2 %latent.1 = (f32[2048,256]{1,0:T(8,128)}, f32[8,128]{1,0:T(8,128)S(1)}) custom-call(bf16[2048,256]{1,0:T(8,128)(2,1)S(1)} %get-tuple-element.31.act_ref, bf16[256,256]{1,0:T(8,128)(2,1)S(1)} %copy-done.1, s32[16,128]{1,0:T(8,128)S(1)} %reshape.32.codes_ref, f32[1024,256]{1,0:T(8,128)S(1)} %copy-done, f32[8,128]{1,0:T(8,128)S(1)} %bitcast.18, ...), custom_call_target="tpu_custom_call" | custom-call | flops 2500000000 | tf_op jit(solution)/shard_map/latent/pallas_call | solution.py:28
  28.4 0.9 %collective-permute-done.5.c_ref = bf16[136,256]{1,0:T(8,128)(2,1)S(1)} collective-permute-done((bf16[136,256]{1,0:T(8,128)(2,1)S(1)}, bf16[136,256]{1,0:T(8,128)(2,1)S(1)}, u32[]{:S(2)}, u32[]{:S(2)}) %collective-permute-start.5) | collective-permute-done | bytes 69664 | tf_op jit(solution)/shard_map/ppermute | solution.py:436
  29.4 1.6 %collective-permute-start.6 = (bf16[136,256]{1,0:T(8,128)(2,1)S(1)}, bf16[136,256]{1,0:T(8,128)(2,1)S(1)}, u32[]{:S(2)}, u32[]{:S(2)}) collective-permute-start(bf16[136,256]{1,0:T(8,128)(2,1)S(1)} %gathered.1.own_ref), channel_id=1, source_target_pairs={{0,8},{1,9},{2,10},{3,11},{4,12},{5,13},{6,14},{7,15},{8,0},{9,1},... | collective-permute-start | bytes 208904 | tf_op jit(solution)/shard_map/ppermute | solution.py:436
  31.0 2.7 %collective-permute-done.6.got_ref = bf16[136,256]{1,0:T(8,128)(2,1)S(1)} collective-permute-done((bf16[136,256]{1,0:T(8,128)(2,1)S(1)}, bf16[136,256]{1,0:T(8,128)(2,1)S(1)}, u32[]{:S(2)}, u32[]{:S(2)}) %collective-permute-start.6) | collective-permute-done | bytes 69664 | tf_op jit(solution)/shard_map/ppermute | solution.py:436
  33.8 2.7 %collective-permute-start.7 = (bf16[136,256]{1,0:T(8,128)(2,1)S(1)}, bf16[136,256]{1,0:T(8,128)(2,1)S(1)}, u32[]{:S(2)}, u32[]{:S(2)}) collective-permute-start(bf16[136,256]{1,0:T(8,128)(2,1)S(1)} %pair.1.own_ref), channel_id=1, source_target_pairs={{0,16},{1,17},{2,18},{3,19},{4,20},{5,21},{6,22},{7,23},{8,24},{9,... | collective-permute-start | bytes 208904 | tf_op jit(solution)/shard_map/ppermute | solution.py:436
  36.4 2.6 %collective-permute-done.7.got_ref = bf16[136,256]{1,0:T(8,128)(2,1)S(1)} collective-permute-done((bf16[136,256]{1,0:T(8,128)(2,1)S(1)}, bf16[136,256]{1,0:T(8,128)(2,1)S(1)}, u32[]{:S(2)}, u32[]{:S(2)}) %collective-permute-start.7) | collective-permute-done | bytes 69664 | tf_op jit(solution)/shard_map/ppermute | solution.py:436
  39.2 1.1 %collective-permute-start.8 = (bf16[136,256]{1,0:T(8,128)(2,1)S(1)}, bf16[136,256]{1,0:T(8,128)(2,1)S(1)}, u32[]{:S(2)}, u32[]{:S(2)}) collective-permute-start(bf16[136,256]{1,0:T(8,128)(2,1)S(1)} %project.1.p0), channel_id=1, source_target_pairs={{0,1},{1,0},{2,3},{3,2},{4,5},{5,4},{6,7},{7,6},{8,9},{9,8},{10,11... | collective-permute-start | bytes 208904 | tf_op jit(solution)/shard_map/ppermute | solution.py:436
  40.3 1.4 %collective-permute-start.10 = (bf16[136,256]{1,0:T(8,128)(2,1)S(1)}, bf16[136,256]{1,0:T(8,128)(2,1)S(1)}, u32[]{:S(2)}, u32[]{:S(2)}) collective-permute-start(bf16[136,256]{1,0:T(8,128)(2,1)S(1)} %project.1.p0), channel_id=1, source_target_pairs={{0,5},{1,4},{2,7},{3,6},{4,1},{5,0},{6,3},{7,2},{8,13},{9,12},{10,... | collective-permute-start | bytes 208904 | tf_op jit(solution)/shard_map/ppermute | solution.py:436
  41.8 1.0 %collective-permute-start.9 = (bf16[136,256]{1,0:T(8,128)(2,1)S(1)}, bf16[136,256]{1,0:T(8,128)(2,1)S(1)}, u32[]{:S(2)}, u32[]{:S(2)}) collective-permute-start(bf16[136,256]{1,0:T(8,128)(2,1)S(1)} %project.1.p0), channel_id=1, source_target_pairs={{0,4},{1,5},{2,6},{3,7},{4,0},{5,1},{6,2},{7,3},{8,12},{9,13},{10,... | collective-permute-start | bytes 208904 | tf_op jit(solution)/shard_map/ppermute | solution.py:436
  42.8 0.8 %collective-permute-done.8.p1 = bf16[136,256]{1,0:T(8,128)(2,1)S(1)} collective-permute-done((bf16[136,256]{1,0:T(8,128)(2,1)S(1)}, bf16[136,256]{1,0:T(8,128)(2,1)S(1)}, u32[]{:S(2)}, u32[]{:S(2)}) %collective-permute-start.8) | collective-permute-done | bytes 69664 | tf_op jit(solution)/shard_map/ppermute | solution.py:436
  43.6 1.9 %collective-permute-done.10.p3 = bf16[136,256]{1,0:T(8,128)(2,1)S(1)} collective-permute-done((bf16[136,256]{1,0:T(8,128)(2,1)S(1)}, bf16[136,256]{1,0:T(8,128)(2,1)S(1)}, u32[]{:S(2)}, u32[]{:S(2)}) %collective-permute-start.10) | collective-permute-done | bytes 69664 | tf_op jit(solution)/shard_map/ppermute | solution.py:436
  45.5 0.5 %collective-permute-done.9.p2 = bf16[136,256]{1,0:T(8,128)(2,1)S(1)} collective-permute-done((bf16[136,256]{1,0:T(8,128)(2,1)S(1)}, bf16[136,256]{1,0:T(8,128)(2,1)S(1)}, u32[]{:S(2)}, u32[]{:S(2)}) %collective-permute-start.9) | collective-permute-done | bytes 69664 | tf_op jit(solution)/shard_map/ppermute | solution.py:436
  46.2 1.1 %early.1 = (f32[1024,256]{1,0:T(8,128)}, f32[8,128]{1,0:T(8,128)S(1)}) custom-call(bf16[136,256]{1,0:T(8,128)(2,1)S(1)} %project.1.p0, bf16[136,256]{1,0:T(8,128)(2,1)S(1)} %collective-permute-done.8.p1, bf16[136,256]{1,0:T(8,128)(2,1)S(1)} %collective-permute-done.9.p2, bf16[136,256]{1,0:T(8,128)(2,1)S(1)} %collective-permute-done.10.p3, ...), custom_call_target="tpu_custom_call" | custom-call | flops 1000000 | tf_op jit(solution)/shard_map/early/pallas_call | solution.py:28
  47.8 1.7 %late.1 = (f32[1024,256]{1,0:T(8,128)}, f32[8,128]{1,0:T(8,128)}) custom-call(bf16[4,136,256]{2,1,0:T(8,128)(2,1)S(1)} %collective-permute-done.11.q_ref, f32[1024,256]{1,0:T(8,128)S(1)} %copy-done, f32[8,128]{1,0:T(8,128)S(1)} %bitcast.20, f32[1024,256]{1,0:T(8,128)} %get-tuple-element.42.book_in, ...), custom_call_target="tpu_custom_call", output_to_operand_aliasing={{0}: (3, {})} | custom-call | flops 1000000 | tf_op jit(solution)/shard_map/late/pallas_call | solution.py:28
  (26 shorter events, 1.2 us)
Async XLA Ops:
  0.6 7.9 %copy-start.3 = (f32[256]{0:T(256)S(1)}, f32[256]{0:T(256)}, u32[]{:S(2)}) copy-start(f32[256]{0:T(256)} %param.9) | copy-start | bytes 3076
  3.2 5.4 %collective-permute-start = (bf16[144,256]{1,0:T(8,128)(2,1)S(1)}, bf16[144,256]{1,0:T(8,128)(2,1)S(1)}, u32[]{:S(2)}, u32[]{:S(2)}) collective-permute-start(bf16[144,256]{1,0:T(8,128)(2,1)S(1)} %get-tuple-element.26), channel_id=1, source_target_pairs={{0,1},{1,0},{2,3},{3,2},{4,5},{5,4},{6,7},{7,6},{8,9},{9,8},{10,11... | collective-permute-start | bytes 221192 | tf_op jit(solution)/shard_map/ppermute | solution.py:436
  8.6 6.8 %copy-start.5 = (s32[2,2,16,32]{3,2,1,0:T(8,128)S(1)}, s32[2,2,16,32]{3,2,1,0:T(8,128)}, u32[]{:S(2)}) copy-start(s32[2,2,16,32]{3,2,1,0:T(8,128)} %param.13) | copy-start | bytes 24580
  8.6 8.6 %copy-start.4 = (f32[256]{0:T(256)S(1)}, f32[256]{0:T(256)}, u32[]{:S(2)}) copy-start(f32[256]{0:T(256)} %param.11) | copy-start | bytes 3076
  13.4 3.8 %collective-permute-start.1 = (f32[16,256]{1,0:T(8,128)S(1)}, f32[16,256]{1,0:T(8,128)S(1)}, u32[]{:S(2)}, u32[]{:S(2)}) collective-permute-start(f32[16,256]{1,0:T(8,128)S(1)} %get-tuple-element.30.near_ref), channel_id=1, source_target_pairs={{0,1},{1,0},{2,3},{3,2},{4,5},{5,4},{6,7},{7,6},{8,9},{9,8},{10,11... | collective-permute-start | bytes 49160 | tf_op jit(solution)/shard_map/ppermute | solution.py:436
  17.1 7.0 %copy-start = (f32[1024,256]{1,0:T(8,128)S(1)}, f32[1024,256]{1,0:T(8,128)}, u32[]{:S(2)}) copy-start(f32[1024,256]{1,0:T(8,128)} %sum_ref.5) | copy-start | bytes 3145732
  17.1 7.0 %copy-start.1 = (bf16[256,256]{1,0:T(8,128)(2,1)S(1)}, bf16[256,256]{1,0:T(8,128)(2,1)}, u32[]{:S(2)}) copy-start(bf16[256,256]{1,0:T(8,128)(2,1)} %w_ref.3) | copy-start | bytes 393220
  17.1 7.1 %copy-start.2 = (f32[1024]{0:T(1024)S(1)}, f32[1024]{0:T(1024)}, u32[]{:S(2)}) copy-start(f32[1024]{0:T(1024)} %param.15) | copy-start | bytes 12292
  18.8 1.6 %collective-permute-start.2 = (bf16[4,136,256]{2,1,0:T(8,128)(2,1)S(1)}, bf16[4,136,256]{2,1,0:T(8,128)(2,1)S(1)}, u32[]{:S(2)}, u32[]{:S(2)}) collective-permute-start(bf16[4,136,256]{2,1,0:T(8,128)(2,1)S(1)} %get-tuple-element.34), channel_id=1, source_target_pairs={{0,2},{1,3},{2,0},{3,1},{4,6},{5,7},{6,4},{7,5},{8,10},{9,11},{10,... | collective-permute-start | bytes 835592 | tf_op jit(solution)/shard_map/ppermute | solution.py:436
  20.5 7.8 %collective-permute-start.3 = (bf16[136,256]{1,0:T(8,128)(2,1)S(1)}, bf16[136,256]{1,0:T(8,128)(2,1)S(1)}, u32[]{:S(2)}, u32[]{:S(2)}) collective-permute-start(bf16[136,256]{1,0:T(8,128)(2,1)S(1)} %get-tuple-element.38), channel_id=1, source_target_pairs={{0,1},{1,0},{2,3},{3,2},{4,5},{5,4},{6,7},{7,6},{8,9},{9,8},{10,11... | collective-permute-start | bytes 208904 | tf_op jit(solution)/shard_map/ppermute | solution.py:436
  22.6 5.8 %collective-permute-start.4 = (bf16[136,256]{1,0:T(8,128)(2,1)S(1)}, bf16[136,256]{1,0:T(8,128)(2,1)S(1)}, u32[]{:S(2)}, u32[]{:S(2)}) collective-permute-start(bf16[136,256]{1,0:T(8,128)(2,1)S(1)} %get-tuple-element.39), channel_id=1, source_target_pairs={{0,4},{1,5},{2,6},{3,7},{4,0},{5,1},{6,2},{7,3},{8,12},{9,13},{10,... | collective-permute-start | bytes 208904 | tf_op jit(solution)/shard_map/ppermute | solution.py:436
  24.1 5.2 %collective-permute-start.5 = (bf16[136,256]{1,0:T(8,128)(2,1)S(1)}, bf16[136,256]{1,0:T(8,128)(2,1)S(1)}, u32[]{:S(2)}, u32[]{:S(2)}) collective-permute-start(bf16[136,256]{1,0:T(8,128)(2,1)S(1)} %get-tuple-element.40), channel_id=1, source_target_pairs={{0,5},{1,4},{2,7},{3,6},{4,1},{5,0},{6,3},{7,2},{8,13},{9,12},{10,... | collective-permute-start | bytes 208904 | tf_op jit(solution)/shard_map/ppermute | solution.py:436
  29.4 4.4 %collective-permute-start.6 = (bf16[136,256]{1,0:T(8,128)(2,1)S(1)}, bf16[136,256]{1,0:T(8,128)(2,1)S(1)}, u32[]{:S(2)}, u32[]{:S(2)}) collective-permute-start(bf16[136,256]{1,0:T(8,128)(2,1)S(1)} %gathered.1.own_ref), channel_id=1, source_target_pairs={{0,8},{1,9},{2,10},{3,11},{4,12},{5,13},{6,14},{7,15},{8,0},{9,1},... | collective-permute-start | bytes 208904 | tf_op jit(solution)/shard_map/ppermute | solution.py:436
  33.8 5.3 %collective-permute-start.7 = (bf16[136,256]{1,0:T(8,128)(2,1)S(1)}, bf16[136,256]{1,0:T(8,128)(2,1)S(1)}, u32[]{:S(2)}, u32[]{:S(2)}) collective-permute-start(bf16[136,256]{1,0:T(8,128)(2,1)S(1)} %pair.1.own_ref), channel_id=1, source_target_pairs={{0,16},{1,17},{2,18},{3,19},{4,20},{5,21},{6,22},{7,23},{8,24},{9,... | collective-permute-start | bytes 208904 | tf_op jit(solution)/shard_map/ppermute | solution.py:436
  39.2 4.4 %collective-permute-start.8 = (bf16[136,256]{1,0:T(8,128)(2,1)S(1)}, bf16[136,256]{1,0:T(8,128)(2,1)S(1)}, u32[]{:S(2)}, u32[]{:S(2)}) collective-permute-start(bf16[136,256]{1,0:T(8,128)(2,1)S(1)} %project.1.p0), channel_id=1, source_target_pairs={{0,1},{1,0},{2,3},{3,2},{4,5},{5,4},{6,7},{7,6},{8,9},{9,8},{10,11... | collective-permute-start | bytes 208904 | tf_op jit(solution)/shard_map/ppermute | solution.py:436
  40.3 5.2 %collective-permute-start.10 = (bf16[136,256]{1,0:T(8,128)(2,1)S(1)}, bf16[136,256]{1,0:T(8,128)(2,1)S(1)}, u32[]{:S(2)}, u32[]{:S(2)}) collective-permute-start(bf16[136,256]{1,0:T(8,128)(2,1)S(1)} %project.1.p0), channel_id=1, source_target_pairs={{0,5},{1,4},{2,7},{3,6},{4,1},{5,0},{6,3},{7,2},{8,13},{9,12},{10,... | collective-permute-start | bytes 208904 | tf_op jit(solution)/shard_map/ppermute | solution.py:436
  41.8 4.3 %collective-permute-start.9 = (bf16[136,256]{1,0:T(8,128)(2,1)S(1)}, bf16[136,256]{1,0:T(8,128)(2,1)S(1)}, u32[]{:S(2)}, u32[]{:S(2)}) collective-permute-start(bf16[136,256]{1,0:T(8,128)(2,1)S(1)} %project.1.p0), channel_id=1, source_target_pairs={{0,4},{1,5},{2,6},{3,7},{4,0},{5,1},{6,2},{7,3},{8,12},{9,13},{10,... | collective-permute-start | bytes 208904 | tf_op jit(solution)/shard_map/ppermute | solution.py:436
  46.1 1.7 %collective-permute-start.11 = (bf16[4,136,256]{2,1,0:T(8,128)(2,1)S(1)}, bf16[4,136,256]{2,1,0:T(8,128)(2,1)S(1)}, u32[]{:S(2)}, u32[]{:S(2)}) collective-permute-start(bf16[4,136,256]{2,1,0:T(8,128)(2,1)S(1)} %pad_maximum_fusion), channel_id=1, source_target_pairs={{0,2},{1,3},{2,0},{3,1},{4,6},{5,7},{6,4},{7,5},{8,10},{9,11},{10,... | collective-permute-start | bytes 835592 | tf_op jit(solution)/shard_map/ppermute | solution.py:436

commit v3 on v2

--- a/solution.py
+++ b/solution.py
@@ -68,28 +68,35 @@
     return out
 
 
-def local_stats(read, clips, blocks, rows, channels):
+def local_stats(read, clips, blocks, rows, channels, ready=lambda c: None):
     matrix = group_matrix(channels)
     members = blocks * rows * (channels // GROUPS)
+
+    def over(c, term):
+        parts = [None] * 2
+        for i in range(blocks):
+            value = term(read(c, i))
+            parts[i % 2] = value if parts[i % 2] is None else parts[i % 2] + value
+        total = parts[0] if parts[1] is None else parts[0] + parts[1]
+        return jnp.sum(total, axis=0, keepdims=True)
+
     sums = []
     for c in range(clips):
-        total = lax.fori_loop(
-            0, blocks, lambda i, acc: acc + read(c, i), jnp.zeros((rows, channels), f32), unroll=8
-        )
-        sums.append(jnp.sum(total, axis=0, keepdims=True))
+        ready(c)
+        sums.append(over(c, lambda x: x))
     means = group_total(stacked(sums, channels), matrix) / members
-    squares = []
-    for c in range(clips):
+
+    def squared(c):
         mean = means[c : c + 1]
 
-        def step(i, acc):
-            away = read(c, i) - mean
-            return acc + away * away
-
-        total = lax.fori_loop(0, blocks, step, jnp.zeros((rows, channels), f32), unroll=8)
-        squares.append(jnp.sum(total, axis=0, keepdims=True))
-    squares = group_total(stacked(squares, channels), matrix)
-    return means, squares, members
+        def term(x):
+            away = x - mean
+            return away * away
+
+        return over(c, term)
+
+    squares = group_total(stacked([squared(c) for c in range(clips)], channels), matrix)
+    return means, squares
 
 
 def merged(mean_a, square_a, mean_b, square_b, members):
@@ -115,18 +122,19 @@
     for load in loads:
         load.start()
     taps.start()
-    for load in loads:
-        load.wait()
+
+    def read(c, i):
+        return video_ref[c, i // rows, i % rows].astype(f32)
+
+    means, squares = local_stats(
+        read, clips, frames * rows, cols, channels, ready=lambda c: loads[c].wait()
+    )
     edge = (1 - strip) * (rows - 1)
     for c in range(clips):
         for t in range(frames):
             at = (c * frames + t) * cols
             pay_ref[at : at + cols] = video_ref[c, t, edge]
 
-    def read(c, i):
-        return video_ref[c, i // rows, i % rows].astype(f32)
-
-    means, squares, _ = local_stats(read, clips, frames * rows, cols, channels)
     loc_ref[0:8] = means
     loc_ref[8:16] = squares
     base = clips * frames * cols
@@ -196,11 +204,12 @@
             hid_ref[c, t * rows * cols : (t + 1) * rows * cols] = total
 
     def read(c, i):
-        return hid_ref[c, pl.ds(pl.multiple_of(i * cols, cols), cols)]
-
-    means, squares, _ = local_stats(read, clips, frames * rows, cols, channels)
-    st_ref[0:8] = means
-    st_ref[8:16] = squares
+        return hid_ref[c, i * cols : (i + 1) * cols]
+
+    means, squares = local_stats(read, clips, frames * rows, cols, channels)
+    st_ref[...] = stacked(
+        [m[c : c + 1] for m in (means, squares) for c in range(clips)], channels
+    )
 
 
 def shard_bits():
@@ -227,51 +236,17 @@
     )
 
 
-def segment_kernel(
-    hid_ref, near_ref, far_ref, gain_ref, codes_ref, act_ref, send_ref, keep_ref, cnt_ref, acc_ref
-):
-    clips, tokens, channels = hid_ref.shape
-    members = tokens * (channels // GROUPS)
-    gain = gain_ref[...]
-    block = 64
-    for c in range(clips):
-        mean, inverse = merged(
-            near_ref[c : c + 1],
-            near_ref[8 + c : 9 + c],
-            far_ref[c : c + 1],
-            far_ref[8 + c : 9 + c],
-            members,
-        )
-        scale = inverse * gain
-
-        def step(i, carry):
-            x = hid_ref[c, pl.ds(pl.multiple_of(i * block, block), block)]
-            act = silu((x - mean) * scale).astype(bf16)
-            act_ref[pl.ds(pl.multiple_of(c * tokens + i * block, block), block)] = act
-            return carry
-
-        lax.fori_loop(0, tokens // block, step, 0, unroll=True)
-
-    me = shard_bits()
-    codes_count = acc_ref.shape[0]
-    share = codes_count // SHARDS
-    codes = codes_ref[...] ^ (me * share)
-    row_code = lax.broadcasted_iota(jnp.int32, (codes_count, LANES), 0)
-    low_code = lax.broadcasted_iota(jnp.int32, (share, LANES), 0)
-    high_code = lax.broadcasted_iota(jnp.int32, (SHARDS, LANES), 0)
-    count = jnp.zeros((SHARDS, LANES), f32)
+def hot_rows(codes_ref, act_ref, acc_ref, first):
+    share = LANES
+    rows = acc_ref.shape[0]
+    codes = codes_ref[...] ^ (shard_bits() * share)
+    row_code = lax.broadcasted_iota(jnp.int32, (rows, LANES), 0) + first * share
     width = 2
-    shift = share.bit_length() - 1
     for k in range(codes.shape[0] // width):
         hot = []
         for j in range(width):
             line = codes[k * width + j : k * width + j + 1]
             hot.append(jnp.where(row_code == line, 1.0, 0.0).astype(bf16))
-            low = jnp.where(low_code == (line & (share - 1)), 1.0, 0.0).astype(bf16)
-            high = jnp.where(high_code == (line >> shift), 1.0, 0.0).astype(bf16)
-            count = count + lax.dot_general(
-                high, low, (((1,), (1,)), ((), ())), preferred_element_type=f32
-            )
         part = jnp.dot(
             jnp.concatenate(hot, axis=1),
             act_ref[k * width * LANES : (k + 1) * width * LANES],
@@ -281,18 +256,58 @@
             acc_ref[...] = part
         else:
             acc_ref[...] += part
+
+
+def segment_kernel(
+    hid_ref, near_ref, far_ref, gain_ref, codes_ref, act_ref, send_ref, cnt_ref, acc_ref
+):
+    clips, tokens, channels = hid_ref.shape
+    members = tokens * (channels // GROUPS)
+    gain = gain_ref[...]
+    block = 64
+    for c in range(clips):
+        mean, inverse = merged(
+            near_ref[c : c + 1],
+            near_ref[clips + c : clips + c + 1],
+            far_ref[c : c + 1],
+            far_ref[clips + c : clips + c + 1],
+            members,
+        )
+        scale = inverse * gain
+        for i in range(tokens // block):
+            x = hid_ref[c, i * block : (i + 1) * block]
+            act = silu((x - mean) * scale).astype(bf16)
+            act_ref[c * tokens + i * block : c * tokens + (i + 1) * block] = act
+
+    share = LANES
+    half = SHARDS // 2
+    codes = codes_ref[...] ^ (shard_bits() * share)
+    low_code = lax.broadcasted_iota(jnp.int32, (share, LANES), 0)
+    high_code = lax.broadcasted_iota(jnp.int32, (SHARDS, LANES), 0)
+    count = jnp.zeros((SHARDS, LANES), f32)
+    shift = share.bit_length() - 1
+    for k in range(codes.shape[0]):
+        line = codes[k : k + 1]
+        low = jnp.where(low_code == (line & (share - 1)), 1.0, 0.0).astype(bf16)
+        high = jnp.where(high_code == (line >> shift), 1.0, 0.0).astype(bf16)
+        count = count + lax.dot_general(
+            high, low, (((1,), (1,)), ((), ())), preferred_element_type=f32
+        )
     cnt_ref[...] = count
-    half = SHARDS // 2
-    keep_ref[...] = acc_ref[: half * share].reshape(half, share, channels)
+    hot_rows(codes_ref, act_ref, acc_ref, half)
     for p in range(half):
-        send_ref[p, :share] = acc_ref[(half + p) * share : (half + p + 1) * share].astype(bf16)
+        send_ref[p, :share] = acc_ref[p * share : (p + 1) * share].astype(bf16)
         send_ref[p, share:] = tail_rows(count[half + p : half + p + 1])
 
 
+def keep_kernel(act_ref, codes_ref, keep_ref):
+    hot_rows(codes_ref, act_ref, keep_ref, 0)
+
+
 def quarter_kernel(keep_ref, cnt_ref, got_ref, mine_ref, mcnt_ref, s1_ref, s2_ref, s3_ref):
-    share = keep_ref.shape[1]
+    share = LANES
     for p, out in enumerate((None, s1_ref, s2_ref, s3_ref)):
-        value = keep_ref[p] + got_ref[p, :share].astype(f32)
+        value = keep_ref[p * share : (p + 1) * share] + got_ref[p, :share].astype(f32)
         count = cnt_ref[p : p + 1] + untail(got_ref[p, share:])
         if out is None:
             mine_ref[...] = value
@@ -378,7 +393,7 @@
     err_ref[...] = jnp.broadcast_to(errors, (8, LANES))
 
 
-def book_kernel(first, tokens, *refs):
+def book_kernel(first, tokens, *refs, done=lambda: None):
     parts, (sum_ref, cnt_ref), rest = refs[:-8], refs[-8:-6], refs[-6:]
     _, _, book_hbm, count_ref, page_ref, sems = rest
     me = shard_bits()
@@ -399,6 +414,7 @@
         page_ref[i] = fresh * inverse
         copies.append(pltpu.make_async_copy(page_ref.at[i], book_hbm.at[at], sems.at[i]))
         copies[-1].start()
+    done()
     for copy in copies:
         copy.wait()
 
@@ -407,14 +423,21 @@
     book_kernel(0, tokens, p0, p1, p2, p3, sum_ref, cnt_ref, None, None, book_hbm, count_ref, page_ref, sems)
 
 
-def late_kernel(tokens, q_ref, sum_ref, cnt_ref, book_in, early_ref, book_hbm, count_ref, page_ref, late_ref, sems):
+def late_kernel(tokens, q_ref, sum_ref, cnt_ref, book_in, early_ref, book_hbm, count_hbm, page_ref, late_ref, line_ref, sems):
+    half = SHARDS // 2
+    copy = pltpu.make_async_copy(line_ref, count_hbm, sems.at[half])
+
+    def counts():
+        me = shard_bits()
+        for i in range(half):
+            line_ref[pl.ds(i ^ me, 1)] = early_ref[i : i + 1]
+            line_ref[pl.ds((half + i) ^ me, 1)] = late_ref[i : i + 1]
+        copy.start()
+
     book_kernel(
-        SHARDS // 2, tokens, q_ref, sum_ref, cnt_ref, None, None, book_hbm, late_ref, page_ref, sems
-    )
-    me = shard_bits()
-    for i in range(SHARDS // 2):
-        count_ref[pl.ds(i ^ me, 1)] = early_ref[i : i + 1]
-        count_ref[pl.ds((SHARDS // 2 + i) ^ me, 1)] = late_ref[i : i + 1]
+        half, tokens, q_ref, sum_ref, cnt_ref, None, None, book_hbm, late_ref, page_ref, sems, done=counts
+    )
+    copy.wait()
 
 
 def error_kernel(scale, p1, err_ref, error_ref):
@@ -456,7 +479,7 @@
     code_lines = codes.reshape(-1, LANES)
     hidden, near_two = call(
         conv_kernel,
-        [((clips, tokens, channels), f32), ((16, channels), f32)],
+        [((clips, tokens, channels), f32), ((8, channels), f32)],
         [held, far_pay, near, gain_first.reshape(1, channels), taps],
         scratch=[VMEM((clips, frames, rows + 2, cols, 3 * channels), bf16)],
         flops=4_000_000_000,
@@ -464,22 +487,29 @@
         name="conv",
     )
     far_two = swap(near_two, 1)
-    act, send, keep, cnt = call(
+    act, send, cnt = call(
         segment_kernel,
         [
             ((clips * tokens, channels), bf16),
             ((SHARDS // 2, share + TAIL, channels), bf16),
-            ((SHARDS // 2, share, channels), f32),
             ((SHARDS, LANES), f32),
         ],
         [hidden, near_two, far_two, gain_second.reshape(1, channels), code_lines],
-        scratch=[VMEM((codes_count, channels), f32)],
+        scratch=[VMEM((codes_count // 2, channels), f32)],
         flops=1_500_000_000,
         limit=24 << 20,
         name="segment",
     )
     core, x_bit = 2, 4
     got = swap(send, core)
+    (keep,) = call(
+        keep_kernel,
+        [((codes_count // 2, channels), f32)],
+        [act, code_lines],
+        flops=1_000_000_000,
+        limit=8 << 20,
+        name="keep",
+    )
     counts = ema_count.reshape(SHARDS, LANES)
     flat = ((share + TAIL, channels), bf16)
     mine, mine_cnt, s1, s2, s3 = call(
@@ -543,12 +573,17 @@
         functools.partial(late_kernel, total_tokens),
         [book_shape, ((SHARDS, LANES), f32)],
         [across, ema_sum, counts, book, early],
-        scratch=[page, VMEM((8, LANES), f32), pltpu.SemaphoreType.DMA((half,))],
+        scratch=[
+            page,
+            VMEM((8, LANES), f32),
+            VMEM((SHARDS, LANES), f32),
+            pltpu.SemaphoreType.DMA((half + 1,)),
+        ],
         flops=1_000_000,
         limit=8 << 20,
         name="late",
         far=(3,),
-        far_outs=(0,),
+        far_outs=(0, 1),
         alias={3: 0},
     )
     return (

time: 49.6 us -> 47.9 us (0.966)
  Pallas kernels: 16.3 us -> 15.3 us
  waiting for transfers between devices: 15.1 us -> 14.3 us
    pallas_call x11 -> x12, Pallas kernels: 16.3 us -> 15.3 us  [call(): pl.pallas_call(kernel, out_shape=tuple((jax.ShapeDtypeStruct(s, d) for s,...]
    ppermute x12, waiting for transfers between devices: 15.1 us -> 14.3 us  [swap(): return lax.ppermute(x, BOTH, [(i, i ^ mask) for i in range(n)])]
  transfers between devices with their start and end apart: 12 -> 12, of which waited for: 9 -> 9; matrix products, arithmetic and copies ran while one was open for 1% -> 1% of each run, Pallas kernels for 11% -> 13%
where the time goes in v3:
time: 47.9 us; the launch traced here: 47.7 us
  starting transfers between devices  16.7 us (35%)
  Pallas kernels  15.3 us (32%)
  waiting for transfers between devices  14.3 us (30%)
  between operations  0.74 us (2%)
  local copies, waits for them, and re-layouts  0.62 us (1%)
    ppermute x12, starting transfers between devices, swap(): return lax.ppermute(x, BOTH, [(i, i ^ mask) for i in range(n)])  16.7 us
    pallas_call x12, Pallas kernels, call(): pl.pallas_call(kernel, out_shape=tuple((jax.ShapeDtypeStruct(s, d) for s,...  15.3 us
    ppermute x12, waiting for transfers between devices, swap(): return lax.ppermute(x, BOTH, [(i, i ^ mask) for i in range(n)])  14.3 us
  transfers between devices with their start and end apart: 12, of which 9 were waited for; matrix products, arithmetic and copies ran while one was open for 1% of the time, Pallas kernels for 13%

profile of v3, /device:TPU:0, one launch (start us, length us, event | category | flops | bytes accessed | tf_op | source)
XLA Modules:
  0.0 47.7 jit_solution(4888707172986034380)
XLA Ops:
  0.6 2.0 %stats.1 = (bf16[144,256]{1,0:T(8,128)(2,1)S(1)}, f32[16,256]{1,0:T(8,128)S(1)}, bf16[2,2,16,32,256]{4,3,2,1,0:T(8,128)(2,1)S(1)}, bf16[2,2304,256]{2,1,0:T(8,128)(2,1)S(1)}) custom-call(bf16[2,2,16,32,256]{4,3,2,1,0:T(8,128)(2,1)} %video_hbm.1, bf16[3,2304,256]{2,1,0:T(8,128)(2,1)} %bitcast.23), custom_call_target="tpu_custom_call" | custom-call | flops 10000000 | tf_op jit(solution)/shard_map/stats/pallas_call | solution.py:28
  2.7 3.1 %collective-permute-start = (bf16[144,256]{1,0:T(8,128)(2,1)S(1)}, bf16[144,256]{1,0:T(8,128)(2,1)S(1)}, u32[]{:S(2)}, u32[]{:S(2)}) collective-permute-start(bf16[144,256]{1,0:T(8,128)(2,1)S(1)} %get-tuple-element.25), channel_id=1, source_target_pairs={{0,1},{1,0},{2,3},{3,2},{4,5},{5,4},{6,7},{7,6},{8,9},{9,8},{10,11... | collective-permute-start | bytes 221192 | tf_op jit(solution)/shard_map/ppermute | solution.py:459
  5.7 2.3 %collective-permute-done.pay_ref = bf16[144,256]{1,0:T(8,128)(2,1)S(1)} collective-permute-done((bf16[144,256]{1,0:T(8,128)(2,1)S(1)}, bf16[144,256]{1,0:T(8,128)(2,1)S(1)}, u32[]{:S(2)}, u32[]{:S(2)}) %collective-permute-start) | collective-permute-done | bytes 73760 | tf_op jit(solution)/shard_map/ppermute | solution.py:459
  8.1 4.8 %conv.1 = (f32[2,1024,256]{2,1,0:T(8,128)S(1)}, f32[8,256]{1,0:T(8,128)S(1)}) custom-call(bf16[2,2,16,32,256]{4,3,2,1,0:T(8,128)(2,1)S(1)} %get-tuple-element.24.video_ref, bf16[144,256]{1,0:T(8,128)(2,1)S(1)} %collective-permute-done.pay_ref, f32[16,256]{1,0:T(8,128)S(1)} %get-tuple-element.26.loc_ref, f32[1,256]{1,0:T(1,128)S(1)} %bitcast.21, ...), custom_call_target="tpu_custom_call" | custom-call | flops 4000000000 | tf_op jit(solution)/shard_map/conv/pallas_call | solution.py:28
  12.9 2.0 %collective-permute-start.1 = (f32[8,256]{1,0:T(8,128)S(1)}, f32[8,256]{1,0:T(8,128)S(1)}, u32[]{:S(2)}, u32[]{:S(2)}) collective-permute-start(f32[8,256]{1,0:T(8,128)S(1)} %get-tuple-element.29.near_ref), channel_id=1, source_target_pairs={{0,1},{1,0},{2,3},{3,2},{4,5},{5,4},{6,7},{7,6},{8,9},{9,8},{10,11... | collective-permute-start | bytes 24584 | tf_op jit(solution)/shard_map/ppermute | solution.py:459
  15.0 1.6 %collective-permute-done.1.far_ref = f32[8,256]{1,0:T(8,128)S(1)} collective-permute-done((f32[8,256]{1,0:T(8,128)S(1)}, f32[8,256]{1,0:T(8,128)S(1)}, u32[]{:S(2)}, u32[]{:S(2)}) %collective-permute-start.1) | collective-permute-done | bytes 8224 | tf_op jit(solution)/shard_map/ppermute | solution.py:459
  16.5 1.1 %segment.1 = (bf16[2048,256]{1,0:T(8,128)(2,1)S(1)}, bf16[4,136,256]{2,1,0:T(8,128)(2,1)S(1)}, f32[8,128]{1,0:T(8,128)S(1)}) custom-call(f32[2,1024,256]{2,1,0:T(8,128)S(1)} %get-tuple-element.28.hid_ref, f32[8,256]{1,0:T(8,128)S(1)} %get-tuple-element.29.near_ref, f32[8,256]{1,0:T(8,128)S(1)} %collective-permute-done.1.far_ref, f32[1,256]{1,0:T(1,128)S(1)} %bitcast.22, ...), custom_call_target="tpu_custom_call" | custom-call | flops 1500000000 | tf_op jit(solution)/shard_map/segment/pallas_call | solution.py:28
  17.8 0.7 %keep.1.keep_ref = f32[512,256]{1,0:T(8,128)S(1)} custom-call(bf16[2048,256]{1,0:T(8,128)(2,1)S(1)} %get-tuple-element.30.act_ref, s32[16,128]{1,0:T(8,128)S(1)} %reshape.32.codes_ref), custom_call_target="tpu_custom_call" | custom-call | flops 1000000000 | tf_op jit(solution)/shard_map/keep/pallas_call | solution.py:28
  18.5 0.8 %collective-permute-done.2.got_ref = bf16[4,136,256]{2,1,0:T(8,128)(2,1)S(1)} collective-permute-done((bf16[4,136,256]{2,1,0:T(8,128)(2,1)S(1)}, bf16[4,136,256]{2,1,0:T(8,128)(2,1)S(1)}, u32[]{:S(2)}, u32[]{:S(2)}) %collective-permute-start.2) | collective-permute-done | bytes 278560 | tf_op jit(solution)/shard_map/ppermute | solution.py:459
  19.4 2.1 %collective-permute-start.3 = (bf16[136,256]{1,0:T(8,128)(2,1)S(1)}, bf16[136,256]{1,0:T(8,128)(2,1)S(1)}, u32[]{:S(2)}, u32[]{:S(2)}) collective-permute-start(bf16[136,256]{1,0:T(8,128)(2,1)S(1)} %get-tuple-element.36), channel_id=1, source_target_pairs={{0,1},{1,0},{2,3},{3,2},{4,5},{5,4},{6,7},{7,6},{8,9},{9,8},{10,11... | collective-permute-start | bytes 208904 | tf_op jit(solution)/shard_map/ppermute | solution.py:459
  21.5 1.5 %collective-permute-start.4 = (bf16[136,256]{1,0:T(8,128)(2,1)S(1)}, bf16[136,256]{1,0:T(8,128)(2,1)S(1)}, u32[]{:S(2)}, u32[]{:S(2)}) collective-permute-start(bf16[136,256]{1,0:T(8,128)(2,1)S(1)} %get-tuple-element.37), channel_id=1, source_target_pairs={{0,4},{1,5},{2,6},{3,7},{4,0},{5,1},{6,2},{7,3},{8,12},{9,13},{10,... | collective-permute-start | bytes 208904 | tf_op jit(solution)/shard_map/ppermute | solution.py:459
  23.0 4.2 %latent.1 = (f32[2048,256]{1,0:T(8,128)}, f32[8,128]{1,0:T(8,128)S(1)}) custom-call(bf16[2048,256]{1,0:T(8,128)(2,1)S(1)} %get-tuple-element.30.act_ref, bf16[256,256]{1,0:T(8,128)(2,1)S(1)} %copy-done.1, s32[16,128]{1,0:T(8,128)S(1)} %reshape.32.codes_ref, f32[1024,256]{1,0:T(8,128)S(1)} %copy-done, f32[8,128]{1,0:T(8,128)S(1)} %bitcast.18, ...), custom_call_target="tpu_custom_call" | custom-call | flops 2500000000 | tf_op jit(solution)/shard_map/latent/pallas_call | solution.py:28
  27.2 0.9 %collective-permute-done.5.c_ref = bf16[136,256]{1,0:T(8,128)(2,1)S(1)} collective-permute-done((bf16[136,256]{1,0:T(8,128)(2,1)S(1)}, bf16[136,256]{1,0:T(8,128)(2,1)S(1)}, u32[]{:S(2)}, u32[]{:S(2)}) %collective-permute-start.5) | collective-permute-done | bytes 69664 | tf_op jit(solution)/shard_map/ppermute | solution.py:459
  28.2 1.6 %collective-permute-start.6 = (bf16[136,256]{1,0:T(8,128)(2,1)S(1)}, bf16[136,256]{1,0:T(8,128)(2,1)S(1)}, u32[]{:S(2)}, u32[]{:S(2)}) collective-permute-start(bf16[136,256]{1,0:T(8,128)(2,1)S(1)} %gathered.1.own_ref), channel_id=1, source_target_pairs={{0,8},{1,9},{2,10},{3,11},{4,12},{5,13},{6,14},{7,15},{8,0},{9,1},... | collective-permute-start | bytes 208904 | tf_op jit(solution)/shard_map/ppermute | solution.py:459
  29.9 2.7 %collective-permute-done.6.got_ref = bf16[136,256]{1,0:T(8,128)(2,1)S(1)} collective-permute-done((bf16[136,256]{1,0:T(8,128)(2,1)S(1)}, bf16[136,256]{1,0:T(8,128)(2,1)S(1)}, u32[]{:S(2)}, u32[]{:S(2)}) %collective-permute-start.6) | collective-permute-done | bytes 69664 | tf_op jit(solution)/shard_map/ppermute | solution.py:459
  32.6 2.7 %collective-permute-start.7 = (bf16[136,256]{1,0:T(8,128)(2,1)S(1)}, bf16[136,256]{1,0:T(8,128)(2,1)S(1)}, u32[]{:S(2)}, u32[]{:S(2)}) collective-permute-start(bf16[136,256]{1,0:T(8,128)(2,1)S(1)} %pair.1.own_ref), channel_id=1, source_target_pairs={{0,16},{1,17},{2,18},{3,19},{4,20},{5,21},{6,22},{7,23},{8,24},{9,... | collective-permute-start | bytes 208904 | tf_op jit(solution)/shard_map/ppermute | solution.py:459
  35.3 2.6 %collective-permute-done.7.got_ref = bf16[136,256]{1,0:T(8,128)(2,1)S(1)} collective-permute-done((bf16[136,256]{1,0:T(8,128)(2,1)S(1)}, bf16[136,256]{1,0:T(8,128)(2,1)S(1)}, u32[]{:S(2)}, u32[]{:S(2)}) %collective-permute-start.7) | collective-permute-done | bytes 69664 | tf_op jit(solution)/shard_map/ppermute | solution.py:459
  38.1 1.1 %collective-permute-start.8 = (bf16[136,256]{1,0:T(8,128)(2,1)S(1)}, bf16[136,256]{1,0:T(8,128)(2,1)S(1)}, u32[]{:S(2)}, u32[]{:S(2)}) collective-permute-start(bf16[136,256]{1,0:T(8,128)(2,1)S(1)} %project.1.p0), channel_id=1, source_target_pairs={{0,1},{1,0},{2,3},{3,2},{4,5},{5,4},{6,7},{7,6},{8,9},{9,8},{10,11... | collective-permute-start | bytes 208904 | tf_op jit(solution)/shard_map/ppermute | solution.py:459
  39.2 1.4 %collective-permute-start.10 = (bf16[136,256]{1,0:T(8,128)(2,1)S(1)}, bf16[136,256]{1,0:T(8,128)(2,1)S(1)}, u32[]{:S(2)}, u32[]{:S(2)}) collective-permute-start(bf16[136,256]{1,0:T(8,128)(2,1)S(1)} %project.1.p0), channel_id=1, source_target_pairs={{0,5},{1,4},{2,7},{3,6},{4,1},{5,0},{6,3},{7,2},{8,13},{9,12},{10,... | collective-permute-start | bytes 208904 | tf_op jit(solution)/shard_map/ppermute | solution.py:459
  40.6 1.0 %collective-permute-start.9 = (bf16[136,256]{1,0:T(8,128)(2,1)S(1)}, bf16[136,256]{1,0:T(8,128)(2,1)S(1)}, u32[]{:S(2)}, u32[]{:S(2)}) collective-permute-start(bf16[136,256]{1,0:T(8,128)(2,1)S(1)} %project.1.p0), channel_id=1, source_target_pairs={{0,4},{1,5},{2,6},{3,7},{4,0},{5,1},{6,2},{7,3},{8,12},{9,13},{10,... | collective-permute-start | bytes 208904 | tf_op jit(solution)/shard_map/ppermute | solution.py:459
  41.6 0.8 %collective-permute-done.8.p1 = bf16[136,256]{1,0:T(8,128)(2,1)S(1)} collective-permute-done((bf16[136,256]{1,0:T(8,128)(2,1)S(1)}, bf16[136,256]{1,0:T(8,128)(2,1)S(1)}, u32[]{:S(2)}, u32[]{:S(2)}) %collective-permute-start.8) | collective-permute-done | bytes 69664 | tf_op jit(solution)/shard_map/ppermute | solution.py:459
  42.5 1.9 %collective-permute-done.10.p3 = bf16[136,256]{1,0:T(8,128)(2,1)S(1)} collective-permute-done((bf16[136,256]{1,0:T(8,128)(2,1)S(1)}, bf16[136,256]{1,0:T(8,128)(2,1)S(1)}, u32[]{:S(2)}, u32[]{:S(2)}) %collective-permute-start.10) | collective-permute-done | bytes 69664 | tf_op jit(solution)/shard_map/ppermute | solution.py:459
  45.1 1.1 %early.1 = (f32[1024,256]{1,0:T(8,128)}, f32[8,128]{1,0:T(8,128)S(1)}) custom-call(bf16[136,256]{1,0:T(8,128)(2,1)S(1)} %project.1.p0, bf16[136,256]{1,0:T(8,128)(2,1)S(1)} %collective-permute-done.8.p1, bf16[136,256]{1,0:T(8,128)(2,1)S(1)} %collective-permute-done.9.p2, bf16[136,256]{1,0:T(8,128)(2,1)S(1)} %collective-permute-done.10.p3, ...), custom_call_target="tpu_custom_call" | custom-call | flops 1000000 | tf_op jit(solution)/shard_map/early/pallas_call | solution.py:28
  46.6 1.1 %late.1 = (f32[1024,256]{1,0:T(8,128)}, f32[8,128]{1,0:T(8,128)}) custom-call(bf16[4,136,256]{2,1,0:T(8,128)(2,1)S(1)} %collective-permute-done.11.q_ref, f32[1024,256]{1,0:T(8,128)S(1)} %copy-done, f32[8,128]{1,0:T(8,128)S(1)} %bitcast.20, f32[1024,256]{1,0:T(8,128)} %get-tuple-element.40.book_in, ...), custom_call_target="tpu_custom_call", output_to_operand_aliasing={{0}: (3, {})} | custom-call | flops 1000000 | tf_op jit(solution)/shard_map/late/pallas_call | solution.py:28
  (27 shorter events, 1.7 us)
Async XLA Ops:
  0.6 7.4 %copy-start.3 = (f32[256]{0:T(256)S(1)}, f32[256]{0:T(256)}, u32[]{:S(2)}) copy-start(f32[256]{0:T(256)} %param.9) | copy-start | bytes 3076
  2.7 5.4 %collective-permute-start = (bf16[144,256]{1,0:T(8,128)(2,1)S(1)}, bf16[144,256]{1,0:T(8,128)(2,1)S(1)}, u32[]{:S(2)}, u32[]{:S(2)}) collective-permute-start(bf16[144,256]{1,0:T(8,128)(2,1)S(1)} %get-tuple-element.25), channel_id=1, source_target_pairs={{0,1},{1,0},{2,3},{3,2},{4,5},{5,4},{6,7},{7,6},{8,9},{9,8},{10,11... | collective-permute-start | bytes 221192 | tf_op jit(solution)/shard_map/ppermute | solution.py:459
  8.1 6.8 %copy-start.5 = (s32[2,2,16,32]{3,2,1,0:T(8,128)S(1)}, s32[2,2,16,32]{3,2,1,0:T(8,128)}, u32[]{:S(2)}) copy-start(s32[2,2,16,32]{3,2,1,0:T(8,128)} %param.13) | copy-start | bytes 24580
  8.1 8.5 %copy-start.4 = (f32[256]{0:T(256)S(1)}, f32[256]{0:T(256)}, u32[]{:S(2)}) copy-start(f32[256]{0:T(256)} %param.11) | copy-start | bytes 3076
  12.9 3.7 %collective-permute-start.1 = (f32[8,256]{1,0:T(8,128)S(1)}, f32[8,256]{1,0:T(8,128)S(1)}, u32[]{:S(2)}, u32[]{:S(2)}) collective-permute-start(f32[8,256]{1,0:T(8,128)S(1)} %get-tuple-element.29.near_ref), channel_id=1, source_target_pairs={{0,1},{1,0},{2,3},{3,2},{4,5},{5,4},{6,7},{7,6},{8,9},{9,8},{10,11... | collective-permute-start | bytes 24584 | tf_op jit(solution)/shard_map/ppermute | solution.py:459
  17.7 5.4 %copy-start = (f32[1024,256]{1,0:T(8,128)S(1)}, f32[1024,256]{1,0:T(8,128)}, u32[]{:S(2)}) copy-start(f32[1024,256]{1,0:T(8,128)} %sum_ref.5) | copy-start | bytes 3145732
  17.7 5.3 %copy-start.1 = (bf16[256,256]{1,0:T(8,128)(2,1)S(1)}, bf16[256,256]{1,0:T(8,128)(2,1)}, u32[]{:S(2)}) copy-start(bf16[256,256]{1,0:T(8,128)(2,1)} %w_ref.3) | copy-start | bytes 393220
  17.7 5.3 %copy-start.2 = (f32[1024]{0:T(1024)S(1)}, f32[1024]{0:T(1024)}, u32[]{:S(2)}) copy-start(f32[1024]{0:T(1024)} %param.15) | copy-start | bytes 12292
  17.7 1.6 %collective-permute-start.2 = (bf16[4,136,256]{2,1,0:T(8,128)(2,1)S(1)}, bf16[4,136,256]{2,1,0:T(8,128)(2,1)S(1)}, u32[]{:S(2)}, u32[]{:S(2)}) collective-permute-start(bf16[4,136,256]{2,1,0:T(8,128)(2,1)S(1)} %get-tuple-element.32), channel_id=1, source_target_pairs={{0,2},{1,3},{2,0},{3,1},{4,6},{5,7},{6,4},{7,5},{8,10},{9,11},{10,... | collective-permute-start | bytes 835592 | tf_op jit(solution)/shard_map/ppermute | solution.py:459
  19.4 7.8 %collective-permute-start.3 = (bf16[136,256]{1,0:T(8,128)(2,1)S(1)}, bf16[136,256]{1,0:T(8,128)(2,1)S(1)}, u32[]{:S(2)}, u32[]{:S(2)}) collective-permute-start(bf16[136,256]{1,0:T(8,128)(2,1)S(1)} %get-tuple-element.36), channel_id=1, source_target_pairs={{0,1},{1,0},{2,3},{3,2},{4,5},{5,4},{6,7},{7,6},{8,9},{9,8},{10,11... | collective-permute-start | bytes 208904 | tf_op jit(solution)/shard_map/ppermute | solution.py:459
  21.5 5.8 %collective-permute-start.4 = (bf16[136,256]{1,0:T(8,128)(2,1)S(1)}, bf16[136,256]{1,0:T(8,128)(2,1)S(1)}, u32[]{:S(2)}, u32[]{:S(2)}) collective-permute-start(bf16[136,256]{1,0:T(8,128)(2,1)S(1)} %get-tuple-element.37), channel_id=1, source_target_pairs={{0,4},{1,5},{2,6},{3,7},{4,0},{5,1},{6,2},{7,3},{8,12},{9,13},{10,... | collective-permute-start | bytes 208904 | tf_op jit(solution)/shard_map/ppermute | solution.py:459
  23.0 5.2 %collective-permute-start.5 = (bf16[136,256]{1,0:T(8,128)(2,1)S(1)}, bf16[136,256]{1,0:T(8,128)(2,1)S(1)}, u32[]{:S(2)}, u32[]{:S(2)}) collective-permute-start(bf16[136,256]{1,0:T(8,128)(2,1)S(1)} %get-tuple-element.38), channel_id=1, source_target_pairs={{0,5},{1,4},{2,7},{3,6},{4,1},{5,0},{6,3},{7,2},{8,13},{9,12},{10,... | collective-permute-start | bytes 208904 | tf_op jit(solution)/shard_map/ppermute | solution.py:459
  28.2 4.4 %collective-permute-start.6 = (bf16[136,256]{1,0:T(8,128)(2,1)S(1)}, bf16[136,256]{1,0:T(8,128)(2,1)S(1)}, u32[]{:S(2)}, u32[]{:S(2)}) collective-permute-start(bf16[136,256]{1,0:T(8,128)(2,1)S(1)} %gathered.1.own_ref), channel_id=1, source_target_pairs={{0,8},{1,9},{2,10},{3,11},{4,12},{5,13},{6,14},{7,15},{8,0},{9,1},... | collective-permute-start | bytes 208904 | tf_op jit(solution)/shard_map/ppermute | solution.py:459
  32.6 5.3 %collective-permute-start.7 = (bf16[136,256]{1,0:T(8,128)(2,1)S(1)}, bf16[136,256]{1,0:T(8,128)(2,1)S(1)}, u32[]{:S(2)}, u32[]{:S(2)}) collective-permute-start(bf16[136,256]{1,0:T(8,128)(2,1)S(1)} %pair.1.own_ref), channel_id=1, source_target_pairs={{0,16},{1,17},{2,18},{3,19},{4,20},{5,21},{6,22},{7,23},{8,24},{9,... | collective-permute-start | bytes 208904 | tf_op jit(solution)/shard_map/ppermute | solution.py:459
  38.1 4.4 %collective-permute-start.8 = (bf16[136,256]{1,0:T(8,128)(2,1)S(1)}, bf16[136,256]{1,0:T(8,128)(2,1)S(1)}, u32[]{:S(2)}, u32[]{:S(2)}) collective-permute-start(bf16[136,256]{1,0:T(8,128)(2,1)S(1)} %project.1.p0), channel_id=1, source_target_pairs={{0,1},{1,0},{2,3},{3,2},{4,5},{5,4},{6,7},{7,6},{8,9},{9,8},{10,11... | collective-permute-start | bytes 208904 | tf_op jit(solution)/shard_map/ppermute | solution.py:459
  39.2 5.2 %collective-permute-start.10 = (bf16[136,256]{1,0:T(8,128)(2,1)S(1)}, bf16[136,256]{1,0:T(8,128)(2,1)S(1)}, u32[]{:S(2)}, u32[]{:S(2)}) collective-permute-start(bf16[136,256]{1,0:T(8,128)(2,1)S(1)} %project.1.p0), channel_id=1, source_target_pairs={{0,5},{1,4},{2,7},{3,6},{4,1},{5,0},{6,3},{7,2},{8,13},{9,12},{10,... | collective-permute-start | bytes 208904 | tf_op jit(solution)/shard_map/ppermute | solution.py:459
  40.6 4.3 %collective-permute-start.9 = (bf16[136,256]{1,0:T(8,128)(2,1)S(1)}, bf16[136,256]{1,0:T(8,128)(2,1)S(1)}, u32[]{:S(2)}, u32[]{:S(2)}) collective-permute-start(bf16[136,256]{1,0:T(8,128)(2,1)S(1)} %project.1.p0), channel_id=1, source_target_pairs={{0,4},{1,5},{2,6},{3,7},{4,0},{5,1},{6,2},{7,3},{8,12},{9,13},{10,... | collective-permute-start | bytes 208904 | tf_op jit(solution)/shard_map/ppermute | solution.py:459
  45.0 1.7 %collective-permute-start.11 = (bf16[4,136,256]{2,1,0:T(8,128)(2,1)S(1)}, bf16[4,136,256]{2,1,0:T(8,128)(2,1)S(1)}, u32[]{:S(2)}, u32[]{:S(2)}) collective-permute-start(bf16[4,136,256]{2,1,0:T(8,128)(2,1)S(1)} %pad_maximum_fusion), channel_id=1, source_target_pairs={{0,2},{1,3},{2,0},{3,1},{4,6},{5,7},{6,4},{7,5},{8,10},{9,11},{10,... | collective-permute-start | bytes 835592 | tf_op jit(solution)/shard_map/ppermute | solution.py:459

commit v4 on v3

--- a/solution.py
+++ b/solution.py
@@ -71,32 +71,39 @@
 def local_stats(read, clips, blocks, rows, channels, ready=lambda c: None):
     matrix = group_matrix(channels)
     members = blocks * rows * (channels // GROUPS)
-
-    def over(c, term):
-        parts = [None] * 2
-        for i in range(blocks):
-            value = term(read(c, i))
-            parts[i % 2] = value if parts[i % 2] is None else parts[i % 2] + value
-        total = parts[0] if parts[1] is None else parts[0] + parts[1]
-        return jnp.sum(total, axis=0, keepdims=True)
-
-    sums = []
+    some = max(1, blocks // 8)
+
+    def over(c, count, *terms):
+        totals = []
+        for term in terms:
+            parts = [None] * 2
+            for i in range(count):
+                value = term(read(c, i))
+                parts[i % 2] = value if parts[i % 2] is None else parts[i % 2] + value
+            total = parts[0] if parts[1] is None else parts[0] + parts[1]
+            totals.append(jnp.sum(total, axis=0, keepdims=True))
+        return totals
+
+    count = blocks * rows
+    points, near, squares = [], [], []
+    passes = []
     for c in range(clips):
         ready(c)
-        sums.append(over(c, lambda x: x))
-    means = group_total(stacked(sums, channels), matrix) / members
-
-    def squared(c):
-        mean = means[c : c + 1]
-
-        def term(x):
-            away = x - mean
-            return away * away
-
-        return over(c, term)
-
-    squares = group_total(stacked([squared(c) for c in range(clips)], channels), matrix)
-    return means, squares
+        point = over(c, some, lambda x: x)[0] * (1.0 / (some * rows))
+        points.append(point)
+        passes.append(over(c, blocks, lambda x: x - point, lambda x: (x - point) * (x - point)))
+    pivot = group_total(stacked(points, channels), matrix) * (count / members)
+    for c in range(clips):
+        point = points[c]
+        total, square = passes[c]
+        apart = point - pivot[c : c + 1]
+        near.append(total + count * apart)
+        squares.append(square + 2.0 * apart * total + count * apart * apart)
+    sums = near
+    totals = group_total(stacked(sums + squares, channels), matrix)
+    offset = totals[0:clips] / members
+    square = jnp.maximum(totals[clips : 2 * clips] - totals[0:clips] * offset, 0.0)
+    return pivot[0:clips] + offset, square
 
 
 def merged(mean_a, square_a, mean_b, square_b, members):
@@ -111,17 +118,21 @@
     return half + half * jnp.tanh(half)
 
 
-def stats_kernel(video_hbm, w_hbm, pay_ref, loc_ref, video_ref, w_ref, sems):
+def taps_kernel(w_hbm, after_ref, w_ref, sem):
+    first_tap = w_hbm.shape[0] - w_ref.shape[0]
+    load = pltpu.make_async_copy(w_hbm.at[pl.ds(first_tap, w_ref.shape[0])], w_ref, sem.at[0])
+    load.start()
+    load.wait()
+
+
+def stats_kernel(video_hbm, pay_ref, loc_ref, video_ref, sems):
     clips, frames, rows, cols, channels = video_ref.shape
     strip = lax.axis_index("strip")
     loads = [
         pltpu.make_async_copy(video_hbm.at[c], video_ref.at[c], sems.at[c]) for c in range(clips)
     ]
-    first_tap = w_hbm.shape[0] - w_ref.shape[0]
-    taps = pltpu.make_async_copy(w_hbm.at[pl.ds(first_tap, w_ref.shape[0])], w_ref, sems.at[clips])
     for load in loads:
         load.start()
-    taps.start()
 
     def read(c, i):
         return video_ref[c, i // rows, i % rows].astype(f32)
@@ -135,8 +146,7 @@
             at = (c * frames + t) * cols
             pay_ref[at : at + cols] = video_ref[c, t, edge]
 
-    loc_ref[0:8] = means
-    loc_ref[8:16] = squares
+    loc_ref[...] = stacked([m[c : c + 1] for m in (means, squares) for c in range(clips)], channels)
     base = clips * frames * cols
     row = lax.broadcasted_iota(jnp.int32, (16, channels), 0)
     out = jnp.zeros((16, channels), f32)
@@ -146,7 +156,6 @@
             for c in range(clips):
                 out = jnp.where(row == (j * clips + c) * 3 + k, piece[c : c + 1], out)
     pay_ref[base : base + 16] = out.astype(bf16)
-    taps.wait()
 
 
 def conv_kernel(video_ref, pay_ref, loc_ref, gain_ref, w_ref, hid_ref, st_ref, buf_ref):
@@ -170,7 +179,7 @@
         at = [(j * clips + c) * 3 for j in (0, 1)]
         far_mean, far_square = [far[i : i + 1] + far[i + 1 : i + 2] + far[i + 2 : i + 3] for i in at]
         mean, inverse = merged(
-            loc_ref[c : c + 1], loc_ref[8 + c : 9 + c], far_mean, far_square, members
+            loc_ref[c : c + 1], loc_ref[clips + c : clips + c + 1], far_mean, far_square, members
         )
         scale = inverse * gain
         for t in range(frames):
@@ -258,8 +267,39 @@
             acc_ref[...] += part
 
 
+def hot_kernel(codes_ref, hot_ref):
+    share = LANES
+    rows = hot_ref.shape[0]
+    codes = codes_ref[...] ^ (shard_bits() * share)
+    row_code = lax.broadcasted_iota(jnp.int32, (rows, LANES), 0) + rows
+    for k in range(codes.shape[0]):
+        hot = jnp.where(row_code == codes[k : k + 1], 1.0, 0.0).astype(bf16)
+        hot_ref[:, k * LANES : (k + 1) * LANES] = hot
+
+
+def count_kernel(codes_ref, after_ref, cnt_ref, tails_ref, hot_ref):
+    hot_kernel(codes_ref, hot_ref)
+    share = LANES
+    half = SHARDS // 2
+    codes = codes_ref[...] ^ (shard_bits() * share)
+    low_code = lax.broadcasted_iota(jnp.int32, (share, LANES), 0)
+    high_code = lax.broadcasted_iota(jnp.int32, (SHARDS, LANES), 0)
+    count = jnp.zeros((SHARDS, LANES), f32)
+    shift = share.bit_length() - 1
+    for k in range(codes.shape[0]):
+        line = codes[k : k + 1]
+        low = jnp.where(low_code == (line & (share - 1)), 1.0, 0.0).astype(bf16)
+        high = jnp.where(high_code == (line >> shift), 1.0, 0.0).astype(bf16)
+        count = count + lax.dot_general(
+            high, low, (((1,), (1,)), ((), ())), preferred_element_type=f32
+        )
+    cnt_ref[...] = count
+    for p in range(half):
+        tails_ref[p] = tail_rows(count[half + p : half + p + 1])
+
+
 def segment_kernel(
-    hid_ref, near_ref, far_ref, gain_ref, codes_ref, act_ref, send_ref, cnt_ref, acc_ref
+    hid_ref, near_ref, far_ref, gain_ref, hot_ref, tails_ref, act_ref, send_ref, acc_ref
 ):
     clips, tokens, channels = hid_ref.shape
     members = tokens * (channels // GROUPS)
@@ -281,23 +321,17 @@
 
     share = LANES
     half = SHARDS // 2
-    codes = codes_ref[...] ^ (shard_bits() * share)
-    low_code = lax.broadcasted_iota(jnp.int32, (share, LANES), 0)
-    high_code = lax.broadcasted_iota(jnp.int32, (SHARDS, LANES), 0)
-    count = jnp.zeros((SHARDS, LANES), f32)
-    shift = share.bit_length() - 1
-    for k in range(codes.shape[0]):
-        line = codes[k : k + 1]
-        low = jnp.where(low_code == (line & (share - 1)), 1.0, 0.0).astype(bf16)
-        high = jnp.where(high_code == (line >> shift), 1.0, 0.0).astype(bf16)
-        count = count + lax.dot_general(
-            high, low, (((1,), (1,)), ((), ())), preferred_element_type=f32
-        )
-    cnt_ref[...] = count
-    hot_rows(codes_ref, act_ref, acc_ref, half)
+    width = act_ref.shape[0] // 2
+    for k in range(2):
+        at = slice(k * width, (k + 1) * width)
+        part = jnp.dot(hot_ref[:, at], act_ref[at], preferred_element_type=f32)
+        if k == 0:
+            acc_ref[...] = part
+        else:
+            acc_ref[...] += part
     for p in range(half):
         send_ref[p, :share] = acc_ref[p * share : (p + 1) * share].astype(bf16)
-        send_ref[p, share:] = tail_rows(count[half + p : half + p + 1])
+        send_ref[p, share:] = tails_ref[p]
 
 
 def keep_kernel(act_ref, codes_ref, keep_ref):
@@ -460,23 +494,34 @@
 
     tokens = frames * rows * cols
     halo = clips * frames * cols
-    pay, near, held, taps = call(
+    pay, near, held = call(
         stats_kernel,
         [
             ((halo + 16, channels), bf16),
-            ((16, channels), f32),
+            ((8, channels), f32),
             (video.shape, bf16),
-            ((min(3, frames), 9 * channels, channels), bf16),
         ],
-        [pltpu.with_memory_space_constraint(video, pltpu.HBM), pltpu.with_memory_space_constraint(conv_weight.reshape(3, 9 * channels, channels), pltpu.HBM)],
-        scratch=[pltpu.SemaphoreType.DMA((clips + 1,))],
+        [pltpu.with_memory_space_constraint(video, pltpu.HBM)],
+        scratch=[pltpu.SemaphoreType.DMA((clips,))],
         flops=10_000_000,
         limit=16 << 20,
         name="stats",
-        far=(0, 1),
+        far=(0,),
     )
     far_pay = swap(pay, 1)
-    code_lines = codes.reshape(-1, LANES)
+    weights = pltpu.with_memory_space_constraint(
+        conv_weight.reshape(3, 9 * channels, channels), pltpu.HBM
+    )
+    (taps,) = call(
+        taps_kernel,
+        [((min(3, frames), 9 * channels, channels), bf16)],
+        [weights, near],
+        scratch=[pltpu.SemaphoreType.DMA((1,))],
+        flops=1_000_000_000,
+        limit=8 << 20,
+        name="taps",
+        far=(0,),
+    )
     hidden, near_two = call(
         conv_kernel,
         [((clips, tokens, channels), f32), ((8, channels), f32)],
@@ -486,15 +531,27 @@
         limit=24 << 20,
         name="conv",
     )
+    code_lines = lax.optimization_barrier((codes, near_two))[0].reshape(-1, LANES)
     far_two = swap(near_two, 1)
-    act, send, cnt = call(
+    cnt, tails, hot = call(
+        count_kernel,
+        [
+            ((SHARDS, LANES), f32),
+            ((SHARDS // 2, TAIL, channels), bf16),
+            ((codes_count // 2, clips * tokens), bf16),
+        ],
+        [code_lines, near_two],
+        flops=500_000_000,
+        limit=8 << 20,
+        name="count",
+    )
+    act, send = call(
         segment_kernel,
         [
             ((clips * tokens, channels), bf16),
             ((SHARDS // 2, share + TAIL, channels), bf16),
-            ((SHARDS, LANES), f32),
         ],
-        [hidden, near_two, far_two, gain_second.reshape(1, channels), code_lines],
+        [hidden, near_two, far_two, gain_second.reshape(1, channels), hot, tails],
         scratch=[VMEM((codes_count // 2, channels), f32)],
         flops=1_500_000_000,
         limit=24 << 20,

time: 47.9 us -> 47 us (0.981)
  waiting for transfers between devices: 14.3 us -> 11.5 us
  Pallas kernels: 15.3 us -> 17.2 us
    ppermute x12, waiting for transfers between devices: 14.3 us -> 11.5 us  [swap(): return lax.ppermute(x, BOTH, [(i, i ^ mask) for i in range(n)])]
    pallas_call x12 -> x14, Pallas kernels: 15.3 us -> 17.2 us  [call(): pl.pallas_call(kernel, out_shape=tuple((jax.ShapeDtypeStruct(s, d) for s,...]
  transfers between devices with their start and end apart: 12 -> 12, of which waited for: 9 -> 9; matrix products, arithmetic and copies ran while one was open for 1% -> 1% of each run, Pallas kernels for 13% -> 19%
where the time goes in v4:
time: 47 us; the launch traced here: 46.9 us
  Pallas kernels  17.2 us (37%)
  starting transfers between devices  16.8 us (36%)
  waiting for transfers between devices  11.5 us (24%)
  between operations  0.76 us (2%)
  local copies, waits for them, and re-layouts  0.61 us (1%)
    pallas_call x14, Pallas kernels, call(): pl.pallas_call(kernel, out_shape=tuple((jax.ShapeDtypeStruct(s, d) for s,...  17.2 us
    ppermute x12, starting transfers between devices, swap(): return lax.ppermute(x, BOTH, [(i, i ^ mask) for i in range(n)])  16.8 us
    ppermute x12, waiting for transfers between devices, swap(): return lax.ppermute(x, BOTH, [(i, i ^ mask) for i in range(n)])  11.5 us
  transfers between devices with their start and end apart: 12, of which 9 were waited for; matrix products, arithmetic and copies ran while one was open for 1% of the time, Pallas kernels for 19%

profile of v4, /device:TPU:0, one launch (start us, length us, event | category | flops | bytes accessed | tf_op | source)
XLA Modules:
  0.0 46.9 jit_solution(9048197669411927226)
XLA Ops:
  0.6 1.7 %stats.1 = (bf16[144,256]{1,0:T(8,128)(2,1)S(1)}, f32[8,256]{1,0:T(8,128)S(1)}, bf16[2,2,16,32,256]{4,3,2,1,0:T(8,128)(2,1)S(1)}) custom-call(bf16[2,2,16,32,256]{4,3,2,1,0:T(8,128)(2,1)} %video_hbm.1), custom_call_target="tpu_custom_call" | custom-call | flops 10000000 | tf_op jit(solution)/shard_map/stats/pallas_call | solution.py:28
  2.3 3.1 %collective-permute-start = (bf16[144,256]{1,0:T(8,128)(2,1)S(1)}, bf16[144,256]{1,0:T(8,128)(2,1)S(1)}, u32[]{:S(2)}, u32[]{:S(2)}) collective-permute-start(bf16[144,256]{1,0:T(8,128)(2,1)S(1)} %get-tuple-element.27), channel_id=1, source_target_pairs={{0,1},{1,0},{2,3},{3,2},{4,5},{5,4},{6,7},{7,6},{8,9},{9,8},{10,11... | collective-permute-start | bytes 221192 | tf_op jit(solution)/shard_map/ppermute | solution.py:493
  5.4 1.7 %taps.1.w_ref = bf16[2,2304,256]{2,1,0:T(8,128)(2,1)S(1)} custom-call(bf16[3,2304,256]{2,1,0:T(8,128)(2,1)} %bitcast.23, f32[8,256]{1,0:T(8,128)S(1)} %get-tuple-element.28.after_ref.loc_ref), custom_call_target="tpu_custom_call" | custom-call | flops 1000000000 | tf_op jit(solution)/shard_map/taps/pallas_call | solution.py:28
  7.1 0.6 %collective-permute-done.pay_ref = bf16[144,256]{1,0:T(8,128)(2,1)S(1)} collective-permute-done((bf16[144,256]{1,0:T(8,128)(2,1)S(1)}, bf16[144,256]{1,0:T(8,128)(2,1)S(1)}, u32[]{:S(2)}, u32[]{:S(2)}) %collective-permute-start) | collective-permute-done | bytes 73760 | tf_op jit(solution)/shard_map/ppermute | solution.py:493
  7.7 4.5 %conv.1 = (f32[2,1024,256]{2,1,0:T(8,128)S(1)}, f32[8,256]{1,0:T(8,128)S(1)}) custom-call(bf16[2,2,16,32,256]{4,3,2,1,0:T(8,128)(2,1)S(1)} %get-tuple-element.26.video_ref, bf16[144,256]{1,0:T(8,128)(2,1)S(1)} %collective-permute-done.pay_ref, f32[8,256]{1,0:T(8,128)S(1)} %get-tuple-element.28.after_ref.loc_ref, f32[1,256]{1,0:T(1,128)S(1)} %bitcast.21, ...), custom_call_target="tpu_custom_call" | custom-call | flops 4000000000 | tf_op jit(solution)/shard_map/conv/pallas_call | solution.py:28
  12.2 2.1 %collective-permute-start.1 = (f32[8,256]{1,0:T(8,128)S(1)}, f32[8,256]{1,0:T(8,128)S(1)}, u32[]{:S(2)}, u32[]{:S(2)}) collective-permute-start(f32[8,256]{1,0:T(8,128)S(1)} %get-tuple-element.30.after_ref.near_ref), channel_id=1, source_target_pairs={{0,1},{1,0},{2,3},{3,2},{4,5},{5,4},{6,7},{7,6},{8,9},{9,8},{10,11... | collective-permute-start | bytes 24584 | tf_op jit(solution)/shard_map/ppermute | solution.py:493
  14.4 1.1 %count.1 = (f32[8,128]{1,0:T(8,128)S(1)}, bf16[4,8,256]{2,1,0:T(8,128)(2,1)S(1)}, bf16[512,2048]{1,0:T(8,128)(2,1)S(1)}) custom-call(s32[16,128]{1,0:T(8,128)S(1)} %reshape.32.codes_ref, f32[8,256]{1,0:T(8,128)S(1)} %get-tuple-element.30.after_ref.near_ref), custom_call_target="tpu_custom_call" | custom-call | flops 500000000 | tf_op jit(solution)/shard_map/count/pallas_call | solution.py:28
  16.0 0.9 %segment.1 = (bf16[2048,256]{1,0:T(8,128)(2,1)S(1)}, bf16[4,136,256]{2,1,0:T(8,128)(2,1)S(1)}) custom-call(f32[2,1024,256]{2,1,0:T(8,128)S(1)} %get-tuple-element.29.hid_ref, f32[8,256]{1,0:T(8,128)S(1)} %get-tuple-element.30.after_ref.near_ref, f32[8,256]{1,0:T(8,128)S(1)} %collective-permute-done.1.far_ref, f32[1,256]{1,0:T(1,128)S(1)} %bitcast.22, ...), custom_call_target="tpu_custom_call" | custom-call | flops 1500000000 | tf_op jit(solution)/shard_map/segment/pallas_call | solution.py:28
  16.9 0.7 %keep.1.keep_ref = f32[512,256]{1,0:T(8,128)S(1)} custom-call(bf16[2048,256]{1,0:T(8,128)(2,1)S(1)} %get-tuple-element.34.act_ref, s32[16,128]{1,0:T(8,128)S(1)} %reshape.32.codes_ref), custom_call_target="tpu_custom_call" | custom-call | flops 1000000000 | tf_op jit(solution)/shard_map/keep/pallas_call | solution.py:28
  17.6 0.8 %collective-permute-done.2.got_ref = bf16[4,136,256]{2,1,0:T(8,128)(2,1)S(1)} collective-permute-done((bf16[4,136,256]{2,1,0:T(8,128)(2,1)S(1)}, bf16[4,136,256]{2,1,0:T(8,128)(2,1)S(1)}, u32[]{:S(2)}, u32[]{:S(2)}) %collective-permute-start.2) | collective-permute-done | bytes 278560 | tf_op jit(solution)/shard_map/ppermute | solution.py:493
  18.5 2.1 %collective-permute-start.3 = (bf16[136,256]{1,0:T(8,128)(2,1)S(1)}, bf16[136,256]{1,0:T(8,128)(2,1)S(1)}, u32[]{:S(2)}, u32[]{:S(2)}) collective-permute-start(bf16[136,256]{1,0:T(8,128)(2,1)S(1)} %get-tuple-element.40), channel_id=1, source_target_pairs={{0,1},{1,0},{2,3},{3,2},{4,5},{5,4},{6,7},{7,6},{8,9},{9,8},{10,11... | collective-permute-start | bytes 208904 | tf_op jit(solution)/shard_map/ppermute | solution.py:493
  20.6 1.5 %collective-permute-start.4 = (bf16[136,256]{1,0:T(8,128)(2,1)S(1)}, bf16[136,256]{1,0:T(8,128)(2,1)S(1)}, u32[]{:S(2)}, u32[]{:S(2)}) collective-permute-start(bf16[136,256]{1,0:T(8,128)(2,1)S(1)} %get-tuple-element.41), channel_id=1, source_target_pairs={{0,4},{1,5},{2,6},{3,7},{4,0},{5,1},{6,2},{7,3},{8,12},{9,13},{10,... | collective-permute-start | bytes 208904 | tf_op jit(solution)/shard_map/ppermute | solution.py:493
  22.1 4.2 %latent.1 = (f32[2048,256]{1,0:T(8,128)}, f32[8,128]{1,0:T(8,128)S(1)}) custom-call(bf16[2048,256]{1,0:T(8,128)(2,1)S(1)} %get-tuple-element.34.act_ref, bf16[256,256]{1,0:T(8,128)(2,1)S(1)} %copy-done.1, s32[16,128]{1,0:T(8,128)S(1)} %reshape.32.codes_ref, f32[1024,256]{1,0:T(8,128)S(1)} %copy-done, f32[8,128]{1,0:T(8,128)S(1)} %bitcast.18, ...), custom_call_target="tpu_custom_call" | custom-call | flops 2500000000 | tf_op jit(solution)/shard_map/latent/pallas_call | solution.py:28
  26.4 0.9 %collective-permute-done.5.c_ref = bf16[136,256]{1,0:T(8,128)(2,1)S(1)} collective-permute-done((bf16[136,256]{1,0:T(8,128)(2,1)S(1)}, bf16[136,256]{1,0:T(8,128)(2,1)S(1)}, u32[]{:S(2)}, u32[]{:S(2)}) %collective-permute-start.5) | collective-permute-done | bytes 69664 | tf_op jit(solution)/shard_map/ppermute | solution.py:493
  27.3 1.6 %collective-permute-start.6 = (bf16[136,256]{1,0:T(8,128)(2,1)S(1)}, bf16[136,256]{1,0:T(8,128)(2,1)S(1)}, u32[]{:S(2)}, u32[]{:S(2)}) collective-permute-start(bf16[136,256]{1,0:T(8,128)(2,1)S(1)} %gathered.1.own_ref), channel_id=1, source_target_pairs={{0,8},{1,9},{2,10},{3,11},{4,12},{5,13},{6,14},{7,15},{8,0},{9,1},... | collective-permute-start | bytes 208904 | tf_op jit(solution)/shard_map/ppermute | solution.py:493
  29.0 2.7 %collective-permute-done.6.got_ref = bf16[136,256]{1,0:T(8,128)(2,1)S(1)} collective-permute-done((bf16[136,256]{1,0:T(8,128)(2,1)S(1)}, bf16[136,256]{1,0:T(8,128)(2,1)S(1)}, u32[]{:S(2)}, u32[]{:S(2)}) %collective-permute-start.6) | collective-permute-done | bytes 69664 | tf_op jit(solution)/shard_map/ppermute | solution.py:493
  31.7 2.6 %collective-permute-start.7 = (bf16[136,256]{1,0:T(8,128)(2,1)S(1)}, bf16[136,256]{1,0:T(8,128)(2,1)S(1)}, u32[]{:S(2)}, u32[]{:S(2)}) collective-permute-start(bf16[136,256]{1,0:T(8,128)(2,1)S(1)} %pair.1.own_ref), channel_id=1, source_target_pairs={{0,16},{1,17},{2,18},{3,19},{4,20},{5,21},{6,22},{7,23},{8,24},{9,... | collective-permute-start | bytes 208904 | tf_op jit(solution)/shard_map/ppermute | solution.py:493
  34.4 2.6 %collective-permute-done.7.got_ref = bf16[136,256]{1,0:T(8,128)(2,1)S(1)} collective-permute-done((bf16[136,256]{1,0:T(8,128)(2,1)S(1)}, bf16[136,256]{1,0:T(8,128)(2,1)S(1)}, u32[]{:S(2)}, u32[]{:S(2)}) %collective-permute-start.7) | collective-permute-done | bytes 69664 | tf_op jit(solution)/shard_map/ppermute | solution.py:493
  37.2 2.0 %collective-permute-start.10 = (bf16[136,256]{1,0:T(8,128)(2,1)S(1)}, bf16[136,256]{1,0:T(8,128)(2,1)S(1)}, u32[]{:S(2)}, u32[]{:S(2)}) collective-permute-start(bf16[136,256]{1,0:T(8,128)(2,1)S(1)} %project.1.p0), channel_id=1, source_target_pairs={{0,5},{1,4},{2,7},{3,6},{4,1},{5,0},{6,3},{7,2},{8,13},{9,12},{10,... | collective-permute-start | bytes 208904 | tf_op jit(solution)/shard_map/ppermute | solution.py:493
  39.8 1.0 %collective-permute-start.8 = (bf16[136,256]{1,0:T(8,128)(2,1)S(1)}, bf16[136,256]{1,0:T(8,128)(2,1)S(1)}, u32[]{:S(2)}, u32[]{:S(2)}) collective-permute-start(bf16[136,256]{1,0:T(8,128)(2,1)S(1)} %project.1.p0), channel_id=1, source_target_pairs={{0,1},{1,0},{2,3},{3,2},{4,5},{5,4},{6,7},{7,6},{8,9},{9,8},{10,11... | collective-permute-start | bytes 208904 | tf_op jit(solution)/shard_map/ppermute | solution.py:493
  40.8 1.7 %collective-permute-done.10.p3 = bf16[136,256]{1,0:T(8,128)(2,1)S(1)} collective-permute-done((bf16[136,256]{1,0:T(8,128)(2,1)S(1)}, bf16[136,256]{1,0:T(8,128)(2,1)S(1)}, u32[]{:S(2)}, u32[]{:S(2)}) %collective-permute-start.10) | collective-permute-done | bytes 69664 | tf_op jit(solution)/shard_map/ppermute | solution.py:493
  42.5 1.1 %collective-permute-done.9.p2 = bf16[136,256]{1,0:T(8,128)(2,1)S(1)} collective-permute-done((bf16[136,256]{1,0:T(8,128)(2,1)S(1)}, bf16[136,256]{1,0:T(8,128)(2,1)S(1)}, u32[]{:S(2)}, u32[]{:S(2)}) %collective-permute-start.9) | collective-permute-done | bytes 69664 | tf_op jit(solution)/shard_map/ppermute | solution.py:493
  44.2 1.1 %early.1 = (f32[1024,256]{1,0:T(8,128)}, f32[8,128]{1,0:T(8,128)S(1)}) custom-call(bf16[136,256]{1,0:T(8,128)(2,1)S(1)} %project.1.p0, bf16[136,256]{1,0:T(8,128)(2,1)S(1)} %collective-permute-done.8.p1, bf16[136,256]{1,0:T(8,128)(2,1)S(1)} %collective-permute-done.9.p2, bf16[136,256]{1,0:T(8,128)(2,1)S(1)} %collective-permute-done.10.p3, ...), custom_call_target="tpu_custom_call" | custom-call | flops 1000000 | tf_op jit(solution)/shard_map/early/pallas_call | solution.py:28
  45.8 1.1 %late.1 = (f32[1024,256]{1,0:T(8,128)}, f32[8,128]{1,0:T(8,128)}) custom-call(bf16[4,136,256]{2,1,0:T(8,128)(2,1)S(1)} %collective-permute-done.11.q_ref, f32[1024,256]{1,0:T(8,128)S(1)} %copy-done, f32[8,128]{1,0:T(8,128)S(1)} %bitcast.20, f32[1024,256]{1,0:T(8,128)} %get-tuple-element.44.book_in, ...), custom_call_target="tpu_custom_call", output_to_operand_aliasing={{0}: (3, {})} | custom-call | flops 1000000 | tf_op jit(solution)/shard_map/late/pallas_call | solution.py:28
  (29 shorter events, 2.7 us)
Async XLA Ops:
  2.3 5.4 %collective-permute-start = (bf16[144,256]{1,0:T(8,128)(2,1)S(1)}, bf16[144,256]{1,0:T(8,128)(2,1)S(1)}, u32[]{:S(2)}, u32[]{:S(2)}) collective-permute-start(bf16[144,256]{1,0:T(8,128)(2,1)S(1)} %get-tuple-element.27), channel_id=1, source_target_pairs={{0,1},{1,0},{2,3},{3,2},{4,5},{5,4},{6,7},{7,6},{8,9},{9,8},{10,11... | collective-permute-start | bytes 221192 | tf_op jit(solution)/shard_map/ppermute | solution.py:493
  5.4 2.3 %copy-start.3 = (f32[256]{0:T(256)S(1)}, f32[256]{0:T(256)}, u32[]{:S(2)}) copy-start(f32[256]{0:T(256)} %param.9) | copy-start | bytes 3076
  7.7 6.6 %copy-start.5 = (s32[2,2,16,32]{3,2,1,0:T(8,128)S(1)}, s32[2,2,16,32]{3,2,1,0:T(8,128)}, u32[]{:S(2)}) copy-start(s32[2,2,16,32]{3,2,1,0:T(8,128)} %param.13) | copy-start | bytes 24580
  7.7 8.2 %copy-start.4 = (f32[256]{0:T(256)S(1)}, f32[256]{0:T(256)}, u32[]{:S(2)}) copy-start(f32[256]{0:T(256)} %param.11) | copy-start | bytes 3076
  12.2 3.7 %collective-permute-start.1 = (f32[8,256]{1,0:T(8,128)S(1)}, f32[8,256]{1,0:T(8,128)S(1)}, u32[]{:S(2)}, u32[]{:S(2)}) collective-permute-start(f32[8,256]{1,0:T(8,128)S(1)} %get-tuple-element.30.after_ref.near_ref), channel_id=1, source_target_pairs={{0,1},{1,0},{2,3},{3,2},{4,5},{5,4},{6,7},{7,6},{8,9},{9,8},{10,11... | collective-permute-start | bytes 24584 | tf_op jit(solution)/shard_map/ppermute | solution.py:493
  16.8 1.6 %collective-permute-start.2 = (bf16[4,136,256]{2,1,0:T(8,128)(2,1)S(1)}, bf16[4,136,256]{2,1,0:T(8,128)(2,1)S(1)}, u32[]{:S(2)}, u32[]{:S(2)}) collective-permute-start(bf16[4,136,256]{2,1,0:T(8,128)(2,1)S(1)} %get-tuple-element.36), channel_id=1, source_target_pairs={{0,2},{1,3},{2,0},{3,1},{4,6},{5,7},{6,4},{7,5},{8,10},{9,11},{10,... | collective-permute-start | bytes 835592 | tf_op jit(solution)/shard_map/ppermute | solution.py:493
  16.9 5.2 %copy-start = (f32[1024,256]{1,0:T(8,128)S(1)}, f32[1024,256]{1,0:T(8,128)}, u32[]{:S(2)}) copy-start(f32[1024,256]{1,0:T(8,128)} %sum_ref.5) | copy-start | bytes 3145732
  16.9 5.2 %copy-start.1 = (bf16[256,256]{1,0:T(8,128)(2,1)S(1)}, bf16[256,256]{1,0:T(8,128)(2,1)}, u32[]{:S(2)}) copy-start(bf16[256,256]{1,0:T(8,128)(2,1)} %w_ref.3) | copy-start | bytes 393220
  16.9 5.2 %copy-start.2 = (f32[1024]{0:T(1024)S(1)}, f32[1024]{0:T(1024)}, u32[]{:S(2)}) copy-start(f32[1024]{0:T(1024)} %param.15) | copy-start | bytes 12292
  18.5 7.9 %collective-permute-start.3 = (bf16[136,256]{1,0:T(8,128)(2,1)S(1)}, bf16[136,256]{1,0:T(8,128)(2,1)S(1)}, u32[]{:S(2)}, u32[]{:S(2)}) collective-permute-start(bf16[136,256]{1,0:T(8,128)(2,1)S(1)} %get-tuple-element.40), channel_id=1, source_target_pairs={{0,1},{1,0},{2,3},{3,2},{4,5},{5,4},{6,7},{7,6},{8,9},{9,8},{10,11... | collective-permute-start | bytes 208904 | tf_op jit(solution)/shard_map/ppermute | solution.py:493
  20.6 5.8 %collective-permute-start.4 = (bf16[136,256]{1,0:T(8,128)(2,1)S(1)}, bf16[136,256]{1,0:T(8,128)(2,1)S(1)}, u32[]{:S(2)}, u32[]{:S(2)}) collective-permute-start(bf16[136,256]{1,0:T(8,128)(2,1)S(1)} %get-tuple-element.41), channel_id=1, source_target_pairs={{0,4},{1,5},{2,6},{3,7},{4,0},{5,1},{6,2},{7,3},{8,12},{9,13},{10,... | collective-permute-start | bytes 208904 | tf_op jit(solution)/shard_map/ppermute | solution.py:493
  22.1 5.2 %collective-permute-start.5 = (bf16[136,256]{1,0:T(8,128)(2,1)S(1)}, bf16[136,256]{1,0:T(8,128)(2,1)S(1)}, u32[]{:S(2)}, u32[]{:S(2)}) collective-permute-start(bf16[136,256]{1,0:T(8,128)(2,1)S(1)} %get-tuple-element.42), channel_id=1, source_target_pairs={{0,5},{1,4},{2,7},{3,6},{4,1},{5,0},{6,3},{7,2},{8,13},{9,12},{10,... | collective-permute-start | bytes 208904 | tf_op jit(solution)/shard_map/ppermute | solution.py:493
  27.3 4.4 %collective-permute-start.6 = (bf16[136,256]{1,0:T(8,128)(2,1)S(1)}, bf16[136,256]{1,0:T(8,128)(2,1)S(1)}, u32[]{:S(2)}, u32[]{:S(2)}) collective-permute-start(bf16[136,256]{1,0:T(8,128)(2,1)S(1)} %gathered.1.own_ref), channel_id=1, source_target_pairs={{0,8},{1,9},{2,10},{3,11},{4,12},{5,13},{6,14},{7,15},{8,0},{9,1},... | collective-permute-start | bytes 208904 | tf_op jit(solution)/shard_map/ppermute | solution.py:493
  31.7 5.3 %collective-permute-start.7 = (bf16[136,256]{1,0:T(8,128)(2,1)S(1)}, bf16[136,256]{1,0:T(8,128)(2,1)S(1)}, u32[]{:S(2)}, u32[]{:S(2)}) collective-permute-start(bf16[136,256]{1,0:T(8,128)(2,1)S(1)} %pair.1.own_ref), channel_id=1, source_target_pairs={{0,16},{1,17},{2,18},{3,19},{4,20},{5,21},{6,22},{7,23},{8,24},{9,... | collective-permute-start | bytes 208904 | tf_op jit(solution)/shard_map/ppermute | solution.py:493
  37.2 5.3 %collective-permute-start.10 = (bf16[136,256]{1,0:T(8,128)(2,1)S(1)}, bf16[136,256]{1,0:T(8,128)(2,1)S(1)}, u32[]{:S(2)}, u32[]{:S(2)}) collective-permute-start(bf16[136,256]{1,0:T(8,128)(2,1)S(1)} %project.1.p0), channel_id=1, source_target_pairs={{0,5},{1,4},{2,7},{3,6},{4,1},{5,0},{6,3},{7,2},{8,13},{9,12},{10,... | collective-permute-start | bytes 208904 | tf_op jit(solution)/shard_map/ppermute | solution.py:493
  39.2 4.3 %collective-permute-start.9 = (bf16[136,256]{1,0:T(8,128)(2,1)S(1)}, bf16[136,256]{1,0:T(8,128)(2,1)S(1)}, u32[]{:S(2)}, u32[]{:S(2)}) collective-permute-start(bf16[136,256]{1,0:T(8,128)(2,1)S(1)} %project.1.p0), channel_id=1, source_target_pairs={{0,4},{1,5},{2,6},{3,7},{4,0},{5,1},{6,2},{7,3},{8,12},{9,13},{10,... | collective-permute-start | bytes 208904 | tf_op jit(solution)/shard_map/ppermute | solution.py:493
  39.8 4.3 %collective-permute-start.8 = (bf16[136,256]{1,0:T(8,128)(2,1)S(1)}, bf16[136,256]{1,0:T(8,128)(2,1)S(1)}, u32[]{:S(2)}, u32[]{:S(2)}) collective-permute-start(bf16[136,256]{1,0:T(8,128)(2,1)S(1)} %project.1.p0), channel_id=1, source_target_pairs={{0,1},{1,0},{2,3},{3,2},{4,5},{5,4},{6,7},{7,6},{8,9},{9,8},{10,11... | collective-permute-start | bytes 208904 | tf_op jit(solution)/shard_map/ppermute | solution.py:493
  44.1 1.7 %collective-permute-start.11 = (bf16[4,136,256]{2,1,0:T(8,128)(2,1)S(1)}, bf16[4,136,256]{2,1,0:T(8,128)(2,1)S(1)}, u32[]{:S(2)}, u32[]{:S(2)}) collective-permute-start(bf16[4,136,256]{2,1,0:T(8,128)(2,1)S(1)} %pad_maximum_fusion), channel_id=1, source_target_pairs={{0,2},{1,3},{2,0},{3,1},{4,6},{5,7},{6,4},{7,5},{8,10},{9,11},{10,... | collective-permute-start | bytes 835592 | tf_op jit(solution)/shard_map/ppermute | solution.py:493

commit v5 on v4

--- a/solution.py
+++ b/solution.py
@@ -453,11 +453,20 @@
         copy.wait()
 
 
-def early_kernel(tokens, p0, p1, p2, p3, sum_ref, cnt_ref, book_hbm, count_ref, page_ref, sems):
+def early_kernel(
+    tokens, scale, p0, p1, p2, p3, sum_ref, cnt_ref, err_ref, book_hbm, count_ref, error_hbm, page_ref, error_ref, sems
+):
+    copy = pltpu.make_async_copy(error_ref, error_hbm, sems.at[SHARDS // 2])
+    errors = (err_ref[0:1] + untail(p1[LANES:], 1)) * scale
+    error_ref[...] = errors[0, : error_ref.shape[0]]
+    copy.start()
     book_kernel(0, tokens, p0, p1, p2, p3, sum_ref, cnt_ref, None, None, book_hbm, count_ref, page_ref, sems)
-
-
-def late_kernel(tokens, q_ref, sum_ref, cnt_ref, book_in, early_ref, book_hbm, count_hbm, page_ref, late_ref, line_ref, sems):
+    copy.wait()
+
+
+def late_kernel(
+    tokens, q0, q1, q2, q3, sum_ref, cnt_ref, book_in, early_ref, book_hbm, count_hbm, page_ref, late_ref, line_ref, sems
+):
     half = SHARDS // 2
     copy = pltpu.make_async_copy(line_ref, count_hbm, sems.at[half])
 
@@ -469,15 +478,9 @@
         copy.start()
 
     book_kernel(
-        half, tokens, q_ref, sum_ref, cnt_ref, None, None, book_hbm, late_ref, page_ref, sems, done=counts
+        half, tokens, q0, q1, q2, q3, sum_ref, cnt_ref, None, None, book_hbm, late_ref, page_ref, sems, done=counts
     )
     copy.wait()
-
-
-def error_kernel(scale, p1, err_ref, error_ref):
-    error_ref[...] = jnp.broadcast_to(
-        (err_ref[0:1] + untail(p1[LANES:], 1)) * scale, (8, LANES)
-    )
 
 
 def body(video, gain_first, conv_weight, gain_second, proj_weight, codes, ema_sum, ema_count):
@@ -602,34 +605,26 @@
         project_kernel, [flat], [own, last, proj_weight, err], flops=1_000_000, limit=8 << 20, name="project"
     )
     peers = [swap(done, m) for m in near_masks]
-    across = swap(jnp.stack([done, *peers]), core)
+    across = [swap(part, core) for part in (done, *peers)]
     scale = 1.0 / (tokens * strips * channels)
     total_tokens = float(clips * tokens * n)
     half = SHARDS // 2
-    (error,) = call(
-        functools.partial(error_kernel, scale),
-        [((8, LANES), f32)],
-        [peers[0], err],
-        flops=1_000_000,
-        limit=8 << 20,
-        name="error",
-    )
     page = VMEM((half, share, channels), f32)
     book_shape = ((codes_count, channels), f32)
-    book, early = call(
-        functools.partial(early_kernel, total_tokens),
-        [book_shape, ((8, LANES), f32)],
-        [done, *peers, ema_sum, counts],
-        scratch=[page, pltpu.SemaphoreType.DMA((half,))],
+    book, early, error = call(
+        functools.partial(early_kernel, total_tokens, scale),
+        [book_shape, ((8, LANES), f32), ((clips,), f32)],
+        [done, *peers, ema_sum, counts, err],
+        scratch=[page, VMEM((clips,), f32), pltpu.SemaphoreType.DMA((half + 1,))],
         flops=1_000_000,
         limit=8 << 20,
         name="early",
-        far_outs=(0,),
+        far_outs=(0, 2),
     )
     book, count = call(
         functools.partial(late_kernel, total_tokens),
         [book_shape, ((SHARDS, LANES), f32)],
-        [across, ema_sum, counts, book, early],
+        [*across, ema_sum, counts, book, early],
         scratch=[
             page,
             VMEM((8, LANES), f32),
@@ -639,15 +634,15 @@
         flops=1_000_000,
         limit=8 << 20,
         name="late",
-        far=(3,),
+        far=(half + 2,),
         far_outs=(0, 1),
-        alias={3: 0},
+        alias={half + 2: 0},
     )
     return (
         latent.reshape(clips, frames, rows, cols, channels),
         book,
         count.reshape(codes_count),
-        error[0, :clips],
+        error,
     )
 
 

time: 47 us -> 46.6 us (level)
  local copies, waits for them, and re-layouts: 0.61 us -> 0.1 us
    squeeze x1 -> x0, local copies, waits for them, and re-layouts: 0.51 us -> none  [body(): error[0, :clips]]
    ppermute x12 -> x15, waiting for transfers between devices: 11.5 us -> 11.6 us  [swap(): return lax.ppermute(x, BOTH, [(i, i ^ mask) for i in range(n)])]
    ppermute x12 -> x15, starting transfers between devices: 16.8 us -> 16.7 us  [swap(): return lax.ppermute(x, BOTH, [(i, i ^ mask) for i in range(n)])]
    pallas_call x14 -> x13, Pallas kernels: 17.2 us -> 17.2 us  [call(): pl.pallas_call(kernel, out_shape=tuple((jax.ShapeDtypeStruct(s, d) for s,...]
  transfers between devices with their start and end apart: 12 -> 15, of which waited for: 9 -> 10; matrix products, arithmetic and copies ran while one was open for 1% -> 0% of each run, Pallas kernels for 19% -> 19%
where the time goes in v5:
time: 46.6 us; the launch traced here: 46.4 us
  Pallas kernels  17.2 us (37%)
  starting transfers between devices  16.7 us (36%)
  waiting for transfers between devices  11.6 us (25%)
  between operations  0.77 us (2%)
    pallas_call x13, Pallas kernels, call(): pl.pallas_call(kernel, out_shape=tuple((jax.ShapeDtypeStruct(s, d) for s,...  17.2 us
    ppermute x15, starting transfers between devices, swap(): return lax.ppermute(x, BOTH, [(i, i ^ mask) for i in range(n)])  16.7 us
    ppermute x15, waiting for transfers between devices, swap(): return lax.ppermute(x, BOTH, [(i, i ^ mask) for i in range(n)])  11.6 us
  transfers between devices with their start and end apart: 15, of which 10 were waited for; matrix products, arithmetic and copies ran while one was open for 0% of the time, Pallas kernels for 19%

profile of v5, /device:TPU:0, one launch (start us, length us, event | category | flops | bytes accessed | tf_op | source)
XLA Modules:
  0.0 46.4 jit_solution(3288065818931775019)
XLA Ops:
  0.6 1.7 %stats.1 = (bf16[144,256]{1,0:T(8,128)(2,1)S(1)}, f32[8,256]{1,0:T(8,128)S(1)}, bf16[2,2,16,32,256]{4,3,2,1,0:T(8,128)(2,1)S(1)}) custom-call(bf16[2,2,16,32,256]{4,3,2,1,0:T(8,128)(2,1)} %video_hbm.1), custom_call_target="tpu_custom_call" | custom-call | flops 10000000 | tf_op jit(solution)/shard_map/stats/pallas_call | solution.py:28
  2.3 3.1 %collective-permute-start = (bf16[144,256]{1,0:T(8,128)(2,1)S(1)}, bf16[144,256]{1,0:T(8,128)(2,1)S(1)}, u32[]{:S(2)}, u32[]{:S(2)}) collective-permute-start(bf16[144,256]{1,0:T(8,128)(2,1)S(1)} %get-tuple-element.28), channel_id=1, source_target_pairs={{0,1},{1,0},{2,3},{3,2},{4,5},{5,4},{6,7},{7,6},{8,9},{9,8},{10,11... | collective-permute-start | bytes 221192 | tf_op jit(solution)/shard_map/ppermute | solution.py:496
  5.4 1.7 %taps.1.w_ref = bf16[2,2304,256]{2,1,0:T(8,128)(2,1)S(1)} custom-call(bf16[3,2304,256]{2,1,0:T(8,128)(2,1)} %bitcast.13, f32[8,256]{1,0:T(8,128)S(1)} %get-tuple-element.29.after_ref.loc_ref), custom_call_target="tpu_custom_call" | custom-call | flops 1000000000 | tf_op jit(solution)/shard_map/taps/pallas_call | solution.py:28
  7.1 0.6 %collective-permute-done.pay_ref = bf16[144,256]{1,0:T(8,128)(2,1)S(1)} collective-permute-done((bf16[144,256]{1,0:T(8,128)(2,1)S(1)}, bf16[144,256]{1,0:T(8,128)(2,1)S(1)}, u32[]{:S(2)}, u32[]{:S(2)}) %collective-permute-start) | collective-permute-done | bytes 73760 | tf_op jit(solution)/shard_map/ppermute | solution.py:496
  7.7 4.5 %conv.1 = (f32[2,1024,256]{2,1,0:T(8,128)S(1)}, f32[8,256]{1,0:T(8,128)S(1)}) custom-call(bf16[2,2,16,32,256]{4,3,2,1,0:T(8,128)(2,1)S(1)} %get-tuple-element.27.video_ref, bf16[144,256]{1,0:T(8,128)(2,1)S(1)} %collective-permute-done.pay_ref, f32[8,256]{1,0:T(8,128)S(1)} %get-tuple-element.29.after_ref.loc_ref, f32[1,256]{1,0:T(1,128)S(1)} %bitcast.11, ...), custom_call_target="tpu_custom_call" | custom-call | flops 4000000000 | tf_op jit(solution)/shard_map/conv/pallas_call | solution.py:28
  12.2 2.1 %collective-permute-start.1 = (f32[8,256]{1,0:T(8,128)S(1)}, f32[8,256]{1,0:T(8,128)S(1)}, u32[]{:S(2)}, u32[]{:S(2)}) collective-permute-start(f32[8,256]{1,0:T(8,128)S(1)} %get-tuple-element.31.after_ref.near_ref), channel_id=1, source_target_pairs={{0,1},{1,0},{2,3},{3,2},{4,5},{5,4},{6,7},{7,6},{8,9},{9,8},{10,11... | collective-permute-start | bytes 24584 | tf_op jit(solution)/shard_map/ppermute | solution.py:496
  14.4 1.1 %count.1 = (f32[8,128]{1,0:T(8,128)S(1)}, bf16[4,8,256]{2,1,0:T(8,128)(2,1)S(1)}, bf16[512,2048]{1,0:T(8,128)(2,1)S(1)}) custom-call(s32[16,128]{1,0:T(8,128)S(1)} %reshape.32.codes_ref, f32[8,256]{1,0:T(8,128)S(1)} %get-tuple-element.31.after_ref.near_ref), custom_call_target="tpu_custom_call" | custom-call | flops 500000000 | tf_op jit(solution)/shard_map/count/pallas_call | solution.py:28
  16.0 0.9 %segment.1 = (bf16[2048,256]{1,0:T(8,128)(2,1)S(1)}, bf16[4,136,256]{2,1,0:T(8,128)(2,1)S(1)}) custom-call(f32[2,1024,256]{2,1,0:T(8,128)S(1)} %get-tuple-element.30.hid_ref, f32[8,256]{1,0:T(8,128)S(1)} %get-tuple-element.31.after_ref.near_ref, f32[8,256]{1,0:T(8,128)S(1)} %collective-permute-done.1.far_ref, f32[1,256]{1,0:T(1,128)S(1)} %bitcast.12, ...), custom_call_target="tpu_custom_call" | custom-call | flops 1500000000 | tf_op jit(solution)/shard_map/segment/pallas_call | solution.py:28
  16.9 0.7 %keep.1.keep_ref = f32[512,256]{1,0:T(8,128)S(1)} custom-call(bf16[2048,256]{1,0:T(8,128)(2,1)S(1)} %get-tuple-element.35.act_ref, s32[16,128]{1,0:T(8,128)S(1)} %reshape.32.codes_ref), custom_call_target="tpu_custom_call" | custom-call | flops 1000000000 | tf_op jit(solution)/shard_map/keep/pallas_call | solution.py:28
  17.6 0.8 %collective-permute-done.2.got_ref = bf16[4,136,256]{2,1,0:T(8,128)(2,1)S(1)} collective-permute-done((bf16[4,136,256]{2,1,0:T(8,128)(2,1)S(1)}, bf16[4,136,256]{2,1,0:T(8,128)(2,1)S(1)}, u32[]{:S(2)}, u32[]{:S(2)}) %collective-permute-start.2) | collective-permute-done | bytes 278560 | tf_op jit(solution)/shard_map/ppermute | solution.py:496
  18.5 2.1 %collective-permute-start.3 = (bf16[136,256]{1,0:T(8,128)(2,1)S(1)}, bf16[136,256]{1,0:T(8,128)(2,1)S(1)}, u32[]{:S(2)}, u32[]{:S(2)}) collective-permute-start(bf16[136,256]{1,0:T(8,128)(2,1)S(1)} %get-tuple-element.41), channel_id=1, source_target_pairs={{0,1},{1,0},{2,3},{3,2},{4,5},{5,4},{6,7},{7,6},{8,9},{9,8},{10,11... | collective-permute-start | bytes 208904 | tf_op jit(solution)/shard_map/ppermute | solution.py:496
  20.6 1.5 %collective-permute-start.4 = (bf16[136,256]{1,0:T(8,128)(2,1)S(1)}, bf16[136,256]{1,0:T(8,128)(2,1)S(1)}, u32[]{:S(2)}, u32[]{:S(2)}) collective-permute-start(bf16[136,256]{1,0:T(8,128)(2,1)S(1)} %get-tuple-element.42), channel_id=1, source_target_pairs={{0,4},{1,5},{2,6},{3,7},{4,0},{5,1},{6,2},{7,3},{8,12},{9,13},{10,... | collective-permute-start | bytes 208904 | tf_op jit(solution)/shard_map/ppermute | solution.py:496
  22.1 4.2 %latent.1 = (f32[2048,256]{1,0:T(8,128)}, f32[8,128]{1,0:T(8,128)S(1)}) custom-call(bf16[2048,256]{1,0:T(8,128)(2,1)S(1)} %get-tuple-element.35.act_ref, bf16[256,256]{1,0:T(8,128)(2,1)S(1)} %copy-done.1, s32[16,128]{1,0:T(8,128)S(1)} %reshape.32.codes_ref, f32[1024,256]{1,0:T(8,128)S(1)} %copy-done, f32[8,128]{1,0:T(8,128)S(1)} %bitcast.8, ...), custom_call_target="tpu_custom_call" | custom-call | flops 2500000000 | tf_op jit(solution)/shard_map/latent/pallas_call | solution.py:28
  26.4 0.9 %collective-permute-done.5.c_ref = bf16[136,256]{1,0:T(8,128)(2,1)S(1)} collective-permute-done((bf16[136,256]{1,0:T(8,128)(2,1)S(1)}, bf16[136,256]{1,0:T(8,128)(2,1)S(1)}, u32[]{:S(2)}, u32[]{:S(2)}) %collective-permute-start.5) | collective-permute-done | bytes 69664 | tf_op jit(solution)/shard_map/ppermute | solution.py:496
  27.3 1.6 %collective-permute-start.6 = (bf16[136,256]{1,0:T(8,128)(2,1)S(1)}, bf16[136,256]{1,0:T(8,128)(2,1)S(1)}, u32[]{:S(2)}, u32[]{:S(2)}) collective-permute-start(bf16[136,256]{1,0:T(8,128)(2,1)S(1)} %gathered.1.own_ref), channel_id=1, source_target_pairs={{0,8},{1,9},{2,10},{3,11},{4,12},{5,13},{6,14},{7,15},{8,0},{9,1},... | collective-permute-start | bytes 208904 | tf_op jit(solution)/shard_map/ppermute | solution.py:496
  29.0 2.7 %collective-permute-done.6.got_ref = bf16[136,256]{1,0:T(8,128)(2,1)S(1)} collective-permute-done((bf16[136,256]{1,0:T(8,128)(2,1)S(1)}, bf16[136,256]{1,0:T(8,128)(2,1)S(1)}, u32[]{:S(2)}, u32[]{:S(2)}) %collective-permute-start.6) | collective-permute-done | bytes 69664 | tf_op jit(solution)/shard_map/ppermute | solution.py:496
  31.7 2.6 %collective-permute-start.7 = (bf16[136,256]{1,0:T(8,128)(2,1)S(1)}, bf16[136,256]{1,0:T(8,128)(2,1)S(1)}, u32[]{:S(2)}, u32[]{:S(2)}) collective-permute-start(bf16[136,256]{1,0:T(8,128)(2,1)S(1)} %pair.1.own_ref), channel_id=1, source_target_pairs={{0,16},{1,17},{2,18},{3,19},{4,20},{5,21},{6,22},{7,23},{8,24},{9,... | collective-permute-start | bytes 208904 | tf_op jit(solution)/shard_map/ppermute | solution.py:496
  34.4 2.6 %collective-permute-done.7.got_ref = bf16[136,256]{1,0:T(8,128)(2,1)S(1)} collective-permute-done((bf16[136,256]{1,0:T(8,128)(2,1)S(1)}, bf16[136,256]{1,0:T(8,128)(2,1)S(1)}, u32[]{:S(2)}, u32[]{:S(2)}) %collective-permute-start.7) | collective-permute-done | bytes 69664 | tf_op jit(solution)/shard_map/ppermute | solution.py:496
  37.2 2.0 %collective-permute-start.13 = (bf16[136,256]{1,0:T(8,128)(2,1)S(1)}, bf16[136,256]{1,0:T(8,128)(2,1)S(1)}, u32[]{:S(2)}, u32[]{:S(2)}) collective-permute-start(bf16[136,256]{1,0:T(8,128)(2,1)S(1)} %project.1.p0), channel_id=1, source_target_pairs={{0,5},{1,4},{2,7},{3,6},{4,1},{5,0},{6,3},{7,2},{8,13},{9,12},{10,... | collective-permute-start | bytes 208904 | tf_op jit(solution)/shard_map/ppermute | solution.py:496
  39.8 1.0 %collective-permute-start.9 = (bf16[136,256]{1,0:T(8,128)(2,1)S(1)}, bf16[136,256]{1,0:T(8,128)(2,1)S(1)}, u32[]{:S(2)}, u32[]{:S(2)}) collective-permute-start(bf16[136,256]{1,0:T(8,128)(2,1)S(1)} %project.1.p0), channel_id=1, source_target_pairs={{0,1},{1,0},{2,3},{3,2},{4,5},{5,4},{6,7},{7,6},{8,9},{9,8},{10,11... | collective-permute-start | bytes 208904 | tf_op jit(solution)/shard_map/ppermute | solution.py:496
  40.8 1.7 %collective-permute-done.13.p3 = bf16[136,256]{1,0:T(8,128)(2,1)S(1)} collective-permute-done((bf16[136,256]{1,0:T(8,128)(2,1)S(1)}, bf16[136,256]{1,0:T(8,128)(2,1)S(1)}, u32[]{:S(2)}, u32[]{:S(2)}) %collective-permute-start.13) | collective-permute-done | bytes 69664 | tf_op jit(solution)/shard_map/ppermute | solution.py:496
  42.5 1.1 %collective-permute-done.11.p2 = bf16[136,256]{1,0:T(8,128)(2,1)S(1)} collective-permute-done((bf16[136,256]{1,0:T(8,128)(2,1)S(1)}, bf16[136,256]{1,0:T(8,128)(2,1)S(1)}, u32[]{:S(2)}, u32[]{:S(2)}) %collective-permute-start.11) | collective-permute-done | bytes 69664 | tf_op jit(solution)/shard_map/ppermute | solution.py:496
  44.1 1.1 %early.1 = (f32[1024,256]{1,0:T(8,128)}, f32[8,128]{1,0:T(8,128)S(1)}, f32[2]{0:T(128)}) custom-call(bf16[136,256]{1,0:T(8,128)(2,1)S(1)} %project.1.p0, bf16[136,256]{1,0:T(8,128)(2,1)S(1)} %collective-permute-done.9.p1, bf16[136,256]{1,0:T(8,128)(2,1)S(1)} %collective-permute-done.11.p2, bf16[136,256]{1,0:T(8,128)(2,1)S(1)} %collective-permute-done.13.p3, ...), custom_call_target="tpu_custom_call" | custom-call | flops 1000000 | tf_op jit(solution)/shard_map/early/pallas_call | solution.py:28
  45.3 1.1 %late.1 = (f32[1024,256]{1,0:T(8,128)}, f32[8,128]{1,0:T(8,128)}) custom-call(bf16[136,256]{1,0:T(8,128)(2,1)S(1)} %collective-permute-done.8.q0, bf16[136,256]{1,0:T(8,128)(2,1)S(1)} %collective-permute-done.10.q1, bf16[136,256]{1,0:T(8,128)(2,1)S(1)} %collective-permute-done.12.q2, ...), custom_call_target="tpu_custom_call", output_to_operand_aliasing={{0}: (6, {})} | custom-call | flops 1000000 | tf_op jit(solution)/shard_map/late/pallas_call | solution.py:28
  (32 shorter events, 2.3 us)
Async XLA Ops:
  2.3 5.4 %collective-permute-start = (bf16[144,256]{1,0:T(8,128)(2,1)S(1)}, bf16[144,256]{1,0:T(8,128)(2,1)S(1)}, u32[]{:S(2)}, u32[]{:S(2)}) collective-permute-start(bf16[144,256]{1,0:T(8,128)(2,1)S(1)} %get-tuple-element.28), channel_id=1, source_target_pairs={{0,1},{1,0},{2,3},{3,2},{4,5},{5,4},{6,7},{7,6},{8,9},{9,8},{10,11... | collective-permute-start | bytes 221192 | tf_op jit(solution)/shard_map/ppermute | solution.py:496
  5.4 2.3 %copy-start.3 = (f32[256]{0:T(256)S(1)}, f32[256]{0:T(256)}, u32[]{:S(2)}) copy-start(f32[256]{0:T(256)} %param.9) | copy-start | bytes 3076
  7.7 6.6 %copy-start.5 = (s32[2,2,16,32]{3,2,1,0:T(8,128)S(1)}, s32[2,2,16,32]{3,2,1,0:T(8,128)}, u32[]{:S(2)}) copy-start(s32[2,2,16,32]{3,2,1,0:T(8,128)} %param.13) | copy-start | bytes 24580
  7.7 8.2 %copy-start.4 = (f32[256]{0:T(256)S(1)}, f32[256]{0:T(256)}, u32[]{:S(2)}) copy-start(f32[256]{0:T(256)} %param.11) | copy-start | bytes 3076
  12.2 3.7 %collective-permute-start.1 = (f32[8,256]{1,0:T(8,128)S(1)}, f32[8,256]{1,0:T(8,128)S(1)}, u32[]{:S(2)}, u32[]{:S(2)}) collective-permute-start(f32[8,256]{1,0:T(8,128)S(1)} %get-tuple-element.31.after_ref.near_ref), channel_id=1, source_target_pairs={{0,1},{1,0},{2,3},{3,2},{4,5},{5,4},{6,7},{7,6},{8,9},{9,8},{10,11... | collective-permute-start | bytes 24584 | tf_op jit(solution)/shard_map/ppermute | solution.py:496
  16.8 1.6 %collective-permute-start.2 = (bf16[4,136,256]{2,1,0:T(8,128)(2,1)S(1)}, bf16[4,136,256]{2,1,0:T(8,128)(2,1)S(1)}, u32[]{:S(2)}, u32[]{:S(2)}) collective-permute-start(bf16[4,136,256]{2,1,0:T(8,128)(2,1)S(1)} %get-tuple-element.37), channel_id=1, source_target_pairs={{0,2},{1,3},{2,0},{3,1},{4,6},{5,7},{6,4},{7,5},{8,10},{9,11},{10,... | collective-permute-start | bytes 835592 | tf_op jit(solution)/shard_map/ppermute | solution.py:496
  16.9 5.2 %copy-start = (f32[1024,256]{1,0:T(8,128)S(1)}, f32[1024,256]{1,0:T(8,128)}, u32[]{:S(2)}) copy-start(f32[1024,256]{1,0:T(8,128)} %sum_ref.5) | copy-start | bytes 3145732
  16.9 5.2 %copy-start.1 = (bf16[256,256]{1,0:T(8,128)(2,1)S(1)}, bf16[256,256]{1,0:T(8,128)(2,1)}, u32[]{:S(2)}) copy-start(bf16[256,256]{1,0:T(8,128)(2,1)} %w_ref.3) | copy-start | bytes 393220
  16.9 5.2 %copy-start.2 = (f32[1024]{0:T(1024)S(1)}, f32[1024]{0:T(1024)}, u32[]{:S(2)}) copy-start(f32[1024]{0:T(1024)} %param.15) | copy-start | bytes 12292
  18.5 7.9 %collective-permute-start.3 = (bf16[136,256]{1,0:T(8,128)(2,1)S(1)}, bf16[136,256]{1,0:T(8,128)(2,1)S(1)}, u32[]{:S(2)}, u32[]{:S(2)}) collective-permute-start(bf16[136,256]{1,0:T(8,128)(2,1)S(1)} %get-tuple-element.41), channel_id=1, source_target_pairs={{0,1},{1,0},{2,3},{3,2},{4,5},{5,4},{6,7},{7,6},{8,9},{9,8},{10,11... | collective-permute-start | bytes 208904 | tf_op jit(solution)/shard_map/ppermute | solution.py:496
  20.6 5.8 %collective-permute-start.4 = (bf16[136,256]{1,0:T(8,128)(2,1)S(1)}, bf16[136,256]{1,0:T(8,128)(2,1)S(1)}, u32[]{:S(2)}, u32[]{:S(2)}) collective-permute-start(bf16[136,256]{1,0:T(8,128)(2,1)S(1)} %get-tuple-element.42), channel_id=1, source_target_pairs={{0,4},{1,5},{2,6},{3,7},{4,0},{5,1},{6,2},{7,3},{8,12},{9,13},{10,... | collective-permute-start | bytes 208904 | tf_op jit(solution)/shard_map/ppermute | solution.py:496
  22.1 5.2 %collective-permute-start.5 = (bf16[136,256]{1,0:T(8,128)(2,1)S(1)}, bf16[136,256]{1,0:T(8,128)(2,1)S(1)}, u32[]{:S(2)}, u32[]{:S(2)}) collective-permute-start(bf16[136,256]{1,0:T(8,128)(2,1)S(1)} %get-tuple-element.43), channel_id=1, source_target_pairs={{0,5},{1,4},{2,7},{3,6},{4,1},{5,0},{6,3},{7,2},{8,13},{9,12},{10,... | collective-permute-start | bytes 208904 | tf_op jit(solution)/shard_map/ppermute | solution.py:496
  27.3 4.4 %collective-permute-start.6 = (bf16[136,256]{1,0:T(8,128)(2,1)S(1)}, bf16[136,256]{1,0:T(8,128)(2,1)S(1)}, u32[]{:S(2)}, u32[]{:S(2)}) collective-permute-start(bf16[136,256]{1,0:T(8,128)(2,1)S(1)} %gathered.1.own_ref), channel_id=1, source_target_pairs={{0,8},{1,9},{2,10},{3,11},{4,12},{5,13},{6,14},{7,15},{8,0},{9,1},... | collective-permute-start | bytes 208904 | tf_op jit(solution)/shard_map/ppermute | solution.py:496
  31.7 5.3 %collective-permute-start.7 = (bf16[136,256]{1,0:T(8,128)(2,1)S(1)}, bf16[136,256]{1,0:T(8,128)(2,1)S(1)}, u32[]{:S(2)}, u32[]{:S(2)}) collective-permute-start(bf16[136,256]{1,0:T(8,128)(2,1)S(1)} %pair.1.own_ref), channel_id=1, source_target_pairs={{0,16},{1,17},{2,18},{3,19},{4,20},{5,21},{6,22},{7,23},{8,24},{9,... | collective-permute-start | bytes 208904 | tf_op jit(solution)/shard_map/ppermute | solution.py:496
  37.2 5.3 %collective-permute-start.13 = (bf16[136,256]{1,0:T(8,128)(2,1)S(1)}, bf16[136,256]{1,0:T(8,128)(2,1)S(1)}, u32[]{:S(2)}, u32[]{:S(2)}) collective-permute-start(bf16[136,256]{1,0:T(8,128)(2,1)S(1)} %project.1.p0), channel_id=1, source_target_pairs={{0,5},{1,4},{2,7},{3,6},{4,1},{5,0},{6,3},{7,2},{8,13},{9,12},{10,... | collective-permute-start | bytes 208904 | tf_op jit(solution)/shard_map/ppermute | solution.py:496
  39.2 4.3 %collective-permute-start.11 = (bf16[136,256]{1,0:T(8,128)(2,1)S(1)}, bf16[136,256]{1,0:T(8,128)(2,1)S(1)}, u32[]{:S(2)}, u32[]{:S(2)}) collective-permute-start(bf16[136,256]{1,0:T(8,128)(2,1)S(1)} %project.1.p0), channel_id=1, source_target_pairs={{0,4},{1,5},{2,6},{3,7},{4,0},{5,1},{6,2},{7,3},{8,12},{9,13},{10,... | collective-permute-start | bytes 208904 | tf_op jit(solution)/shard_map/ppermute | solution.py:496
  39.8 4.3 %collective-permute-start.9 = (bf16[136,256]{1,0:T(8,128)(2,1)S(1)}, bf16[136,256]{1,0:T(8,128)(2,1)S(1)}, u32[]{:S(2)}, u32[]{:S(2)}) collective-permute-start(bf16[136,256]{1,0:T(8,128)(2,1)S(1)} %project.1.p0), channel_id=1, source_target_pairs={{0,1},{1,0},{2,3},{3,2},{4,5},{5,4},{6,7},{7,6},{8,9},{9,8},{10,11... | collective-permute-start | bytes 208904 | tf_op jit(solution)/shard_map/ppermute | solution.py:496
  40.8 4.4 %collective-permute-start.8 = (bf16[136,256]{1,0:T(8,128)(2,1)S(1)}, bf16[136,256]{1,0:T(8,128)(2,1)S(1)}, u32[]{:S(2)}, u32[]{:S(2)}) collective-permute-start(bf16[136,256]{1,0:T(8,128)(2,1)S(1)} %project.1.p0), channel_id=1, source_target_pairs={{0,2},{1,3},{2,0},{3,1},{4,6},{5,7},{6,4},{7,5},{8,10},{9,11},{10,... | collective-permute-start | bytes 208904 | tf_op jit(solution)/shard_map/ppermute | solution.py:496
  42.5 2.7 %collective-permute-start.14 = (bf16[136,256]{1,0:T(8,128)(2,1)S(1)}, bf16[136,256]{1,0:T(8,128)(2,1)S(1)}, u32[]{:S(2)}, u32[]{:S(2)}) collective-permute-start(bf16[136,256]{1,0:T(8,128)(2,1)S(1)} %collective-permute-done.13.p3), channel_id=1, source_target_pairs={{0,2},{1,3},{2,0},{3,1},{4,6},{5,7},{6,4},{7,5},{8,10},{9,11},{10,... | collective-permute-start | bytes 208904 | tf_op jit(solution)/shard_map/ppermute | solution.py:496
  43.5 1.6 %collective-permute-start.12 = (bf16[136,256]{1,0:T(8,128)(2,1)S(1)}, bf16[136,256]{1,0:T(8,128)(2,1)S(1)}, u32[]{:S(2)}, u32[]{:S(2)}) collective-permute-start(bf16[136,256]{1,0:T(8,128)(2,1)S(1)} %collective-permute-done.11.p2), channel_id=1, source_target_pairs={{0,2},{1,3},{2,0},{3,1},{4,6},{5,7},{6,4},{7,5},{8,10},{9,11},{10,... | collective-permute-start | bytes 208904 | tf_op jit(solution)/shard_map/ppermute | solution.py:496
  44.1 1.3 %collective-permute-start.10 = (bf16[136,256]{1,0:T(8,128)(2,1)S(1)}, bf16[136,256]{1,0:T(8,128)(2,1)S(1)}, u32[]{:S(2)}, u32[]{:S(2)}) collective-permute-start(bf16[136,256]{1,0:T(8,128)(2,1)S(1)} %collective-permute-done.9.p1), channel_id=1, source_target_pairs={{0,2},{1,3},{2,0},{3,1},{4,6},{5,7},{6,4},{7,5},{8,10},{9,11},{10,... | collective-permute-start | bytes 208904 | tf_op jit(solution)/shard_map/ppermute | solution.py:496

commit v6 on v5

--- a/solution.py
+++ b/solution.py
@@ -195,21 +195,19 @@
             put(c, t, rows + 1, jnp.where(strip > 0, 0.0, halo))
 
         def patches(t):
-            return jnp.concatenate(
-                [
-                    buf_ref[c, t, b : b + rows].reshape(rows * cols, 3 * channels)
-                    for b in range(3)
-                ],
-                axis=1,
-            )
+            return [
+                buf_ref[c, t, b : b + rows].reshape(rows * cols, 3 * channels) for b in range(3)
+            ]
 
         for t in range(frames):
             total = video_ref[c, t].reshape(rows * cols, channels).astype(f32)
             for a in range(3):
                 if t + a - 2 >= 0:
-                    total = total + jnp.dot(
-                        patches(t + a - 2), w_ref[a - first_tap], preferred_element_type=f32
-                    )
+                    for b, part in enumerate(patches(t + a - 2)):
+                        rows_at = slice(b * 3 * channels, (b + 1) * 3 * channels)
+                        total = total + jnp.dot(
+                            part, w_ref[a - first_tap, rows_at], preferred_element_type=f32
+                        )
             hid_ref[c, t * rows * cols : (t + 1) * rows * cols] = total
 
     def read(c, i):
@@ -321,14 +319,7 @@
 
     share = LANES
     half = SHARDS // 2
-    width = act_ref.shape[0] // 2
-    for k in range(2):
-        at = slice(k * width, (k + 1) * width)
-        part = jnp.dot(hot_ref[:, at], act_ref[at], preferred_element_type=f32)
-        if k == 0:
-            acc_ref[...] = part
-        else:
-            acc_ref[...] += part
+    acc_ref[...] = jnp.dot(hot_ref[...], act_ref[...], preferred_element_type=f32)
     for p in range(half):
         send_ref[p, :share] = acc_ref[p * share : (p + 1) * share].astype(bf16)
         send_ref[p, share:] = tails_ref[p]

time: 46.6 us -> 46.6 us (level)
  no operation moved by 1% of the time
where the time goes in v6:
time: 46.6 us; the launch traced here: 46.4 us
  Pallas kernels  17.2 us (37%)
  starting transfers between devices  16.7 us (36%)
  waiting for transfers between devices  11.6 us (25%)
  between operations  0.77 us (2%)
    pallas_call x13, Pallas kernels, call(): pl.pallas_call(kernel, out_shape=tuple((jax.ShapeDtypeStruct(s, d) for s,...  17.2 us
    ppermute x15, starting transfers between devices, swap(): return lax.ppermute(x, BOTH, [(i, i ^ mask) for i in range(n)])  16.7 us
    ppermute x15, waiting for transfers between devices, swap(): return lax.ppermute(x, BOTH, [(i, i ^ mask) for i in range(n)])  11.6 us
  transfers between devices with their start and end apart: 15, of which 10 were waited for; matrix products, arithmetic and copies ran while one was open for 0% of the time, Pallas kernels for 19%

profile of v6, /device:TPU:0, one launch (start us, length us, event | category | flops | bytes accessed | tf_op | source)
XLA Modules:
  0.0 46.4 jit_solution(2431542253844778069)
XLA Ops:
  0.6 1.7 %stats.1 = (bf16[144,256]{1,0:T(8,128)(2,1)S(1)}, f32[8,256]{1,0:T(8,128)S(1)}, bf16[2,2,16,32,256]{4,3,2,1,0:T(8,128)(2,1)S(1)}) custom-call(bf16[2,2,16,32,256]{4,3,2,1,0:T(8,128)(2,1)} %video_hbm.1), custom_call_target="tpu_custom_call" | custom-call | flops 10000000 | tf_op jit(solution)/shard_map/stats/pallas_call | solution.py:28
  2.3 3.1 %collective-permute-start = (bf16[144,256]{1,0:T(8,128)(2,1)S(1)}, bf16[144,256]{1,0:T(8,128)(2,1)S(1)}, u32[]{:S(2)}, u32[]{:S(2)}) collective-permute-start(bf16[144,256]{1,0:T(8,128)(2,1)S(1)} %get-tuple-element.28), channel_id=1, source_target_pairs={{0,1},{1,0},{2,3},{3,2},{4,5},{5,4},{6,7},{7,6},{8,9},{9,8},{10,11... | collective-permute-start | bytes 221192 | tf_op jit(solution)/shard_map/ppermute | solution.py:487
  5.4 1.7 %taps.1.w_ref = bf16[2,2304,256]{2,1,0:T(8,128)(2,1)S(1)} custom-call(bf16[3,2304,256]{2,1,0:T(8,128)(2,1)} %bitcast.13, f32[8,256]{1,0:T(8,128)S(1)} %get-tuple-element.29.after_ref.loc_ref), custom_call_target="tpu_custom_call" | custom-call | flops 1000000000 | tf_op jit(solution)/shard_map/taps/pallas_call | solution.py:28
  7.1 0.6 %collective-permute-done.pay_ref = bf16[144,256]{1,0:T(8,128)(2,1)S(1)} collective-permute-done((bf16[144,256]{1,0:T(8,128)(2,1)S(1)}, bf16[144,256]{1,0:T(8,128)(2,1)S(1)}, u32[]{:S(2)}, u32[]{:S(2)}) %collective-permute-start) | collective-permute-done | bytes 73760 | tf_op jit(solution)/shard_map/ppermute | solution.py:487
  7.7 4.5 %conv.1 = (f32[2,1024,256]{2,1,0:T(8,128)S(1)}, f32[8,256]{1,0:T(8,128)S(1)}) custom-call(bf16[2,2,16,32,256]{4,3,2,1,0:T(8,128)(2,1)S(1)} %get-tuple-element.27.video_ref, bf16[144,256]{1,0:T(8,128)(2,1)S(1)} %collective-permute-done.pay_ref, f32[8,256]{1,0:T(8,128)S(1)} %get-tuple-element.29.after_ref.loc_ref, f32[1,256]{1,0:T(1,128)S(1)} %bitcast.11, ...), custom_call_target="tpu_custom_call" | custom-call | flops 4000000000 | tf_op jit(solution)/shard_map/conv/pallas_call | solution.py:28
  12.2 2.1 %collective-permute-start.1 = (f32[8,256]{1,0:T(8,128)S(1)}, f32[8,256]{1,0:T(8,128)S(1)}, u32[]{:S(2)}, u32[]{:S(2)}) collective-permute-start(f32[8,256]{1,0:T(8,128)S(1)} %get-tuple-element.31.after_ref.near_ref), channel_id=1, source_target_pairs={{0,1},{1,0},{2,3},{3,2},{4,5},{5,4},{6,7},{7,6},{8,9},{9,8},{10,11... | collective-permute-start | bytes 24584 | tf_op jit(solution)/shard_map/ppermute | solution.py:487
  14.4 1.1 %count.1 = (f32[8,128]{1,0:T(8,128)S(1)}, bf16[4,8,256]{2,1,0:T(8,128)(2,1)S(1)}, bf16[512,2048]{1,0:T(8,128)(2,1)S(1)}) custom-call(s32[16,128]{1,0:T(8,128)S(1)} %reshape.32.codes_ref, f32[8,256]{1,0:T(8,128)S(1)} %get-tuple-element.31.after_ref.near_ref), custom_call_target="tpu_custom_call" | custom-call | flops 500000000 | tf_op jit(solution)/shard_map/count/pallas_call | solution.py:28
  16.0 0.9 %segment.1 = (bf16[2048,256]{1,0:T(8,128)(2,1)S(1)}, bf16[4,136,256]{2,1,0:T(8,128)(2,1)S(1)}) custom-call(f32[2,1024,256]{2,1,0:T(8,128)S(1)} %get-tuple-element.30.hid_ref, f32[8,256]{1,0:T(8,128)S(1)} %get-tuple-element.31.after_ref.near_ref, f32[8,256]{1,0:T(8,128)S(1)} %collective-permute-done.1.far_ref, f32[1,256]{1,0:T(1,128)S(1)} %bitcast.12, ...), custom_call_target="tpu_custom_call" | custom-call | flops 1500000000 | tf_op jit(solution)/shard_map/segment/pallas_call | solution.py:28
  16.9 0.7 %keep.1.keep_ref = f32[512,256]{1,0:T(8,128)S(1)} custom-call(bf16[2048,256]{1,0:T(8,128)(2,1)S(1)} %get-tuple-element.35.act_ref, s32[16,128]{1,0:T(8,128)S(1)} %reshape.32.codes_ref), custom_call_target="tpu_custom_call" | custom-call | flops 1000000000 | tf_op jit(solution)/shard_map/keep/pallas_call | solution.py:28
  17.6 0.8 %collective-permute-done.2.got_ref = bf16[4,136,256]{2,1,0:T(8,128)(2,1)S(1)} collective-permute-done((bf16[4,136,256]{2,1,0:T(8,128)(2,1)S(1)}, bf16[4,136,256]{2,1,0:T(8,128)(2,1)S(1)}, u32[]{:S(2)}, u32[]{:S(2)}) %collective-permute-start.2) | collective-permute-done | bytes 278560 | tf_op jit(solution)/shard_map/ppermute | solution.py:487
  18.5 2.1 %collective-permute-start.3 = (bf16[136,256]{1,0:T(8,128)(2,1)S(1)}, bf16[136,256]{1,0:T(8,128)(2,1)S(1)}, u32[]{:S(2)}, u32[]{:S(2)}) collective-permute-start(bf16[136,256]{1,0:T(8,128)(2,1)S(1)} %get-tuple-element.41), channel_id=1, source_target_pairs={{0,1},{1,0},{2,3},{3,2},{4,5},{5,4},{6,7},{7,6},{8,9},{9,8},{10,11... | collective-permute-start | bytes 208904 | tf_op jit(solution)/shard_map/ppermute | solution.py:487
  20.6 1.5 %collective-permute-start.4 = (bf16[136,256]{1,0:T(8,128)(2,1)S(1)}, bf16[136,256]{1,0:T(8,128)(2,1)S(1)}, u32[]{:S(2)}, u32[]{:S(2)}) collective-permute-start(bf16[136,256]{1,0:T(8,128)(2,1)S(1)} %get-tuple-element.42), channel_id=1, source_target_pairs={{0,4},{1,5},{2,6},{3,7},{4,0},{5,1},{6,2},{7,3},{8,12},{9,13},{10,... | collective-permute-start | bytes 208904 | tf_op jit(solution)/shard_map/ppermute | solution.py:487
  22.1 4.2 %latent.1 = (f32[2048,256]{1,0:T(8,128)}, f32[8,128]{1,0:T(8,128)S(1)}) custom-call(bf16[2048,256]{1,0:T(8,128)(2,1)S(1)} %get-tuple-element.35.act_ref, bf16[256,256]{1,0:T(8,128)(2,1)S(1)} %copy-done.1, s32[16,128]{1,0:T(8,128)S(1)} %reshape.32.codes_ref, f32[1024,256]{1,0:T(8,128)S(1)} %copy-done, f32[8,128]{1,0:T(8,128)S(1)} %bitcast.8, ...), custom_call_target="tpu_custom_call" | custom-call | flops 2500000000 | tf_op jit(solution)/shard_map/latent/pallas_call | solution.py:28
  26.4 0.9 %collective-permute-done.5.c_ref = bf16[136,256]{1,0:T(8,128)(2,1)S(1)} collective-permute-done((bf16[136,256]{1,0:T(8,128)(2,1)S(1)}, bf16[136,256]{1,0:T(8,128)(2,1)S(1)}, u32[]{:S(2)}, u32[]{:S(2)}) %collective-permute-start.5) | collective-permute-done | bytes 69664 | tf_op jit(solution)/shard_map/ppermute | solution.py:487
  27.3 1.6 %collective-permute-start.6 = (bf16[136,256]{1,0:T(8,128)(2,1)S(1)}, bf16[136,256]{1,0:T(8,128)(2,1)S(1)}, u32[]{:S(2)}, u32[]{:S(2)}) collective-permute-start(bf16[136,256]{1,0:T(8,128)(2,1)S(1)} %gathered.1.own_ref), channel_id=1, source_target_pairs={{0,8},{1,9},{2,10},{3,11},{4,12},{5,13},{6,14},{7,15},{8,0},{9,1},... | collective-permute-start | bytes 208904 | tf_op jit(solution)/shard_map/ppermute | solution.py:487
  29.0 2.7 %collective-permute-done.6.got_ref = bf16[136,256]{1,0:T(8,128)(2,1)S(1)} collective-permute-done((bf16[136,256]{1,0:T(8,128)(2,1)S(1)}, bf16[136,256]{1,0:T(8,128)(2,1)S(1)}, u32[]{:S(2)}, u32[]{:S(2)}) %collective-permute-start.6) | collective-permute-done | bytes 69664 | tf_op jit(solution)/shard_map/ppermute | solution.py:487
  31.7 2.7 %collective-permute-start.7 = (bf16[136,256]{1,0:T(8,128)(2,1)S(1)}, bf16[136,256]{1,0:T(8,128)(2,1)S(1)}, u32[]{:S(2)}, u32[]{:S(2)}) collective-permute-start(bf16[136,256]{1,0:T(8,128)(2,1)S(1)} %pair.1.own_ref), channel_id=1, source_target_pairs={{0,16},{1,17},{2,18},{3,19},{4,20},{5,21},{6,22},{7,23},{8,24},{9,... | collective-permute-start | bytes 208904 | tf_op jit(solution)/shard_map/ppermute | solution.py:487
  34.4 2.6 %collective-permute-done.7.got_ref = bf16[136,256]{1,0:T(8,128)(2,1)S(1)} collective-permute-done((bf16[136,256]{1,0:T(8,128)(2,1)S(1)}, bf16[136,256]{1,0:T(8,128)(2,1)S(1)}, u32[]{:S(2)}, u32[]{:S(2)}) %collective-permute-start.7) | collective-permute-done | bytes 69664 | tf_op jit(solution)/shard_map/ppermute | solution.py:487
  37.2 2.0 %collective-permute-start.13 = (bf16[136,256]{1,0:T(8,128)(2,1)S(1)}, bf16[136,256]{1,0:T(8,128)(2,1)S(1)}, u32[]{:S(2)}, u32[]{:S(2)}) collective-permute-start(bf16[136,256]{1,0:T(8,128)(2,1)S(1)} %project.1.p0), channel_id=1, source_target_pairs={{0,5},{1,4},{2,7},{3,6},{4,1},{5,0},{6,3},{7,2},{8,13},{9,12},{10,... | collective-permute-start | bytes 208904 | tf_op jit(solution)/shard_map/ppermute | solution.py:487
  39.8 1.0 %collective-permute-start.9 = (bf16[136,256]{1,0:T(8,128)(2,1)S(1)}, bf16[136,256]{1,0:T(8,128)(2,1)S(1)}, u32[]{:S(2)}, u32[]{:S(2)}) collective-permute-start(bf16[136,256]{1,0:T(8,128)(2,1)S(1)} %project.1.p0), channel_id=1, source_target_pairs={{0,1},{1,0},{2,3},{3,2},{4,5},{5,4},{6,7},{7,6},{8,9},{9,8},{10,11... | collective-permute-start | bytes 208904 | tf_op jit(solution)/shard_map/ppermute | solution.py:487
  40.8 1.7 %collective-permute-done.13.p3 = bf16[136,256]{1,0:T(8,128)(2,1)S(1)} collective-permute-done((bf16[136,256]{1,0:T(8,128)(2,1)S(1)}, bf16[136,256]{1,0:T(8,128)(2,1)S(1)}, u32[]{:S(2)}, u32[]{:S(2)}) %collective-permute-start.13) | collective-permute-done | bytes 69664 | tf_op jit(solution)/shard_map/ppermute | solution.py:487
  42.5 1.1 %collective-permute-done.11.p2 = bf16[136,256]{1,0:T(8,128)(2,1)S(1)} collective-permute-done((bf16[136,256]{1,0:T(8,128)(2,1)S(1)}, bf16[136,256]{1,0:T(8,128)(2,1)S(1)}, u32[]{:S(2)}, u32[]{:S(2)}) %collective-permute-start.11) | collective-permute-done | bytes 69664 | tf_op jit(solution)/shard_map/ppermute | solution.py:487
  44.1 1.1 %early.1 = (f32[1024,256]{1,0:T(8,128)}, f32[8,128]{1,0:T(8,128)S(1)}, f32[2]{0:T(128)}) custom-call(bf16[136,256]{1,0:T(8,128)(2,1)S(1)} %project.1.p0, bf16[136,256]{1,0:T(8,128)(2,1)S(1)} %collective-permute-done.9.p1, bf16[136,256]{1,0:T(8,128)(2,1)S(1)} %collective-permute-done.11.p2, bf16[136,256]{1,0:T(8,128)(2,1)S(1)} %collective-permute-done.13.p3, ...), custom_call_target="tpu_custom_call" | custom-call | flops 1000000 | tf_op jit(solution)/shard_map/early/pallas_call | solution.py:28
  45.3 1.1 %late.1 = (f32[1024,256]{1,0:T(8,128)}, f32[8,128]{1,0:T(8,128)}) custom-call(bf16[136,256]{1,0:T(8,128)(2,1)S(1)} %collective-permute-done.8.q0, bf16[136,256]{1,0:T(8,128)(2,1)S(1)} %collective-permute-done.10.q1, bf16[136,256]{1,0:T(8,128)(2,1)S(1)} %collective-permute-done.12.q2, ...), custom_call_target="tpu_custom_call", output_to_operand_aliasing={{0}: (6, {})} | custom-call | flops 1000000 | tf_op jit(solution)/shard_map/late/pallas_call | solution.py:28
  (32 shorter events, 2.3 us)
Async XLA Ops:
  2.3 5.4 %collective-permute-start = (bf16[144,256]{1,0:T(8,128)(2,1)S(1)}, bf16[144,256]{1,0:T(8,128)(2,1)S(1)}, u32[]{:S(2)}, u32[]{:S(2)}) collective-permute-start(bf16[144,256]{1,0:T(8,128)(2,1)S(1)} %get-tuple-element.28), channel_id=1, source_target_pairs={{0,1},{1,0},{2,3},{3,2},{4,5},{5,4},{6,7},{7,6},{8,9},{9,8},{10,11... | collective-permute-start | bytes 221192 | tf_op jit(solution)/shard_map/ppermute | solution.py:487
  5.4 2.3 %copy-start.3 = (f32[256]{0:T(256)S(1)}, f32[256]{0:T(256)}, u32[]{:S(2)}) copy-start(f32[256]{0:T(256)} %param.9) | copy-start | bytes 3076
  7.7 6.6 %copy-start.5 = (s32[2,2,16,32]{3,2,1,0:T(8,128)S(1)}, s32[2,2,16,32]{3,2,1,0:T(8,128)}, u32[]{:S(2)}) copy-start(s32[2,2,16,32]{3,2,1,0:T(8,128)} %param.13) | copy-start | bytes 24580
  7.7 8.2 %copy-start.4 = (f32[256]{0:T(256)S(1)}, f32[256]{0:T(256)}, u32[]{:S(2)}) copy-start(f32[256]{0:T(256)} %param.11) | copy-start | bytes 3076
  12.2 3.7 %collective-permute-start.1 = (f32[8,256]{1,0:T(8,128)S(1)}, f32[8,256]{1,0:T(8,128)S(1)}, u32[]{:S(2)}, u32[]{:S(2)}) collective-permute-start(f32[8,256]{1,0:T(8,128)S(1)} %get-tuple-element.31.after_ref.near_ref), channel_id=1, source_target_pairs={{0,1},{1,0},{2,3},{3,2},{4,5},{5,4},{6,7},{7,6},{8,9},{9,8},{10,11... | collective-permute-start | bytes 24584 | tf_op jit(solution)/shard_map/ppermute | solution.py:487
  16.8 1.6 %collective-permute-start.2 = (bf16[4,136,256]{2,1,0:T(8,128)(2,1)S(1)}, bf16[4,136,256]{2,1,0:T(8,128)(2,1)S(1)}, u32[]{:S(2)}, u32[]{:S(2)}) collective-permute-start(bf16[4,136,256]{2,1,0:T(8,128)(2,1)S(1)} %get-tuple-element.37), channel_id=1, source_target_pairs={{0,2},{1,3},{2,0},{3,1},{4,6},{5,7},{6,4},{7,5},{8,10},{9,11},{10,... | collective-permute-start | bytes 835592 | tf_op jit(solution)/shard_map/ppermute | solution.py:487
  16.9 5.2 %copy-start = (f32[1024,256]{1,0:T(8,128)S(1)}, f32[1024,256]{1,0:T(8,128)}, u32[]{:S(2)}) copy-start(f32[1024,256]{1,0:T(8,128)} %sum_ref.5) | copy-start | bytes 3145732
  16.9 5.2 %copy-start.1 = (bf16[256,256]{1,0:T(8,128)(2,1)S(1)}, bf16[256,256]{1,0:T(8,128)(2,1)}, u32[]{:S(2)}) copy-start(bf16[256,256]{1,0:T(8,128)(2,1)} %w_ref.3) | copy-start | bytes 393220
  16.9 5.2 %copy-start.2 = (f32[1024]{0:T(1024)S(1)}, f32[1024]{0:T(1024)}, u32[]{:S(2)}) copy-start(f32[1024]{0:T(1024)} %param.15) | copy-start | bytes 12292
  18.5 7.9 %collective-permute-start.3 = (bf16[136,256]{1,0:T(8,128)(2,1)S(1)}, bf16[136,256]{1,0:T(8,128)(2,1)S(1)}, u32[]{:S(2)}, u32[]{:S(2)}) collective-permute-start(bf16[136,256]{1,0:T(8,128)(2,1)S(1)} %get-tuple-element.41), channel_id=1, source_target_pairs={{0,1},{1,0},{2,3},{3,2},{4,5},{5,4},{6,7},{7,6},{8,9},{9,8},{10,11... | collective-permute-start | bytes 208904 | tf_op jit(solution)/shard_map/ppermute | solution.py:487
  20.6 5.8 %collective-permute-start.4 = (bf16[136,256]{1,0:T(8,128)(2,1)S(1)}, bf16[136,256]{1,0:T(8,128)(2,1)S(1)}, u32[]{:S(2)}, u32[]{:S(2)}) collective-permute-start(bf16[136,256]{1,0:T(8,128)(2,1)S(1)} %get-tuple-element.42), channel_id=1, source_target_pairs={{0,4},{1,5},{2,6},{3,7},{4,0},{5,1},{6,2},{7,3},{8,12},{9,13},{10,... | collective-permute-start | bytes 208904 | tf_op jit(solution)/shard_map/ppermute | solution.py:487
  22.1 5.2 %collective-permute-start.5 = (bf16[136,256]{1,0:T(8,128)(2,1)S(1)}, bf16[136,256]{1,0:T(8,128)(2,1)S(1)}, u32[]{:S(2)}, u32[]{:S(2)}) collective-permute-start(bf16[136,256]{1,0:T(8,128)(2,1)S(1)} %get-tuple-element.43), channel_id=1, source_target_pairs={{0,5},{1,4},{2,7},{3,6},{4,1},{5,0},{6,3},{7,2},{8,13},{9,12},{10,... | collective-permute-start | bytes 208904 | tf_op jit(solution)/shard_map/ppermute | solution.py:487
  27.3 4.4 %collective-permute-start.6 = (bf16[136,256]{1,0:T(8,128)(2,1)S(1)}, bf16[136,256]{1,0:T(8,128)(2,1)S(1)}, u32[]{:S(2)}, u32[]{:S(2)}) collective-permute-start(bf16[136,256]{1,0:T(8,128)(2,1)S(1)} %gathered.1.own_ref), channel_id=1, source_target_pairs={{0,8},{1,9},{2,10},{3,11},{4,12},{5,13},{6,14},{7,15},{8,0},{9,1},... | collective-permute-start | bytes 208904 | tf_op jit(solution)/shard_map/ppermute | solution.py:487
  31.7 5.3 %collective-permute-start.7 = (bf16[136,256]{1,0:T(8,128)(2,1)S(1)}, bf16[136,256]{1,0:T(8,128)(2,1)S(1)}, u32[]{:S(2)}, u32[]{:S(2)}) collective-permute-start(bf16[136,256]{1,0:T(8,128)(2,1)S(1)} %pair.1.own_ref), channel_id=1, source_target_pairs={{0,16},{1,17},{2,18},{3,19},{4,20},{5,21},{6,22},{7,23},{8,24},{9,... | collective-permute-start | bytes 208904 | tf_op jit(solution)/shard_map/ppermute | solution.py:487
  37.2 5.3 %collective-permute-start.13 = (bf16[136,256]{1,0:T(8,128)(2,1)S(1)}, bf16[136,256]{1,0:T(8,128)(2,1)S(1)}, u32[]{:S(2)}, u32[]{:S(2)}) collective-permute-start(bf16[136,256]{1,0:T(8,128)(2,1)S(1)} %project.1.p0), channel_id=1, source_target_pairs={{0,5},{1,4},{2,7},{3,6},{4,1},{5,0},{6,3},{7,2},{8,13},{9,12},{10,... | collective-permute-start | bytes 208904 | tf_op jit(solution)/shard_map/ppermute | solution.py:487
  39.2 4.3 %collective-permute-start.11 = (bf16[136,256]{1,0:T(8,128)(2,1)S(1)}, bf16[136,256]{1,0:T(8,128)(2,1)S(1)}, u32[]{:S(2)}, u32[]{:S(2)}) collective-permute-start(bf16[136,256]{1,0:T(8,128)(2,1)S(1)} %project.1.p0), channel_id=1, source_target_pairs={{0,4},{1,5},{2,6},{3,7},{4,0},{5,1},{6,2},{7,3},{8,12},{9,13},{10,... | collective-permute-start | bytes 208904 | tf_op jit(solution)/shard_map/ppermute | solution.py:487
  39.8 4.3 %collective-permute-start.9 = (bf16[136,256]{1,0:T(8,128)(2,1)S(1)}, bf16[136,256]{1,0:T(8,128)(2,1)S(1)}, u32[]{:S(2)}, u32[]{:S(2)}) collective-permute-start(bf16[136,256]{1,0:T(8,128)(2,1)S(1)} %project.1.p0), channel_id=1, source_target_pairs={{0,1},{1,0},{2,3},{3,2},{4,5},{5,4},{6,7},{7,6},{8,9},{9,8},{10,11... | collective-permute-start | bytes 208904 | tf_op jit(solution)/shard_map/ppermute | solution.py:487
  40.8 4.4 %collective-permute-start.8 = (bf16[136,256]{1,0:T(8,128)(2,1)S(1)}, bf16[136,256]{1,0:T(8,128)(2,1)S(1)}, u32[]{:S(2)}, u32[]{:S(2)}) collective-permute-start(bf16[136,256]{1,0:T(8,128)(2,1)S(1)} %project.1.p0), channel_id=1, source_target_pairs={{0,2},{1,3},{2,0},{3,1},{4,6},{5,7},{6,4},{7,5},{8,10},{9,11},{10,... | collective-permute-start | bytes 208904 | tf_op jit(solution)/shard_map/ppermute | solution.py:487
  42.5 2.7 %collective-permute-start.14 = (bf16[136,256]{1,0:T(8,128)(2,1)S(1)}, bf16[136,256]{1,0:T(8,128)(2,1)S(1)}, u32[]{:S(2)}, u32[]{:S(2)}) collective-permute-start(bf16[136,256]{1,0:T(8,128)(2,1)S(1)} %collective-permute-done.13.p3), channel_id=1, source_target_pairs={{0,2},{1,3},{2,0},{3,1},{4,6},{5,7},{6,4},{7,5},{8,10},{9,11},{10,... | collective-permute-start | bytes 208904 | tf_op jit(solution)/shard_map/ppermute | solution.py:487
  43.5 1.6 %collective-permute-start.12 = (bf16[136,256]{1,0:T(8,128)(2,1)S(1)}, bf16[136,256]{1,0:T(8,128)(2,1)S(1)}, u32[]{:S(2)}, u32[]{:S(2)}) collective-permute-start(bf16[136,256]{1,0:T(8,128)(2,1)S(1)} %collective-permute-done.11.p2), channel_id=1, source_target_pairs={{0,2},{1,3},{2,0},{3,1},{4,6},{5,7},{6,4},{7,5},{8,10},{9,11},{10,... | collective-permute-start | bytes 208904 | tf_op jit(solution)/shard_map/ppermute | solution.py:487
  44.1 1.3 %collective-permute-start.10 = (bf16[136,256]{1,0:T(8,128)(2,1)S(1)}, bf16[136,256]{1,0:T(8,128)(2,1)S(1)}, u32[]{:S(2)}, u32[]{:S(2)}) collective-permute-start(bf16[136,256]{1,0:T(8,128)(2,1)S(1)} %collective-permute-done.9.p1), channel_id=1, source_target_pairs={{0,2},{1,3},{2,0},{3,1},{4,6},{5,7},{6,4},{7,5},{8,10},{9,11},{10,... | collective-permute-start | bytes 208904 | tf_op jit(solution)/shard_map/ppermute | solution.py:487
